TPU v7x, 128 devices: a whole 4x4x4 slice. The times are simulated.
128 devices in a mesh: op: 4 (over z), row: 32 (over y, x, core).
Axes of the slice: x: 4, y: 4, z: 4, core: 2. Of those that a mesh axis runs over, the one named last changes fastest.
Arguments:
- wannier_ops: bfloat16 [2, 4000, 2, 128, 128], P(None, 'row'), may hold values from -0.09375 to 0.09375
- r_coords: int32 [4000, 3], P('row'), may hold values from -8 to 8
- degeneracy: int32 [4000], P('row'), may hold values from 1 to 4
- kpoints: int32 [256, 3], replicated, may hold values from 0 to 15
- bloch_vectors: bfloat16 [256, 2, 64, 128], P(('op', 'row')), may hold values from -0.375 to 0.375
Outputs:
- covariant: float32 [256, 2, 4096], P(('op', 'row'))
Inputs may be any that keep to these rules, and one draw needn't show every extreme that they name: `r_coords`: these coordinates are small integers; a program may pack several of them into one int32 word when it moves them. `degeneracy`: these degeneracies are small integers; a program may pack several of them into one int32 word when it moves them.
All inputs are finite; a program needn't handle non-finite values.
Results may differ from a plain program's by a relative error of at most 0.0038.
Values may be sent and summed in bfloat16 or wider, within the bound.
No kernel may reach another device: no remote copies, remote signals or barrier semaphores. Data moves between devices by JAX's collectives and lax.ppermute only.
A program may use at most 192 MiB of HBM per device.

v0:
```python
import functools
import math

import jax
import jax.numpy as jnp
from jax import lax
from jax.experimental import pallas as pl
from jax.experimental.pallas import tpu as pltpu
from jax.sharding import Mesh
from jax.sharding import PartitionSpec as P

GRID = 16
RMAX = 8
TWO_PI = 6.283185307179586
PLANE = ("y", "x", "c")
WHOLE = ("z", "y", "x", "c")
LINK = jnp.bfloat16
SIDE = 4
ROWS = 128
FOURIER_VMEM = 14 << 20
ROTATE_VMEM = 12 << 20


def owner_place(k, y, x, core):
    s1, s2 = (k // 8) % SIDE, (k // 2) % SIDE
    y_step = jnp.where(core == 0, s1, s2)
    x_step = jnp.where(core == 0, s2, s1)
    return (y + y_step) % SIDE, (x + x_step) % SIDE


def place_of(me):
    return me // 32, (me // 8) % SIDE, (me // 2) % SIDE, me % 2


def phase_matrix(me, coords, degeneracy, kpoints):
    count = coords.shape[1]
    z, y, x, c = place_of(me)
    at = lax.broadcasted_iota(jnp.int32, (64, 256), 0)
    core = (c + at // 32) % 2
    y_own, x_own = owner_place(at % 32, y, x, core)
    owned = z * 64 + (y_own * SIDE + x_own) * 4 + core * 2 + at % 2
    chosen = (lax.broadcasted_iota(jnp.int32, (64, 256), 1) == owned).astype(jnp.float32)
    turns = jnp.zeros((64, count), jnp.int32)
    for axis in range(3):
        line = kpoints[axis : axis + 1, :].astype(jnp.float32)
        k_axis = jnp.sum(chosen * line, axis=1, keepdims=True).astype(jnp.int32)
        turns = turns + k_axis * coords[axis : axis + 1, :]
    angles = (turns & (GRID - 1)).astype(jnp.float32) * (TWO_PI / GRID)
    weights = 1.0 / degeneracy.astype(jnp.float32)
    cosine = jnp.cos(angles) * weights
    sine = jnp.sin(angles) * weights
    along_x = coords[0:1, :].astype(jnp.float32) / RMAX
    rows = []
    for re, im in ((cosine, sine), (-along_x * sine, along_x * cosine)):
        for first, second in ((re, -im), (im, re)):
            pad = jnp.zeros((64, ROWS - count), jnp.float32)
            rows.append(jnp.concatenate([first, pad, second, pad], axis=1))
    return jnp.concatenate(rows, axis=0).astype(jnp.bfloat16)


def fourier_sums(op, rows, left, o_ref, f_ref, raw_ref, sem):
    step = pl.program_id(0)
    depth = raw_ref.shape[0]

    def fetch(at):
        block = pl.multiple_of(at * rows, rows)
        return pltpu.make_async_copy(
            o_ref.at[op, :, :, pl.ds(block, rows), :], raw_ref.at[at % depth], sem.at[at % depth]
        )

    @pl.when(step == 0)
    def _():
        for at in range(depth - 1):
            fetch(at).start()

    @pl.when(step + depth - 1 < pl.num_programs(0))
    def _():
        fetch(step + depth - 1).start()

    matrix = left()
    fetch(step).wait()
    count = raw_ref.shape[1]
    halves = []
    for part in range(2):
        block = raw_ref[step % depth, :, part]
        block = jnp.concatenate([block, jnp.zeros((ROWS - count, rows, 128), jnp.bfloat16)], axis=0)
        halves.append(jnp.swapaxes(block, 0, 1))
    stacked = jnp.concatenate(halves, axis=1)
    sums = []
    for pair in range(rows // 2):
        right = jnp.concatenate([stacked[2 * pair], stacked[2 * pair + 1]], axis=1)
        both = jnp.dot(matrix, right, preferred_element_type=jnp.float32).astype(f_ref.dtype)
        sums += [both[:, :128], both[:, 128:]]
    at = pl.multiple_of(step * rows, rows)
    f_ref[:, pl.ds(at, rows), :] = jnp.swapaxes(jnp.stack(sums, axis=0), 0, 1)


def fourier_first(rows, me_ref, c_ref, d_ref, k_ref, o_ref, f_ref, l_ref, cv_ref, dv_ref, kv_ref, raw_ref, sem, in_sem):
    step = pl.program_id(0)
    moves = [
        pltpu.make_async_copy(src, dst, in_sem.at[i])
        for i, (src, dst) in enumerate(((c_ref, cv_ref), (d_ref, dv_ref), (k_ref, kv_ref)))
    ]

    @pl.when(step == 0)
    def _():
        for move in moves:
            move.start()

    def left():
        @pl.when(step == 0)
        def _():
            for move in moves:
                move.wait()
            l_ref[...] = phase_matrix(me_ref[0], cv_ref[...], dv_ref[...], kv_ref[...])

        return l_ref[...]

    fourier_sums(0, rows, left, o_ref, f_ref, raw_ref, sem)


def fourier_second(rows, l_ref, o_ref, f_ref, raw_ref, sem):
    fourier_sums(1, rows, lambda: l_ref[...], o_ref, f_ref, raw_ref, sem)


def fourier(op, small, ops, rows=32, depth=3):
    _, count, _, width, _ = ops.shape
    lines = 256
    local, far = pl.BlockSpec(memory_space=pltpu.VMEM), pl.BlockSpec(memory_space=pltpu.HBM)
    scratch = [pltpu.VMEM((depth, count, 2, rows, width), jnp.bfloat16), pltpu.SemaphoreType.DMA((depth,))]
    out = [jax.ShapeDtypeStruct((lines, width, width), jnp.bfloat16)]
    params = pltpu.CompilerParams(dimension_semantics=("arbitrary",), vmem_limit_bytes=FOURIER_VMEM)
    cost = pl.CostEstimate(flops=4_000_000_000, bytes_accessed=16_000_000, transcendentals=0)
    if op == 0:
        copies = [pltpu.VMEM(part.shape, part.dtype) for part in small[1:]]
        return pl.pallas_call(
            functools.partial(fourier_first, rows),
            grid_spec=pltpu.PrefetchScalarGridSpec(
                num_scalar_prefetch=1,
                grid=(width // rows,),
                in_specs=[far] * 4,
                out_specs=[local, local],
                scratch_shapes=[*copies, *scratch, pltpu.SemaphoreType.DMA((3,))],
            ),
            out_shape=[*out, jax.ShapeDtypeStruct((lines, 2 * ROWS), jnp.bfloat16)],
            compiler_params=params,
            cost_estimate=cost,
            name="fourier_first",
        )(*small, ops)
    return pl.pallas_call(
        functools.partial(fourier_second, rows),
        grid=(width // rows,),
        in_specs=[local, far],
        out_specs=local,
        out_shape=out[0],
        scratch_shapes=scratch,
        compiler_params=params,
        cost_estimate=cost,
        name="fourier_second",
    )(small, ops)


def rotate_body(shifts, half, *refs):
    v_refs, f_refs, b_ref = refs[: len(shifts)], refs[-3:-1], refs[-1]
    for group, shift in enumerate(shifts):
        pairs, mids = [], []
        for j in range(8):
            k = half * 32 + shift * 8 + j
            v_re, v_im = v_refs[group][j, 0], v_refs[group][j, 1]
            pairs.append((v_re, v_im))
            left = jnp.concatenate(
                [jnp.concatenate([v_re, v_im], axis=1), jnp.concatenate([-v_im, v_re], axis=1)], axis=0
            )
            found = []
            for o in range(2):
                right = jnp.concatenate(
                    [jnp.concatenate([f_refs[o][2 * p, k], f_refs[o][2 * p + 1, k]], axis=0) for p in range(2)], axis=1
                )
                found.append(jnp.dot(left, right, preferred_element_type=jnp.float32))
            mids.append(found)
        for j in range(8):
            v_re, v_im = pairs[j]
            lines = []
            for o in range(2):
                for p in range(2):
                    tile = mids[j][o][:, 128 * p : 128 * p + 128]
                    lines.append(jnp.concatenate([tile[:64], tile[64:]], axis=1))
            high, low = halves_of(jnp.concatenate(lines, axis=0))
            right = jnp.concatenate(
                [jnp.concatenate([v_re, -v_im], axis=1), jnp.concatenate([v_im, v_re], axis=1)], axis=0
            )
            out = lax.dot_general(
                jnp.concatenate([high, low], axis=0),
                right,
                (((1,), (1,)), ((), ())),
                preferred_element_type=jnp.float32,
            )
            b_ref[8 * group + j] = (out[:256] + out[256:]).reshape(4, 64, 128)


def rotate(vectors, sums, half, shifts):
    count = 8 * len(shifts)
    whole = pl.BlockSpec(memory_space=pltpu.VMEM)
    return pl.pallas_call(
        functools.partial(rotate_body, shifts, half),
        in_specs=[whole] * (len(shifts) + 2),
        out_specs=whole,
        out_shape=jax.ShapeDtypeStruct((count, 4, 64, 128), jnp.float32),
        compiler_params=pltpu.CompilerParams(vmem_limit_bytes=ROTATE_VMEM),
        cost_estimate=pl.CostEstimate(flops=count * 120_000_000, bytes_accessed=count * 400_000, transcendentals=0),
        name="rotate",
    )(*[vectors[shift] for shift in shifts], *sums)


def halves_of(value):
    high = value.astype(jnp.bfloat16)
    return high, (value - high.astype(jnp.float32)).astype(jnp.bfloat16)


def final_body(kept_ref, *refs):
    came, o_ref, hold_ref = refs[:-2], refs[-2], refs[-1]
    factor = 1.0 / math.sqrt(64)

    def wide(re, im):
        return jnp.concatenate(
            [jnp.concatenate([re, im], axis=1), jnp.concatenate([-im, re], axis=1)], axis=0
        )

    for k in range(kept_ref.shape[0]):
        ham, deriv, posit, extra = (
            sum((ref[k, j].astype(jnp.float32) for ref in came), kept_ref[k, j]) for j in range(4)
        )
        h_re, h_im = ham[:, :64], ham[:, 64:]
        d_re, d_im = deriv[:, :64], deriv[:, 64:]
        left = jnp.concatenate([posit, h_re + d_im, h_im - d_re], axis=1)
        right = jnp.concatenate(
            [wide(h_re - d_im, h_im + d_re), wide(posit[:, :64], posit[:, 64:])], axis=0
        )
        l_high, l_low = halves_of(left)
        r_high, r_low = halves_of(right)
        product = jnp.dot(
            jnp.concatenate([l_high, l_low, l_high], axis=1),
            jnp.concatenate([r_high, r_high, r_low], axis=0),
            preferred_element_type=jnp.float32,
        )
        hold_ref[...] = extra + factor * product
        even = hold_ref[pl.ds(0, 32, stride=2), :]
        odd = hold_ref[pl.ds(1, 32, stride=2), :]
        for part in range(2):
            at = 64 * part
            flat = jnp.concatenate([even[:, at : at + 64], odd[:, at : at + 64]], axis=1)
            for j in range(32):
                o_ref[k, part : part + 1, 128 * j : 128 * j + 128] = flat[j : j + 1, :]


def final(kept, came):
    return pl.pallas_call(
        final_body,
        out_shape=jax.ShapeDtypeStruct((kept.shape[0], 2, 64 * 64), jnp.float32),
        scratch_shapes=[pltpu.VMEM((64, 128), jnp.float32)],
        compiler_params=pltpu.CompilerParams(vmem_limit_bytes=8 << 20),
        name="final",
    )(kept, *came)


def shift_pairs(stage, shift):
    pairs = []
    for z in range(4):
        for y in range(SIDE):
            for x in range(SIDE):
                for c in range(2):
                    along_y = (c == 0) == (stage == 0)
                    y_to, x_to = ((y + shift) % SIDE, x) if along_y else (y, (x + shift) % SIDE)
                    at = ((z * SIDE + y) * SIDE + x) * 2 + c
                    to = ((z * SIDE + y_to) * SIDE + x_to) * 2 + c
                    pairs.append((at, to))
    return pairs


def on_device(wannier_ops, r_coords, degeneracy, kpoints, bloch_vectors):
    me = lax.axis_index(WHOLE).astype(jnp.int32).reshape(1)
    slots = bloch_vectors.shape[0]
    swap = [(0, 1), (1, 0)]

    partner = lax.ppermute(bloch_vectors, "c", swap)
    near = []
    for shift in (1, 2, 3):
        near.append(lax.ppermute(partner, WHOLE, shift_pairs(0, -shift)))
    far = [pltpu.with_memory_space_constraint(part, pltpu.HBM) for part in (r_coords.T, degeneracy.reshape(1, -1), kpoints.T)]
    ops = pltpu.with_memory_space_constraint(wannier_ops, pltpu.HBM)
    first, phases = fourier(0, (me, *far), ops)
    near, first, phases = lax.optimization_barrier((near, first, phases))
    near = jnp.concatenate([partner, *near], axis=0)
    theirs = {0: near}
    for shift in (2, 1, 3):
        theirs[shift] = lax.ppermute(near, WHOLE, shift_pairs(1, -shift))
    second = fourier(1, phases, ops)
    theirs, first, second = lax.optimization_barrier((theirs, first, second))
    mine = {}
    for shift in (2, 1, 3, 0):
        mine[shift] = lax.ppermute(theirs[shift], "c", swap)
    sums = [part.reshape(4, 64, 128, 128) for part in (first, second)]

    parts, came, got = {}, {}, {}
    for whose, shift in ((1, 2), (1, 1), (0, 2), (1, 3), (0, 1), (0, 3), (1, 0), (0, 0)):
        made = rotate((mine, theirs)[whose], sums, whose, (shift,))
        sums, made = lax.optimization_barrier((sums, made))
        if whose:
            got[shift] = lax.ppermute(made, "c", swap)
            continue
        parts[shift] = made + got[shift]
        if shift:
            came[shift] = lax.ppermute(parts[shift].astype(LINK), WHOLE, shift_pairs(0, shift))
    total = parts[0]
    for shift in (2, 1, 3):
        total = total + came[shift].astype(jnp.float32)
    parts = total.reshape(SIDE, slots, 4, 64, 128)
    return final(parts[0], [lax.ppermute(parts[s], WHOLE, shift_pairs(1, s)) for s in (2, 1, 3)])


def solution(mesh):
    torus = Mesh(mesh.devices.reshape(4, 4, 4, 2), WHOLE)
    in_specs = (
        P(None, PLANE, None, None, None),
        P(PLANE, None),
        P(PLANE),
        P(),
        P(WHOLE, None, None, None),
    )
    return jax.shard_map(
        on_device, mesh=torus, in_specs=in_specs, out_specs=P(WHOLE, None, None), check_vma=False
    )
```

profile of v0, /device:TPU:24, one launch (start us, length us, event | category | flops | bytes accessed | tf_op | source)
XLA Modules:
  0.0 74.6 jit_solution(16498596519005203618)
XLA Ops:
  0.0 0.0 collective-permute-start
  0.0 9.4 %fourier_first.1 = (bf16[256,128,128]{2,1,0:T(8,128)(2,1)S(1)}, bf16[256,256]{1,0:T(8,128)(2,1)S(1)}) custom-call(s32[1]{0:T(128)} %bitcast.me_ref, s32[3,125]{1,0:T(4,128)} %bitcast.23, s32[1,125]{1,0:T(1,128)} %bitcast.24, s32[3,256]{1,0:T(4,128)} %bitcast.22, bf16[2,125,2,128,128]{4,3,2,1,0:T(8,128)(2,1)} %o_ref.3), custom_call_target="tpu_custom_call" | custom-call | flops 4000000000 | bytes 16000000 | tf_op jit(solution)/shard_map/fourier_first/pallas_call | solution.py:136
  9.4 0.0 collective-permute-done
  9.5 0.8 %collective-permute-start.1 = (bf16[2,2,64,128]{3,2,1,0:T(8,128)(2,1)S(1)}, bf16[2,2,64,128]{3,2,1,0:T(8,128)(2,1)S(1)}, u32[]{:S(2)}, u32[]{:S(2)}) collective-permute-start(bf16[2,2,64,128]{3,2,1,0:T(8,128)(2,1)S(1)} %collective-permute-done), channel_id=1, source_target_pairs={{0,24},{1,7},{2,26},{3,1},{4,28},{5,3},{6,30},{7,5},{8,0},{9,15},{... | collective-permute-start | bytes 196616 | tf_op jit(solution)/shard_map/ppermute | solution.py:288
  10.3 0.8 %collective-permute-start.2 = (bf16[2,2,64,128]{3,2,1,0:T(8,128)(2,1)S(1)}, bf16[2,2,64,128]{3,2,1,0:T(8,128)(2,1)S(1)}, u32[]{:S(2)}, u32[]{:S(2)}) collective-permute-start(bf16[2,2,64,128]{3,2,1,0:T(8,128)(2,1)S(1)} %collective-permute-done), channel_id=1, source_target_pairs={{0,16},{1,5},{2,18},{3,7},{4,20},{5,1},{6,22},{7,3},{8,24},{9,13},... | collective-permute-start | bytes 196616 | tf_op jit(solution)/shard_map/ppermute | solution.py:288
  11.1 2.3 %collective-permute-start.3 = (bf16[2,2,64,128]{3,2,1,0:T(8,128)(2,1)S(1)}, bf16[2,2,64,128]{3,2,1,0:T(8,128)(2,1)S(1)}, u32[]{:S(2)}, u32[]{:S(2)}) collective-permute-start(bf16[2,2,64,128]{3,2,1,0:T(8,128)(2,1)S(1)} %collective-permute-done), channel_id=1, source_target_pairs={{0,8},{1,3},{2,10},{3,5},{4,12},{5,7},{6,14},{7,1},{8,16},{9,11},{... | collective-permute-start | bytes 196616 | tf_op jit(solution)/shard_map/ppermute | solution.py:288
  13.4 1.6 %collective-permute-done.1 = bf16[2,2,64,128]{3,2,1,0:T(8,128)(2,1)S(1)} collective-permute-done((bf16[2,2,64,128]{3,2,1,0:T(8,128)(2,1)S(1)}, bf16[2,2,64,128]{3,2,1,0:T(8,128)(2,1)S(1)}, u32[]{:S(2)}, u32[]{:S(2)}) %collective-permute-start.1) | collective-permute-done | bytes 65568 | tf_op jit(solution)/shard_map/ppermute | solution.py:288
  15.0 1.0 %collective-permute-done.2 = bf16[2,2,64,128]{3,2,1,0:T(8,128)(2,1)S(1)} collective-permute-done((bf16[2,2,64,128]{3,2,1,0:T(8,128)(2,1)S(1)}, bf16[2,2,64,128]{3,2,1,0:T(8,128)(2,1)S(1)}, u32[]{:S(2)}, u32[]{:S(2)}) %collective-permute-start.2) | collective-permute-done | bytes 65568 | tf_op jit(solution)/shard_map/ppermute | solution.py:288
  16.0 0.5 collective-permute-done.3
  16.6 2.8 %collective-permute-start.4 = (bf16[8,2,64,128]{3,2,1,0:T(8,128)(2,1)S(1)}, bf16[8,2,64,128]{3,2,1,0:T(8,128)(2,1)S(1)}, u32[]{:S(2)}, u32[]{:S(2)}) collective-permute-start(bf16[8,2,64,128]{3,2,1,0:T(8,128)(2,1)S(1)} %constant_dynamic-update-slice_fusion.refs_0_), channel_id=1, source_target_pairs={{0,6},{1,25},{2,0},{3,27},{4,2},{5,29},{6,4},{7,31},{8,14},{9,1},{... | collective-permute-start | bytes 786440 | tf_op jit(solution)/shard_map/ppermute | solution.py:296
  19.4 0.8 %collective-permute-start.5 = (bf16[8,2,64,128]{3,2,1,0:T(8,128)(2,1)S(1)}, bf16[8,2,64,128]{3,2,1,0:T(8,128)(2,1)S(1)}, u32[]{:S(2)}, u32[]{:S(2)}) collective-permute-start(bf16[8,2,64,128]{3,2,1,0:T(8,128)(2,1)S(1)} %constant_dynamic-update-slice_fusion.refs_0_), channel_id=1, source_target_pairs={{0,4},{1,17},{2,6},{3,19},{4,0},{5,21},{6,2},{7,23},{8,12},{9,25},... | collective-permute-start | bytes 786440 | tf_op jit(solution)/shard_map/ppermute | solution.py:296
  20.2 0.9 %collective-permute-start.6 = (bf16[8,2,64,128]{3,2,1,0:T(8,128)(2,1)S(1)}, bf16[8,2,64,128]{3,2,1,0:T(8,128)(2,1)S(1)}, u32[]{:S(2)}, u32[]{:S(2)}) collective-permute-start(bf16[8,2,64,128]{3,2,1,0:T(8,128)(2,1)S(1)} %constant_dynamic-update-slice_fusion.refs_0_), channel_id=1, source_target_pairs={{0,2},{1,9},{2,4},{3,11},{4,6},{5,13},{6,0},{7,15},{8,10},{9,17},{... | collective-permute-start | bytes 786440 | tf_op jit(solution)/shard_map/ppermute | solution.py:296
  21.1 8.5 %fourier_second.1 = bf16[256,128,128]{2,1,0:T(8,128)(2,1)S(1)} custom-call(bf16[256,256]{1,0:T(8,128)(2,1)S(1)} %get-tuple-element.46.l_ref, bf16[2,125,2,128,128]{4,3,2,1,0:T(8,128)(2,1)} %o_ref.3), custom_call_target="tpu_custom_call" | custom-call | flops 4000000000 | bytes 16000000 | tf_op jit(solution)/shard_map/fourier_second/pallas_call | solution.py:150
  29.7 0.0 collective-permute-done.4.refs_0_
  29.7 0.0 collective-permute-done.5.refs_0_
  29.7 0.4 collective-permute-done.6.refs_0_
  30.1 1.0 %rotate.8 = f32[8,4,64,128]{3,2,1,0:T(8,128)S(1)} custom-call(bf16[8,2,64,128]{3,2,1,0:T(8,128)(2,1)S(1)} %collective-permute-done.5.refs_0_, bf16[4,64,128,128]{3,2,1,0:T(8,128)(2,1)S(1)} %bitcast.14, bf16[4,64,128,128]{3,2,1,0:T(8,128)(2,1)S(1)} %bitcast.6), custom_call_target="tpu_custom_call" | custom-call | flops 960000000 | bytes 3200000 | tf_op jit(solution)/shard_map/rotate/pallas_call | solution.py:204
  31.2 1.0 %rotate.9 = f32[8,4,64,128]{3,2,1,0:T(8,128)S(1)} custom-call(bf16[8,2,64,128]{3,2,1,0:T(8,128)(2,1)S(1)} %collective-permute-done.4.refs_0_, bf16[4,64,128,128]{3,2,1,0:T(8,128)(2,1)S(1)} %bitcast.15, bf16[4,64,128,128]{3,2,1,0:T(8,128)(2,1)S(1)} %bitcast.7), custom_call_target="tpu_custom_call" | custom-call | flops 960000000 | bytes 3200000 | tf_op jit(solution)/shard_map/rotate/pallas_call | solution.py:204
  32.2 0.1 collective-permute-start.14
  32.3 0.5 collective-permute-start.7
  32.8 0.1 collective-permute-start.12
  32.9 0.4 collective-permute-start.8
  33.3 2.0 %collective-permute-done.7.refs_0_ = bf16[8,2,64,128]{3,2,1,0:T(8,128)(2,1)S(1)} collective-permute-done((bf16[8,2,64,128]{3,2,1,0:T(8,128)(2,1)S(1)}, bf16[8,2,64,128]{3,2,1,0:T(8,128)(2,1)S(1)}, u32[]{:S(2)}, u32[]{:S(2)}) %collective-permute-start.7) | collective-permute-done | bytes 262176 | tf_op jit(solution)/shard_map/ppermute | solution.py:301
  35.3 1.0 %rotate.10 = f32[8,4,64,128]{3,2,1,0:T(8,128)S(1)} custom-call(bf16[8,2,64,128]{3,2,1,0:T(8,128)(2,1)S(1)} %collective-permute-done.7.refs_0_, bf16[4,64,128,128]{3,2,1,0:T(8,128)(2,1)S(1)} %bitcast.16, bf16[4,64,128,128]{3,2,1,0:T(8,128)(2,1)S(1)} %bitcast.8), custom_call_target="tpu_custom_call" | custom-call | flops 960000000 | bytes 3200000 | tf_op jit(solution)/shard_map/rotate/pallas_call | solution.py:204
  36.3 1.0 %rotate.11 = f32[8,4,64,128]{3,2,1,0:T(8,128)S(1)} custom-call(bf16[8,2,64,128]{3,2,1,0:T(8,128)(2,1)S(1)} %collective-permute-done.6.refs_0_, bf16[4,64,128,128]{3,2,1,0:T(8,128)(2,1)S(1)} %bitcast.17, bf16[4,64,128,128]{3,2,1,0:T(8,128)(2,1)S(1)} %bitcast.9), custom_call_target="tpu_custom_call" | custom-call | flops 960000000 | bytes 3200000 | tf_op jit(solution)/shard_map/rotate/pallas_call | solution.py:204
  37.4 0.2 collective-permute-start.16
  37.6 0.4 collective-permute-start.9
  38.0 0.0 collective-permute-done.8.refs_0_
  38.0 1.0 %rotate.12 = f32[8,4,64,128]{3,2,1,0:T(8,128)S(1)} custom-call(bf16[8,2,64,128]{3,2,1,0:T(8,128)(2,1)S(1)} %collective-permute-done.8.refs_0_, bf16[4,64,128,128]{3,2,1,0:T(8,128)(2,1)S(1)} %bitcast.18, bf16[4,64,128,128]{3,2,1,0:T(8,128)(2,1)S(1)} %bitcast.10), custom_call_target="tpu_custom_call" | custom-call | flops 960000000 | bytes 3200000 | tf_op jit(solution)/shard_map/rotate/pallas_call | solution.py:204
  39.0 1.5 %collective-permute-done.9.refs_0_ = bf16[8,2,64,128]{3,2,1,0:T(8,128)(2,1)S(1)} collective-permute-done((bf16[8,2,64,128]{3,2,1,0:T(8,128)(2,1)S(1)}, bf16[8,2,64,128]{3,2,1,0:T(8,128)(2,1)S(1)}, u32[]{:S(2)}, u32[]{:S(2)}) %collective-permute-start.9) | collective-permute-done | bytes 262176 | tf_op jit(solution)/shard_map/ppermute | solution.py:301
  40.5 1.0 %rotate.13 = f32[8,4,64,128]{3,2,1,0:T(8,128)S(1)} custom-call(bf16[8,2,64,128]{3,2,1,0:T(8,128)(2,1)S(1)} %collective-permute-done.9.refs_0_, bf16[4,64,128,128]{3,2,1,0:T(8,128)(2,1)S(1)} %bitcast.19, bf16[4,64,128,128]{3,2,1,0:T(8,128)(2,1)S(1)} %bitcast.11), custom_call_target="tpu_custom_call" | custom-call | flops 960000000 | bytes 3200000 | tf_op jit(solution)/shard_map/rotate/pallas_call | solution.py:204
  41.5 1.0 %rotate.14 = f32[8,4,64,128]{3,2,1,0:T(8,128)S(1)} custom-call(bf16[8,2,64,128]{3,2,1,0:T(8,128)(2,1)S(1)} %constant_dynamic-update-slice_fusion.refs_0_, bf16[4,64,128,128]{3,2,1,0:T(8,128)(2,1)S(1)} %bitcast.20, bf16[4,64,128,128]{3,2,1,0:T(8,128)(2,1)S(1)} %bitcast.12), custom_call_target="tpu_custom_call" | custom-call | flops 960000000 | bytes 3200000 | tf_op jit(solution)/shard_map/rotate/pallas_call | solution.py:204
  42.6 0.2 collective-permute-start.11
  42.8 0.0 collective-permute-done.14
  42.8 0.2 add_convert_fusion.1
  43.0 2.7 %collective-permute-start.15 = (bf16[8,4,64,128]{3,2,1,0:T(8,128)(2,1)S(1)}, bf16[8,4,64,128]{3,2,1,0:T(8,128)(2,1)S(1)}, u32[]{:S(2)}, u32[]{:S(2)}) collective-permute-start(bf16[8,4,64,128]{3,2,1,0:T(8,128)(2,1)S(1)} %add_convert_fusion.1), channel_id=1, source_target_pairs={{0,8},{1,3},{2,10},{3,5},{4,12},{5,7},{6,14},{7,1},{8,16},{9,11},{... | collective-permute-start | bytes 1572872 | tf_op jit(solution)/shard_map/ppermute | solution.py:313
  45.7 0.0 collective-permute-done.12
  45.7 0.2 add_convert_fusion.2
  45.9 0.8 %collective-permute-start.13 = (bf16[8,4,64,128]{3,2,1,0:T(8,128)(2,1)S(1)}, bf16[8,4,64,128]{3,2,1,0:T(8,128)(2,1)S(1)}, u32[]{:S(2)}, u32[]{:S(2)}) collective-permute-start(bf16[8,4,64,128]{3,2,1,0:T(8,128)(2,1)S(1)} %add_convert_fusion.2), channel_id=1, source_target_pairs={{0,16},{1,5},{2,18},{3,7},{4,20},{5,1},{6,22},{7,3},{8,24},{9,13},... | collective-permute-start | bytes 1572872 | tf_op jit(solution)/shard_map/ppermute | solution.py:313
  46.7 0.0 collective-permute-done.16
  46.7 0.2 add_convert_fusion
  46.9 0.2 collective-permute-start.17
  47.1 0.3 collective-permute-start.10
  47.4 1.2 %collective-permute-done.10.refs_0_ = bf16[8,2,64,128]{3,2,1,0:T(8,128)(2,1)S(1)} collective-permute-done((bf16[8,2,64,128]{3,2,1,0:T(8,128)(2,1)S(1)}, bf16[8,2,64,128]{3,2,1,0:T(8,128)(2,1)S(1)}, u32[]{:S(2)}, u32[]{:S(2)}) %collective-permute-start.10) | collective-permute-done | bytes 262176 | tf_op jit(solution)/shard_map/ppermute | solution.py:301
  48.6 1.0 %rotate.15 = f32[8,4,64,128]{3,2,1,0:T(8,128)S(1)} custom-call(bf16[8,2,64,128]{3,2,1,0:T(8,128)(2,1)S(1)} %collective-permute-done.10.refs_0_, bf16[4,64,128,128]{3,2,1,0:T(8,128)(2,1)S(1)} %bitcast.21, bf16[4,64,128,128]{3,2,1,0:T(8,128)(2,1)S(1)} %bitcast.13), custom_call_target="tpu_custom_call" | custom-call | flops 960000000 | bytes 3200000 | tf_op jit(solution)/shard_map/rotate/pallas_call | solution.py:204
  49.7 0.0 collective-permute-done.11
  49.7 8.4 %collective-permute-done.15 = bf16[8,4,64,128]{3,2,1,0:T(8,128)(2,1)S(1)} collective-permute-done((bf16[8,4,64,128]{3,2,1,0:T(8,128)(2,1)S(1)}, bf16[8,4,64,128]{3,2,1,0:T(8,128)(2,1)S(1)}, u32[]{:S(2)}, u32[]{:S(2)}) %collective-permute-start.15) | collective-permute-done | bytes 524320 | tf_op jit(solution)/shard_map/ppermute | solution.py:313
  58.1 0.0 collective-permute-done.13
  58.1 4.2 %collective-permute-done.17 = bf16[8,4,64,128]{3,2,1,0:T(8,128)(2,1)S(1)} collective-permute-done((bf16[8,4,64,128]{3,2,1,0:T(8,128)(2,1)S(1)}, bf16[8,4,64,128]{3,2,1,0:T(8,128)(2,1)S(1)}, u32[]{:S(2)}, u32[]{:S(2)}) %collective-permute-start.17) | collective-permute-done | bytes 524320 | tf_op jit(solution)/shard_map/ppermute | solution.py:313
  62.3 0.4 convert_add_fusion
  62.7 0.1 fusion
  62.7 1.5 %collective-permute-start.18 = (f32[2,4,64,128]{3,2,1,0:T(8,128)S(1)}, f32[2,4,64,128]{3,2,1,0:T(8,128)S(1)}, u32[]{:S(2)}, u32[]{:S(2)}) collective-permute-start(f32[2,4,64,128]{3,2,1,0:T(8,128)S(1)} %get-tuple-element.77), channel_id=1, source_target_pairs={{0,4},{1,17},{2,6},{3,19},{4,0},{5,21},{6,2},{7,23},{8,12},{9,25},... | collective-permute-start | bytes 786440 | tf_op jit(solution)/shard_map/ppermute | solution.py:318
  64.2 1.4 %collective-permute-start.19 = (f32[2,4,64,128]{3,2,1,0:T(8,128)S(1)}, f32[2,4,64,128]{3,2,1,0:T(8,128)S(1)}, u32[]{:S(2)}, u32[]{:S(2)}) collective-permute-start(f32[2,4,64,128]{3,2,1,0:T(8,128)S(1)} %get-tuple-element.76), channel_id=1, source_target_pairs={{0,2},{1,9},{2,4},{3,11},{4,6},{5,13},{6,0},{7,15},{8,10},{9,17},{... | collective-permute-start | bytes 786440 | tf_op jit(solution)/shard_map/ppermute | solution.py:318
  65.6 1.9 %collective-permute-start.20 = (f32[2,4,64,128]{3,2,1,0:T(8,128)S(1)}, f32[2,4,64,128]{3,2,1,0:T(8,128)S(1)}, u32[]{:S(2)}, u32[]{:S(2)}) collective-permute-start(f32[2,4,64,128]{3,2,1,0:T(8,128)S(1)} %get-tuple-element.75), channel_id=1, source_target_pairs={{0,6},{1,25},{2,0},{3,27},{4,2},{5,29},{6,4},{7,31},{8,14},{9,1},{... | collective-permute-start | bytes 786440 | tf_op jit(solution)/shard_map/ppermute | solution.py:318
  67.5 3.3 %collective-permute-done.18.refs_0_ = f32[2,4,64,128]{3,2,1,0:T(8,128)S(1)} collective-permute-done((f32[2,4,64,128]{3,2,1,0:T(8,128)S(1)}, f32[2,4,64,128]{3,2,1,0:T(8,128)S(1)}, u32[]{:S(2)}, u32[]{:S(2)}) %collective-permute-start.18) | collective-permute-done | bytes 262176 | tf_op jit(solution)/shard_map/ppermute | solution.py:318
  70.8 2.7 %collective-permute-done.19.refs_1_ = f32[2,4,64,128]{3,2,1,0:T(8,128)S(1)} collective-permute-done((f32[2,4,64,128]{3,2,1,0:T(8,128)S(1)}, f32[2,4,64,128]{3,2,1,0:T(8,128)S(1)}, u32[]{:S(2)}, u32[]{:S(2)}) %collective-permute-start.19) | collective-permute-done | bytes 262176 | tf_op jit(solution)/shard_map/ppermute | solution.py:318
  73.5 0.0 collective-permute-done.20.refs_2_
  73.5 1.1 %final.1 = f32[2,2,4096]{2,1,0:T(2,128)} custom-call(f32[2,4,64,128]{3,2,1,0:T(8,128)S(1)} %get-tuple-element.78.kept_ref, f32[2,4,64,128]{3,2,1,0:T(8,128)S(1)} %collective-permute-done.18.refs_0_, f32[2,4,64,128]{3,2,1,0:T(8,128)S(1)} %collective-permute-done.19.refs_1_, f32[2,4,64,128]{3,2,1,0:T(8,128)S(1)} %collective-permute-done.20.refs_2_), custom_call_target="tpu_custom_call" | custom-call | tf_op jit(solution)/shard_map/final/pallas_call | solution.py:257
  (4 shorter events, 0.0 us)
Async XLA Ops:
  0.0 9.4 %collective-permute-start = (bf16[2,2,64,128]{3,2,1,0:T(8,128)(2,1)}, bf16[2,2,64,128]{3,2,1,0:T(8,128)(2,1)S(1)}, u32[]{:S(2)}, u32[]{:S(2)}) collective-permute-start(bf16[2,2,64,128]{3,2,1,0:T(8,128)(2,1)} %param.9), channel_id=1, source_target_pairs={{0,1},{1,0},{2,3},{3,2},{4,5},{5,4},{6,7},{7,6},{8,9},{9,8},{10,11... | collective-permute-start | bytes 196616 | tf_op jit(solution)/shard_map/ppermute | solution.py:285
  9.5 5.5 %collective-permute-start.1 = (bf16[2,2,64,128]{3,2,1,0:T(8,128)(2,1)S(1)}, bf16[2,2,64,128]{3,2,1,0:T(8,128)(2,1)S(1)}, u32[]{:S(2)}, u32[]{:S(2)}) collective-permute-start(bf16[2,2,64,128]{3,2,1,0:T(8,128)(2,1)S(1)} %collective-permute-done), channel_id=1, source_target_pairs={{0,24},{1,7},{2,26},{3,1},{4,28},{5,3},{6,30},{7,5},{8,0},{9,15},{... | collective-permute-start | bytes 196616 | tf_op jit(solution)/shard_map/ppermute | solution.py:288
  10.3 5.8 %collective-permute-start.2 = (bf16[2,2,64,128]{3,2,1,0:T(8,128)(2,1)S(1)}, bf16[2,2,64,128]{3,2,1,0:T(8,128)(2,1)S(1)}, u32[]{:S(2)}, u32[]{:S(2)}) collective-permute-start(bf16[2,2,64,128]{3,2,1,0:T(8,128)(2,1)S(1)} %collective-permute-done), channel_id=1, source_target_pairs={{0,16},{1,5},{2,18},{3,7},{4,20},{5,1},{6,22},{7,3},{8,24},{9,13},... | collective-permute-start | bytes 196616 | tf_op jit(solution)/shard_map/ppermute | solution.py:288
  11.1 5.5 %collective-permute-start.3 = (bf16[2,2,64,128]{3,2,1,0:T(8,128)(2,1)S(1)}, bf16[2,2,64,128]{3,2,1,0:T(8,128)(2,1)S(1)}, u32[]{:S(2)}, u32[]{:S(2)}) collective-permute-start(bf16[2,2,64,128]{3,2,1,0:T(8,128)(2,1)S(1)} %collective-permute-done), channel_id=1, source_target_pairs={{0,8},{1,3},{2,10},{3,5},{4,12},{5,7},{6,14},{7,1},{8,16},{9,11},{... | collective-permute-start | bytes 196616 | tf_op jit(solution)/shard_map/ppermute | solution.py:288
  16.6 13.1 %collective-permute-start.4 = (bf16[8,2,64,128]{3,2,1,0:T(8,128)(2,1)S(1)}, bf16[8,2,64,128]{3,2,1,0:T(8,128)(2,1)S(1)}, u32[]{:S(2)}, u32[]{:S(2)}) collective-permute-start(bf16[8,2,64,128]{3,2,1,0:T(8,128)(2,1)S(1)} %constant_dynamic-update-slice_fusion.refs_0_), channel_id=1, source_target_pairs={{0,6},{1,25},{2,0},{3,27},{4,2},{5,29},{6,4},{7,31},{8,14},{9,1},{... | collective-permute-start | bytes 786440 | tf_op jit(solution)/shard_map/ppermute | solution.py:296
  19.4 10.3 %collective-permute-start.5 = (bf16[8,2,64,128]{3,2,1,0:T(8,128)(2,1)S(1)}, bf16[8,2,64,128]{3,2,1,0:T(8,128)(2,1)S(1)}, u32[]{:S(2)}, u32[]{:S(2)}) collective-permute-start(bf16[8,2,64,128]{3,2,1,0:T(8,128)(2,1)S(1)} %constant_dynamic-update-slice_fusion.refs_0_), channel_id=1, source_target_pairs={{0,4},{1,17},{2,6},{3,19},{4,0},{5,21},{6,2},{7,23},{8,12},{9,25},... | collective-permute-start | bytes 786440 | tf_op jit(solution)/shard_map/ppermute | solution.py:296
  20.2 9.9 %collective-permute-start.6 = (bf16[8,2,64,128]{3,2,1,0:T(8,128)(2,1)S(1)}, bf16[8,2,64,128]{3,2,1,0:T(8,128)(2,1)S(1)}, u32[]{:S(2)}, u32[]{:S(2)}) collective-permute-start(bf16[8,2,64,128]{3,2,1,0:T(8,128)(2,1)S(1)} %constant_dynamic-update-slice_fusion.refs_0_), channel_id=1, source_target_pairs={{0,2},{1,9},{2,4},{3,11},{4,6},{5,13},{6,0},{7,15},{8,10},{9,17},{... | collective-permute-start | bytes 786440 | tf_op jit(solution)/shard_map/ppermute | solution.py:296
  32.2 10.6 %collective-permute-start.14 = (f32[8,4,64,128]{3,2,1,0:T(8,128)S(1)}, f32[8,4,64,128]{3,2,1,0:T(8,128)S(1)}, u32[]{:S(2)}, u32[]{:S(2)}) collective-permute-start(f32[8,4,64,128]{3,2,1,0:T(8,128)S(1)} %rotate.9), channel_id=1, source_target_pairs={{0,1},{1,0},{2,3},{3,2},{4,5},{5,4},{6,7},{7,6},{8,9},{9,8},{10,11... | collective-permute-start | bytes 3145736 | tf_op jit(solution)/shard_map/ppermute | solution.py:309
  32.3 3.0 %collective-permute-start.7 = (bf16[8,2,64,128]{3,2,1,0:T(8,128)(2,1)S(1)}, bf16[8,2,64,128]{3,2,1,0:T(8,128)(2,1)S(1)}, u32[]{:S(2)}, u32[]{:S(2)}) collective-permute-start(bf16[8,2,64,128]{3,2,1,0:T(8,128)(2,1)S(1)} %collective-permute-done.5.refs_0_), channel_id=1, source_target_pairs={{0,1},{1,0},{2,3},{3,2},{4,5},{5,4},{6,7},{7,6},{8,9},{9,8},{10,11... | collective-permute-start | bytes 786440 | tf_op jit(solution)/shard_map/ppermute | solution.py:301
  32.8 12.9 %collective-permute-start.12 = (f32[8,4,64,128]{3,2,1,0:T(8,128)S(1)}, f32[8,4,64,128]{3,2,1,0:T(8,128)S(1)}, u32[]{:S(2)}, u32[]{:S(2)}) collective-permute-start(f32[8,4,64,128]{3,2,1,0:T(8,128)S(1)} %rotate.8), channel_id=1, source_target_pairs={{0,1},{1,0},{2,3},{3,2},{4,5},{5,4},{6,7},{7,6},{8,9},{9,8},{10,11... | collective-permute-start | bytes 3145736 | tf_op jit(solution)/shard_map/ppermute | solution.py:309
  32.9 5.1 %collective-permute-start.8 = (bf16[8,2,64,128]{3,2,1,0:T(8,128)(2,1)S(1)}, bf16[8,2,64,128]{3,2,1,0:T(8,128)(2,1)S(1)}, u32[]{:S(2)}, u32[]{:S(2)}) collective-permute-start(bf16[8,2,64,128]{3,2,1,0:T(8,128)(2,1)S(1)} %collective-permute-done.4.refs_0_), channel_id=1, source_target_pairs={{0,1},{1,0},{2,3},{3,2},{4,5},{5,4},{6,7},{7,6},{8,9},{9,8},{10,11... | collective-permute-start | bytes 786440 | tf_op jit(solution)/shard_map/ppermute | solution.py:301
  37.4 9.3 %collective-permute-start.16 = (f32[8,4,64,128]{3,2,1,0:T(8,128)S(1)}, f32[8,4,64,128]{3,2,1,0:T(8,128)S(1)}, u32[]{:S(2)}, u32[]{:S(2)}) collective-permute-start(f32[8,4,64,128]{3,2,1,0:T(8,128)S(1)} %rotate.11), channel_id=1, source_target_pairs={{0,1},{1,0},{2,3},{3,2},{4,5},{5,4},{6,7},{7,6},{8,9},{9,8},{10,11... | collective-permute-start | bytes 3145736 | tf_op jit(solution)/shard_map/ppermute | solution.py:309
  37.6 2.9 %collective-permute-start.9 = (bf16[8,2,64,128]{3,2,1,0:T(8,128)(2,1)S(1)}, bf16[8,2,64,128]{3,2,1,0:T(8,128)(2,1)S(1)}, u32[]{:S(2)}, u32[]{:S(2)}) collective-permute-start(bf16[8,2,64,128]{3,2,1,0:T(8,128)(2,1)S(1)} %collective-permute-done.6.refs_0_), channel_id=1, source_target_pairs={{0,1},{1,0},{2,3},{3,2},{4,5},{5,4},{6,7},{7,6},{8,9},{9,8},{10,11... | collective-permute-start | bytes 786440 | tf_op jit(solution)/shard_map/ppermute | solution.py:301
  42.6 7.1 %collective-permute-start.11 = (f32[8,4,64,128]{3,2,1,0:T(8,128)S(1)}, f32[8,4,64,128]{3,2,1,0:T(8,128)S(1)}, u32[]{:S(2)}, u32[]{:S(2)}) collective-permute-start(f32[8,4,64,128]{3,2,1,0:T(8,128)S(1)} %rotate.14), channel_id=1, source_target_pairs={{0,1},{1,0},{2,3},{3,2},{4,5},{5,4},{6,7},{7,6},{8,9},{9,8},{10,11... | collective-permute-start | bytes 3145736 | tf_op jit(solution)/shard_map/ppermute | solution.py:309
  43.0 15.1 %collective-permute-start.15 = (bf16[8,4,64,128]{3,2,1,0:T(8,128)(2,1)S(1)}, bf16[8,4,64,128]{3,2,1,0:T(8,128)(2,1)S(1)}, u32[]{:S(2)}, u32[]{:S(2)}) collective-permute-start(bf16[8,4,64,128]{3,2,1,0:T(8,128)(2,1)S(1)} %add_convert_fusion.1), channel_id=1, source_target_pairs={{0,8},{1,3},{2,10},{3,5},{4,12},{5,7},{6,14},{7,1},{8,16},{9,11},{... | collective-permute-start | bytes 1572872 | tf_op jit(solution)/shard_map/ppermute | solution.py:313
  45.9 12.2 %collective-permute-start.13 = (bf16[8,4,64,128]{3,2,1,0:T(8,128)(2,1)S(1)}, bf16[8,4,64,128]{3,2,1,0:T(8,128)(2,1)S(1)}, u32[]{:S(2)}, u32[]{:S(2)}) collective-permute-start(bf16[8,4,64,128]{3,2,1,0:T(8,128)(2,1)S(1)} %add_convert_fusion.2), channel_id=1, source_target_pairs={{0,16},{1,5},{2,18},{3,7},{4,20},{5,1},{6,22},{7,3},{8,24},{9,13},... | collective-permute-start | bytes 1572872 | tf_op jit(solution)/shard_map/ppermute | solution.py:313
  46.9 15.4 %collective-permute-start.17 = (bf16[8,4,64,128]{3,2,1,0:T(8,128)(2,1)S(1)}, bf16[8,4,64,128]{3,2,1,0:T(8,128)(2,1)S(1)}, u32[]{:S(2)}, u32[]{:S(2)}) collective-permute-start(bf16[8,4,64,128]{3,2,1,0:T(8,128)(2,1)S(1)} %add_convert_fusion), channel_id=1, source_target_pairs={{0,24},{1,7},{2,26},{3,1},{4,28},{5,3},{6,30},{7,5},{8,0},{9,15},{... | collective-permute-start | bytes 1572872 | tf_op jit(solution)/shard_map/ppermute | solution.py:313
  47.1 1.5 %collective-permute-start.10 = (bf16[8,2,64,128]{3,2,1,0:T(8,128)(2,1)S(1)}, bf16[8,2,64,128]{3,2,1,0:T(8,128)(2,1)S(1)}, u32[]{:S(2)}, u32[]{:S(2)}) collective-permute-start(bf16[8,2,64,128]{3,2,1,0:T(8,128)(2,1)S(1)} %constant_dynamic-update-slice_fusion.refs_0_), channel_id=1, source_target_pairs={{0,1},{1,0},{2,3},{3,2},{4,5},{5,4},{6,7},{7,6},{8,9},{9,8},{10,11... | collective-permute-start | bytes 786440 | tf_op jit(solution)/shard_map/ppermute | solution.py:301
  62.7 8.1 %collective-permute-start.18 = (f32[2,4,64,128]{3,2,1,0:T(8,128)S(1)}, f32[2,4,64,128]{3,2,1,0:T(8,128)S(1)}, u32[]{:S(2)}, u32[]{:S(2)}) collective-permute-start(f32[2,4,64,128]{3,2,1,0:T(8,128)S(1)} %get-tuple-element.77), channel_id=1, source_target_pairs={{0,4},{1,17},{2,6},{3,19},{4,0},{5,21},{6,2},{7,23},{8,12},{9,25},... | collective-permute-start | bytes 786440 | tf_op jit(solution)/shard_map/ppermute | solution.py:318
  64.2 9.3 %collective-permute-start.19 = (f32[2,4,64,128]{3,2,1,0:T(8,128)S(1)}, f32[2,4,64,128]{3,2,1,0:T(8,128)S(1)}, u32[]{:S(2)}, u32[]{:S(2)}) collective-permute-start(f32[2,4,64,128]{3,2,1,0:T(8,128)S(1)} %get-tuple-element.76), channel_id=1, source_target_pairs={{0,2},{1,9},{2,4},{3,11},{4,6},{5,13},{6,0},{7,15},{8,10},{9,17},{... | collective-permute-start | bytes 786440 | tf_op jit(solution)/shard_map/ppermute | solution.py:318
  65.6 7.9 %collective-permute-start.20 = (f32[2,4,64,128]{3,2,1,0:T(8,128)S(1)}, f32[2,4,64,128]{3,2,1,0:T(8,128)S(1)}, u32[]{:S(2)}, u32[]{:S(2)}) collective-permute-start(f32[2,4,64,128]{3,2,1,0:T(8,128)S(1)} %get-tuple-element.75), channel_id=1, source_target_pairs={{0,6},{1,25},{2,0},{3,27},{4,2},{5,29},{6,4},{7,31},{8,14},{9,1},{... | collective-permute-start | bytes 786440 | tf_op jit(solution)/shard_map/ppermute | solution.py:318
where the time goes:
time: 75.2 us; the launch traced here: 74.6 us
  Pallas kernels  27.3 us (36%)
  waiting for transfers between devices  26.9 us (36%)
  starting transfers between devices  19.2 us (26%)
  other arithmetic  0.89 us (1%)
    ppermute x3, waiting for transfers between devices, on_device(): lax.ppermute(parts[shift].astype(LINK), WHOLE, shift_pairs(0, shift))  12.6 us
    pallas_call x1, Pallas kernels, fourier(): pl.pallas_call(functools.partial(fourier_first, rows), grid_spec=pltpu.Pr...  9.43 us
    pallas_call x1, Pallas kernels, fourier(): pl.pallas_call(functools.partial(fourier_second, rows), grid=(width // ro...  8.54 us
    pallas_call x8, Pallas kernels, rotate(): pl.pallas_call(functools.partial(rotate_body, shifts, half), in_specs=[wh...  8.22 us
    ppermute x3, waiting for transfers between devices, on_device(): lax.ppermute(parts[s], WHOLE, shift_pairs(1, s))  6.03 us
    ppermute x3, starting transfers between devices, on_device(): lax.ppermute(parts[s], WHOLE, shift_pairs(1, s))  4.73 us
    ppermute x4, waiting for transfers between devices, on_device(): mine[shift] = lax.ppermute(theirs[shift], 'c', swap)  4.71 us
    ppermute x3, starting transfers between devices, on_device(): theirs[shift] = lax.ppermute(near, WHOLE, shift_pairs(1, -shift))  4.52 us
  transfers between devices with their start and end apart: 21, of which 11 were waited for; matrix products, arithmetic and copies ran while one was open for 1% of the time, Pallas kernels for 32%

commit v1 on v0

--- a/solution.py
+++ b/solution.py
@@ -17,8 +17,10 @@
 LINK = jnp.bfloat16
 SIDE = 4
 ROWS = 128
-FOURIER_VMEM = 14 << 20
+FOURIER_VMEM = 10 << 20
 ROTATE_VMEM = 12 << 20
+IN_STEP = 20
+OUT_STEP = 260
 
 
 def owner_place(k, y, x, core):
@@ -58,7 +60,7 @@
     return jnp.concatenate(rows, axis=0).astype(jnp.bfloat16)
 
 
-def fourier_sums(op, rows, left, o_ref, f_ref, raw_ref, sem):
+def fourier_sums(op, rows, left, o_ref, f_ref, raw_ref, turn_ref, sem):
     step = pl.program_id(0)
     depth = raw_ref.shape[0]
 
@@ -80,22 +82,28 @@
     matrix = left()
     fetch(step).wait()
     count = raw_ref.shape[1]
-    halves = []
+
+    @pl.when(step == 0)
+    def _():
+        for part in range(2):
+            for r in range(count, ROWS):
+                turn_ref[pl.ds((part * ROWS + r) * IN_STEP, rows), :] = jnp.zeros((rows, 128), jnp.float32)
+
     for part in range(2):
-        block = raw_ref[step % depth, :, part]
-        block = jnp.concatenate([block, jnp.zeros((ROWS - count, rows, 128), jnp.bfloat16)], axis=0)
-        halves.append(jnp.swapaxes(block, 0, 1))
-    stacked = jnp.concatenate(halves, axis=1)
-    sums = []
+        for r in range(count):
+            block = raw_ref[step % depth, r, part].astype(jnp.float32)
+            turn_ref[pl.ds((part * ROWS + r) * IN_STEP, rows), :] = block
     for pair in range(rows // 2):
-        right = jnp.concatenate([stacked[2 * pair], stacked[2 * pair + 1]], axis=1)
-        both = jnp.dot(matrix, right, preferred_element_type=jnp.float32).astype(f_ref.dtype)
-        sums += [both[:, :128], both[:, 128:]]
-    at = pl.multiple_of(step * rows, rows)
-    f_ref[:, pl.ds(at, rows), :] = jnp.swapaxes(jnp.stack(sums, axis=0), 0, 1)
-
-
-def fourier_first(rows, me_ref, c_ref, d_ref, k_ref, o_ref, f_ref, l_ref, cv_ref, dv_ref, kv_ref, raw_ref, sem, in_sem):
+        right = [
+            turn_ref[pl.ds(2 * pair + i, 2 * ROWS, stride=IN_STEP), :].astype(jnp.bfloat16) for i in range(2)
+        ]
+        both = jnp.dot(matrix, jnp.concatenate(right, axis=1), preferred_element_type=jnp.float32)
+        for i in range(2):
+            at = (step * rows + 2 * pair + i) * OUT_STEP
+            f_ref[pl.ds(at, both.shape[0]), :] = both[:, 128 * i : 128 * i + 128]
+
+
+def fourier_first(rows, me_ref, c_ref, d_ref, k_ref, o_ref, f_ref, l_ref, cv_ref, dv_ref, kv_ref, raw_ref, turn_ref, sem, in_sem):
     step = pl.program_id(0)
     moves = [
         pltpu.make_async_copy(src, dst, in_sem.at[i])
@@ -116,19 +124,23 @@
 
         return l_ref[...]
 
-    fourier_sums(0, rows, left, o_ref, f_ref, raw_ref, sem)
-
-
-def fourier_second(rows, l_ref, o_ref, f_ref, raw_ref, sem):
-    fourier_sums(1, rows, lambda: l_ref[...], o_ref, f_ref, raw_ref, sem)
-
-
-def fourier(op, small, ops, rows=32, depth=3):
+    fourier_sums(0, rows, left, o_ref, f_ref, raw_ref, turn_ref, sem)
+
+
+def fourier_second(rows, l_ref, o_ref, f_ref, raw_ref, turn_ref, sem):
+    fourier_sums(1, rows, lambda: l_ref[...], o_ref, f_ref, raw_ref, turn_ref, sem)
+
+
+def fourier(op, small, ops, rows=16, depth=4):
     _, count, _, width, _ = ops.shape
     lines = 256
     local, far = pl.BlockSpec(memory_space=pltpu.VMEM), pl.BlockSpec(memory_space=pltpu.HBM)
-    scratch = [pltpu.VMEM((depth, count, 2, rows, width), jnp.bfloat16), pltpu.SemaphoreType.DMA((depth,))]
-    out = [jax.ShapeDtypeStruct((lines, width, width), jnp.bfloat16)]
+    scratch = [
+        pltpu.VMEM((depth, count, 2, rows, width), jnp.bfloat16),
+        pltpu.VMEM((2 * ROWS * IN_STEP, width), jnp.float32),
+        pltpu.SemaphoreType.DMA((depth,)),
+    ]
+    out = [jax.ShapeDtypeStruct((width * OUT_STEP, width), jnp.float32)]
     params = pltpu.CompilerParams(dimension_semantics=("arbitrary",), vmem_limit_bytes=FOURIER_VMEM)
     cost = pl.CostEstimate(flops=4_000_000_000, bytes_accessed=16_000_000, transcendentals=0)
     if op == 0:
@@ -173,8 +185,11 @@
             )
             found = []
             for o in range(2):
+                parts = [
+                    f_refs[o][pl.ds(64 * line + k, 128, stride=OUT_STEP), :].astype(jnp.bfloat16) for line in range(4)
+                ]
                 right = jnp.concatenate(
-                    [jnp.concatenate([f_refs[o][2 * p, k], f_refs[o][2 * p + 1, k]], axis=0) for p in range(2)], axis=1
+                    [jnp.concatenate(parts[2 * p : 2 * p + 2], axis=0) for p in range(2)], axis=1
                 )
                 found.append(jnp.dot(left, right, preferred_element_type=jnp.float32))
             mids.append(found)
@@ -282,33 +297,35 @@
     slots = bloch_vectors.shape[0]
     swap = [(0, 1), (1, 0)]
 
-    partner = lax.ppermute(bloch_vectors, "c", swap)
     near = []
     for shift in (1, 2, 3):
-        near.append(lax.ppermute(partner, WHOLE, shift_pairs(0, -shift)))
+        near.append(lax.ppermute(bloch_vectors, WHOLE, shift_pairs(1, -shift)))
     far = [pltpu.with_memory_space_constraint(part, pltpu.HBM) for part in (r_coords.T, degeneracy.reshape(1, -1), kpoints.T)]
     ops = pltpu.with_memory_space_constraint(wannier_ops, pltpu.HBM)
     first, phases = fourier(0, (me, *far), ops)
     near, first, phases = lax.optimization_barrier((near, first, phases))
-    near = jnp.concatenate([partner, *near], axis=0)
-    theirs = {0: near}
+    near = jnp.concatenate([bloch_vectors, *near], axis=0)
+    mine, theirs = {0: near}, {}
     for shift in (2, 1, 3):
-        theirs[shift] = lax.ppermute(near, WHOLE, shift_pairs(1, -shift))
+        mine[shift] = lax.ppermute(near, WHOLE, shift_pairs(0, -shift))
+    theirs[0] = lax.ppermute(near, "c", swap)
     second = fourier(1, phases, ops)
-    theirs, first, second = lax.optimization_barrier((theirs, first, second))
-    mine = {}
-    for shift in (2, 1, 3, 0):
-        mine[shift] = lax.ppermute(theirs[shift], "c", swap)
-    sums = [part.reshape(4, 64, 128, 128) for part in (first, second)]
-
-    parts, came, got = {}, {}, {}
-    for whose, shift in ((1, 2), (1, 1), (0, 2), (1, 3), (0, 1), (0, 3), (1, 0), (0, 0)):
+    sums = [first, second]
+
+    parts, came, got, own = {}, {}, {}, {}
+    for whose, shift in ((0, 0), (1, 0), (0, 2), (1, 2), (1, 1), (1, 3), (0, 1), (0, 3)):
         made = rotate((mine, theirs)[whose], sums, whose, (shift,))
         sums, made = lax.optimization_barrier((sums, made))
-        if whose:
+        if not whose:
+            own[shift] = made
+        else:
             got[shift] = lax.ppermute(made, "c", swap)
-            continue
-        parts[shift] = made + got[shift]
+        if (whose, shift) == (1, 0):
+            sums, mine = lax.optimization_barrier((sums, mine))
+            for other in (2, 1, 3):
+                theirs[other] = lax.ppermute(mine[other], "c", swap)
+    for shift in (2, 1, 3, 0):
+        parts[shift] = own[shift] + got[shift]
         if shift:
             came[shift] = lax.ppermute(parts[shift].astype(LINK), WHOLE, shift_pairs(0, shift))
     total = parts[0]

time: 75.2 us -> 66.5 us (0.88)
  the two profiles are of different devices: /device:TPU:24 before, /device:TPU:98 now
where the time goes in v1:
time: 66.5 us; the launch traced here: 66.4 us
  Pallas kernels  24.3 us (37%)
  starting transfers between devices  20.1 us (30%)
  waiting for transfers between devices  19.9 us (30%)
  other arithmetic  0.97 us (1%)
  local copies, waits for them, and re-layouts  0.96 us (1%)
    ppermute x3, waiting for transfers between devices, on_device(): lax.ppermute(parts[shift].astype(LINK), WHOLE, shift_pairs(0, shift))  11.1 us
    pallas_call x8, Pallas kernels, rotate(): pl.pallas_call(functools.partial(rotate_body, shifts, half), in_specs=[wh...  10.6 us
    ppermute x3, waiting for transfers between devices, on_device(): lax.ppermute(parts[s], WHOLE, shift_pairs(1, s))  7.27 us
    pallas_call x1, Pallas kernels, fourier(): pl.pallas_call(functools.partial(fourier_first, rows), grid_spec=pltpu.Pr...  6.77 us
    pallas_call x1, Pallas kernels, fourier(): pl.pallas_call(functools.partial(fourier_second, rows), grid=(width // ro...  5.88 us
    ppermute x3, starting transfers between devices, on_device(): lax.ppermute(parts[shift].astype(LINK), WHOLE, shift_pairs(0, shift))  4.94 us
    ppermute x3, starting transfers between devices, on_device(): near.append(lax.ppermute(bloch_vectors, WHOLE, shift_pairs(1, -shift)))  4.76 us
    ppermute x3, starting transfers between devices, on_device(): mine[shift] = lax.ppermute(near, WHOLE, shift_pairs(0, -shift))  4.68 us
  transfers between devices with their start and end apart: 20, of which 7 were waited for; matrix products, arithmetic and copies ran while one was open for 2% of the time, Pallas kernels for 35%

profile of v1, /device:TPU:98, one launch (start us, length us, event | category | flops | bytes accessed | tf_op | source)
XLA Modules:
  0.0 66.4 jit_solution(10105449160390944101)
XLA Ops:
  0.0 0.5 collective-permute-start
  0.5 2.4 %collective-permute-start.1 = (bf16[2,2,64,128]{3,2,1,0:T(8,128)(2,1)}, bf16[2,2,64,128]{3,2,1,0:T(8,128)(2,1)S(1)}, u32[]{:S(2)}, u32[]{:S(2)}) collective-permute-start(bf16[2,2,64,128]{3,2,1,0:T(8,128)(2,1)} %param.9), channel_id=1, source_target_pairs={{0,4},{1,17},{2,6},{3,19},{4,0},{5,21},{6,2},{7,23},{8,12},{9,25},... | collective-permute-start | bytes 196616 | tf_op jit(solution)/shard_map/ppermute | solution.py:302
  3.0 1.8 %collective-permute-start.2 = (bf16[2,2,64,128]{3,2,1,0:T(8,128)(2,1)}, bf16[2,2,64,128]{3,2,1,0:T(8,128)(2,1)S(1)}, u32[]{:S(2)}, u32[]{:S(2)}) collective-permute-start(bf16[2,2,64,128]{3,2,1,0:T(8,128)(2,1)} %param.9), channel_id=1, source_target_pairs={{0,2},{1,9},{2,4},{3,11},{4,6},{5,13},{6,0},{7,15},{8,10},{9,17},{... | collective-permute-start | bytes 196616 | tf_op jit(solution)/shard_map/ppermute | solution.py:302
  4.8 6.8 %fourier_first.1 = (f32[33280,128]{1,0:T(8,128)S(1)}, bf16[256,256]{1,0:T(8,128)(2,1)S(1)}) custom-call(s32[1]{0:T(128)} %bitcast.me_ref, s32[3,125]{1,0:T(4,128)} %bitcast.5, s32[1,125]{1,0:T(1,128)} %bitcast.6, s32[3,256]{1,0:T(4,128)} %bitcast.4, bf16[2,125,2,128,128]{4,3,2,1,0:T(8,128)(2,1)} %o_ref.3), custom_call_target="tpu_custom_call" | custom-call | flops 4000000000 | bytes 16000000 | tf_op jit(solution)/shard_map/fourier_first/pallas_call | solution.py:148
  11.5 0.8 %constant_dynamic-update-slice_fusion.3 = bf16[8,2,64,128]{3,2,1,0:T(8,128)(2,1)S(1)} fusion(bf16[2,2,64,128]{3,2,1,0:T(8,128)(2,1)} %param.9), kind=kLoop, calls=%fused_computation.7 | loop fusion | bytes 131072
  12.4 0.0 collective-permute-done
  12.4 0.0 collective-permute-done.1
  12.4 0.0 collective-permute-done.2
  12.5 0.1 collective-permute-start.3
  12.6 3.1 %collective-permute-start.5 = (bf16[8,2,64,128]{3,2,1,0:T(8,128)(2,1)S(1)}, bf16[8,2,64,128]{3,2,1,0:T(8,128)(2,1)S(1)}, u32[]{:S(2)}, u32[]{:S(2)}) collective-permute-start(bf16[8,2,64,128]{3,2,1,0:T(8,128)(2,1)S(1)} %constant_dynamic-update-slice_fusion.refs_0_), channel_id=1, source_target_pairs={{0,24},{1,7},{2,26},{3,1},{4,28},{5,3},{6,30},{7,5},{8,0},{9,15},{... | collective-permute-start | bytes 786440 | tf_op jit(solution)/shard_map/ppermute | solution.py:310
  15.6 0.6 collective-permute-start.6
  16.3 1.0 %collective-permute-start.7 = (bf16[8,2,64,128]{3,2,1,0:T(8,128)(2,1)S(1)}, bf16[8,2,64,128]{3,2,1,0:T(8,128)(2,1)S(1)}, u32[]{:S(2)}, u32[]{:S(2)}) collective-permute-start(bf16[8,2,64,128]{3,2,1,0:T(8,128)(2,1)S(1)} %constant_dynamic-update-slice_fusion.refs_0_), channel_id=1, source_target_pairs={{0,8},{1,3},{2,10},{3,5},{4,12},{5,7},{6,14},{7,1},{8,16},{9,11},{... | collective-permute-start | bytes 786440 | tf_op jit(solution)/shard_map/ppermute | solution.py:310
  17.2 5.9 %fourier_second.1.refs_2_ = f32[33280,128]{1,0:T(8,128)S(1)} custom-call(bf16[256,256]{1,0:T(8,128)(2,1)S(1)} %get-tuple-element.42.l_ref, bf16[2,125,2,128,128]{4,3,2,1,0:T(8,128)(2,1)} %o_ref.3), custom_call_target="tpu_custom_call" | custom-call | flops 4000000000 | bytes 16000000 | tf_op jit(solution)/shard_map/fourier_second/pallas_call | solution.py:162
  23.1 1.3 %rotate.8 = f32[8,4,64,128]{3,2,1,0:T(8,128)S(1)} custom-call(bf16[8,2,64,128]{3,2,1,0:T(8,128)(2,1)S(1)} %constant_dynamic-update-slice_fusion.refs_0_, f32[33280,128]{1,0:T(8,128)S(1)} %get-tuple-element.69.refs_1_, f32[33280,128]{1,0:T(8,128)S(1)} %fourier_second.1.refs_2_), custom_call_target="tpu_custom_call" | custom-call | flops 960000000 | bytes 3200000 | tf_op jit(solution)/shard_map/rotate/pallas_call | solution.py:219
  24.5 0.0 collective-permute-done.3.refs_0_
  24.5 1.3 %rotate.9 = f32[8,4,64,128]{3,2,1,0:T(8,128)S(1)} custom-call(bf16[8,2,64,128]{3,2,1,0:T(8,128)(2,1)S(1)} %collective-permute-done.3.refs_0_, f32[33280,128]{1,0:T(8,128)S(1)} %get-tuple-element.69.refs_1_, f32[33280,128]{1,0:T(8,128)S(1)} %fourier_second.1.refs_2_), custom_call_target="tpu_custom_call" | custom-call | flops 960000000 | bytes 3200000 | tf_op jit(solution)/shard_map/rotate/pallas_call | solution.py:219
  25.8 0.0 collective-permute-done.5.refs_0_
  25.8 0.0 collective-permute-done.6.refs_0_
  25.8 0.5 collective-permute-done.7.refs_0_
  26.3 0.0 collective-permute-start.8
  26.3 1.3 %rotate.10 = f32[8,4,64,128]{3,2,1,0:T(8,128)S(1)} custom-call(bf16[8,2,64,128]{3,2,1,0:T(8,128)(2,1)S(1)} %collective-permute-done.6.refs_0_, f32[33280,128]{1,0:T(8,128)S(1)} %get-tuple-element.69.refs_1_, f32[33280,128]{1,0:T(8,128)S(1)} %fourier_second.1.refs_2_), custom_call_target="tpu_custom_call" | custom-call | flops 960000000 | bytes 3200000 | tf_op jit(solution)/shard_map/rotate/pallas_call | solution.py:219
  27.7 0.6 collective-permute-start.11
  28.2 0.0 collective-permute-done.8.refs_0_
  28.2 1.3 %rotate.11 = f32[8,4,64,128]{3,2,1,0:T(8,128)S(1)} custom-call(bf16[8,2,64,128]{3,2,1,0:T(8,128)(2,1)S(1)} %collective-permute-done.8.refs_0_, f32[33280,128]{1,0:T(8,128)S(1)} %get-tuple-element.69.refs_1_, f32[33280,128]{1,0:T(8,128)S(1)} %fourier_second.1.refs_2_), custom_call_target="tpu_custom_call" | custom-call | flops 960000000 | bytes 3200000 | tf_op jit(solution)/shard_map/rotate/pallas_call | solution.py:219
  29.6 0.1 collective-permute-start.9
  29.7 0.5 collective-permute-start.12
  30.2 0.0 collective-permute-done.11.refs_0_
  30.2 1.3 %rotate.12 = f32[8,4,64,128]{3,2,1,0:T(8,128)S(1)} custom-call(bf16[8,2,64,128]{3,2,1,0:T(8,128)(2,1)S(1)} %collective-permute-done.11.refs_0_, f32[33280,128]{1,0:T(8,128)S(1)} %get-tuple-element.69.refs_1_, f32[33280,128]{1,0:T(8,128)S(1)} %fourier_second.1.refs_2_), custom_call_target="tpu_custom_call" | custom-call | flops 960000000 | bytes 3200000 | tf_op jit(solution)/shard_map/rotate/pallas_call | solution.py:219
  31.5 0.2 collective-permute-start.13
  31.7 1.0 %collective-permute-done.12.refs_0_ = bf16[8,2,64,128]{3,2,1,0:T(8,128)(2,1)S(1)} collective-permute-done((bf16[8,2,64,128]{3,2,1,0:T(8,128)(2,1)S(1)}, bf16[8,2,64,128]{3,2,1,0:T(8,128)(2,1)S(1)}, u32[]{:S(2)}, u32[]{:S(2)}) %collective-permute-start.12) | collective-permute-done | bytes 262176 | tf_op jit(solution)/shard_map/ppermute | solution.py:326
  32.7 1.3 %rotate.13 = f32[8,4,64,128]{3,2,1,0:T(8,128)S(1)} custom-call(bf16[8,2,64,128]{3,2,1,0:T(8,128)(2,1)S(1)} %collective-permute-done.12.refs_0_, f32[33280,128]{1,0:T(8,128)S(1)} %get-tuple-element.69.refs_1_, f32[33280,128]{1,0:T(8,128)S(1)} %fourier_second.1.refs_2_), custom_call_target="tpu_custom_call" | custom-call | flops 960000000 | bytes 3200000 | tf_op jit(solution)/shard_map/rotate/pallas_call | solution.py:219
  34.0 0.4 collective-permute-start.15
  34.4 0.4 collective-permute-start.4
  34.8 1.3 %rotate.14 = f32[8,4,64,128]{3,2,1,0:T(8,128)S(1)} custom-call(bf16[8,2,64,128]{3,2,1,0:T(8,128)(2,1)S(1)} %collective-permute-done.5.refs_0_, f32[33280,128]{1,0:T(8,128)S(1)} %get-tuple-element.69.refs_1_, f32[33280,128]{1,0:T(8,128)S(1)} %fourier_second.1.refs_2_), custom_call_target="tpu_custom_call" | custom-call | flops 960000000 | bytes 3200000 | tf_op jit(solution)/shard_map/rotate/pallas_call | solution.py:219
  36.1 1.3 %rotate.15 = f32[8,4,64,128]{3,2,1,0:T(8,128)S(1)} custom-call(bf16[8,2,64,128]{3,2,1,0:T(8,128)(2,1)S(1)} %collective-permute-done.7.refs_0_, f32[33280,128]{1,0:T(8,128)S(1)} %get-tuple-element.69.refs_1_, f32[33280,128]{1,0:T(8,128)S(1)} %fourier_second.1.refs_2_), custom_call_target="tpu_custom_call" | custom-call | flops 960000000 | bytes 3200000 | tf_op jit(solution)/shard_map/rotate/pallas_call | solution.py:219
  37.5 0.0 collective-permute-done.9
  37.5 0.2 add_convert_fusion.2
  37.7 1.6 %collective-permute-start.10 = (bf16[8,4,64,128]{3,2,1,0:T(8,128)(2,1)S(1)}, bf16[8,4,64,128]{3,2,1,0:T(8,128)(2,1)S(1)}, u32[]{:S(2)}, u32[]{:S(2)}) collective-permute-start(bf16[8,4,64,128]{3,2,1,0:T(8,128)(2,1)S(1)} %add_convert_fusion.2), channel_id=1, source_target_pairs={{0,16},{1,5},{2,18},{3,7},{4,20},{5,1},{6,22},{7,3},{8,24},{9,13},... | collective-permute-start | bytes 1572872 | tf_op jit(solution)/shard_map/ppermute | solution.py:330
  39.2 0.0 collective-permute-done.13
  39.2 0.2 add_convert_fusion.1
  39.4 1.3 %collective-permute-start.14 = (bf16[8,4,64,128]{3,2,1,0:T(8,128)(2,1)S(1)}, bf16[8,4,64,128]{3,2,1,0:T(8,128)(2,1)S(1)}, u32[]{:S(2)}, u32[]{:S(2)}) collective-permute-start(bf16[8,4,64,128]{3,2,1,0:T(8,128)(2,1)S(1)} %add_convert_fusion.1), channel_id=1, source_target_pairs={{0,8},{1,3},{2,10},{3,5},{4,12},{5,7},{6,14},{7,1},{8,16},{9,11},{... | collective-permute-start | bytes 1572872 | tf_op jit(solution)/shard_map/ppermute | solution.py:330
  40.7 0.0 collective-permute-done.15
  40.7 0.2 add_convert_fusion
  40.9 2.1 %collective-permute-start.16 = (bf16[8,4,64,128]{3,2,1,0:T(8,128)(2,1)S(1)}, bf16[8,4,64,128]{3,2,1,0:T(8,128)(2,1)S(1)}, u32[]{:S(2)}, u32[]{:S(2)}) collective-permute-start(bf16[8,4,64,128]{3,2,1,0:T(8,128)(2,1)S(1)} %add_convert_fusion), channel_id=1, source_target_pairs={{0,24},{1,7},{2,26},{3,1},{4,28},{5,3},{6,30},{7,5},{8,0},{9,15},{... | collective-permute-start | bytes 1572872 | tf_op jit(solution)/shard_map/ppermute | solution.py:330
  43.0 0.0 collective-permute-done.4
  43.0 5.5 %collective-permute-done.10 = bf16[8,4,64,128]{3,2,1,0:T(8,128)(2,1)S(1)} collective-permute-done((bf16[8,4,64,128]{3,2,1,0:T(8,128)(2,1)S(1)}, bf16[8,4,64,128]{3,2,1,0:T(8,128)(2,1)S(1)}, u32[]{:S(2)}, u32[]{:S(2)}) %collective-permute-start.10) | collective-permute-done | bytes 524320 | tf_op jit(solution)/shard_map/ppermute | solution.py:330
  48.5 5.5 %collective-permute-done.14 = bf16[8,4,64,128]{3,2,1,0:T(8,128)(2,1)S(1)} collective-permute-done((bf16[8,4,64,128]{3,2,1,0:T(8,128)(2,1)S(1)}, bf16[8,4,64,128]{3,2,1,0:T(8,128)(2,1)S(1)}, u32[]{:S(2)}, u32[]{:S(2)}) %collective-permute-start.14) | collective-permute-done | bytes 524320 | tf_op jit(solution)/shard_map/ppermute | solution.py:330
  54.0 0.0 collective-permute-done.16
  54.0 0.4 convert_add_fusion
  54.5 0.1 fusion
  54.5 1.5 %collective-permute-start.17 = (f32[2,4,64,128]{3,2,1,0:T(8,128)S(1)}, f32[2,4,64,128]{3,2,1,0:T(8,128)S(1)}, u32[]{:S(2)}, u32[]{:S(2)}) collective-permute-start(f32[2,4,64,128]{3,2,1,0:T(8,128)S(1)} %get-tuple-element.75), channel_id=1, source_target_pairs={{0,4},{1,17},{2,6},{3,19},{4,0},{5,21},{6,2},{7,23},{8,12},{9,25},... | collective-permute-start | bytes 786440 | tf_op jit(solution)/shard_map/ppermute | solution.py:335
  56.0 0.3 collective-permute-start.18
  56.3 1.7 %collective-permute-start.19 = (f32[2,4,64,128]{3,2,1,0:T(8,128)S(1)}, f32[2,4,64,128]{3,2,1,0:T(8,128)S(1)}, u32[]{:S(2)}, u32[]{:S(2)}) collective-permute-start(f32[2,4,64,128]{3,2,1,0:T(8,128)S(1)} %get-tuple-element.73), channel_id=1, source_target_pairs={{0,6},{1,25},{2,0},{3,27},{4,2},{5,29},{6,4},{7,31},{8,14},{9,1},{... | collective-permute-start | bytes 786440 | tf_op jit(solution)/shard_map/ppermute | solution.py:335
  58.0 4.6 %collective-permute-done.17.refs_0_ = f32[2,4,64,128]{3,2,1,0:T(8,128)S(1)} collective-permute-done((f32[2,4,64,128]{3,2,1,0:T(8,128)S(1)}, f32[2,4,64,128]{3,2,1,0:T(8,128)S(1)}, u32[]{:S(2)}, u32[]{:S(2)}) %collective-permute-start.17) | collective-permute-done | bytes 262176 | tf_op jit(solution)/shard_map/ppermute | solution.py:335
  62.6 1.3 %collective-permute-done.18.refs_1_ = f32[2,4,64,128]{3,2,1,0:T(8,128)S(1)} collective-permute-done((f32[2,4,64,128]{3,2,1,0:T(8,128)S(1)}, f32[2,4,64,128]{3,2,1,0:T(8,128)S(1)}, u32[]{:S(2)}, u32[]{:S(2)}) %collective-permute-start.18) | collective-permute-done | bytes 262176 | tf_op jit(solution)/shard_map/ppermute | solution.py:335
  63.9 1.4 %collective-permute-done.19.refs_2_ = f32[2,4,64,128]{3,2,1,0:T(8,128)S(1)} collective-permute-done((f32[2,4,64,128]{3,2,1,0:T(8,128)S(1)}, f32[2,4,64,128]{3,2,1,0:T(8,128)S(1)}, u32[]{:S(2)}, u32[]{:S(2)}) %collective-permute-start.19) | collective-permute-done | bytes 262176 | tf_op jit(solution)/shard_map/ppermute | solution.py:335
  65.3 1.1 %final.1 = f32[2,2,4096]{2,1,0:T(2,128)} custom-call(f32[2,4,64,128]{3,2,1,0:T(8,128)S(1)} %get-tuple-element.76.kept_ref, f32[2,4,64,128]{3,2,1,0:T(8,128)S(1)} %collective-permute-done.17.refs_0_, f32[2,4,64,128]{3,2,1,0:T(8,128)S(1)} %collective-permute-done.18.refs_1_, f32[2,4,64,128]{3,2,1,0:T(8,128)S(1)} %collective-permute-done.19.refs_2_), custom_call_target="tpu_custom_call" | custom-call | tf_op jit(solution)/shard_map/final/pallas_call | solution.py:272
  (3 shorter events, 0.0 us)
Async XLA Ops:
  0.0 12.4 %collective-permute-start = (bf16[2,2,64,128]{3,2,1,0:T(8,128)(2,1)}, bf16[2,2,64,128]{3,2,1,0:T(8,128)(2,1)S(1)}, u32[]{:S(2)}, u32[]{:S(2)}) collective-permute-start(bf16[2,2,64,128]{3,2,1,0:T(8,128)(2,1)} %param.9), channel_id=1, source_target_pairs={{0,6},{1,25},{2,0},{3,27},{4,2},{5,29},{6,4},{7,31},{8,14},{9,1},{... | collective-permute-start | bytes 196616 | tf_op jit(solution)/shard_map/ppermute | solution.py:302
  0.5 11.9 %collective-permute-start.1 = (bf16[2,2,64,128]{3,2,1,0:T(8,128)(2,1)}, bf16[2,2,64,128]{3,2,1,0:T(8,128)(2,1)S(1)}, u32[]{:S(2)}, u32[]{:S(2)}) collective-permute-start(bf16[2,2,64,128]{3,2,1,0:T(8,128)(2,1)} %param.9), channel_id=1, source_target_pairs={{0,4},{1,17},{2,6},{3,19},{4,0},{5,21},{6,2},{7,23},{8,12},{9,25},... | collective-permute-start | bytes 196616 | tf_op jit(solution)/shard_map/ppermute | solution.py:302
  3.0 9.4 %collective-permute-start.2 = (bf16[2,2,64,128]{3,2,1,0:T(8,128)(2,1)}, bf16[2,2,64,128]{3,2,1,0:T(8,128)(2,1)S(1)}, u32[]{:S(2)}, u32[]{:S(2)}) collective-permute-start(bf16[2,2,64,128]{3,2,1,0:T(8,128)(2,1)} %param.9), channel_id=1, source_target_pairs={{0,2},{1,9},{2,4},{3,11},{4,6},{5,13},{6,0},{7,15},{8,10},{9,17},{... | collective-permute-start | bytes 196616 | tf_op jit(solution)/shard_map/ppermute | solution.py:302
  12.5 12.0 %collective-permute-start.3 = (bf16[8,2,64,128]{3,2,1,0:T(8,128)(2,1)S(1)}, bf16[8,2,64,128]{3,2,1,0:T(8,128)(2,1)S(1)}, u32[]{:S(2)}, u32[]{:S(2)}) collective-permute-start(bf16[8,2,64,128]{3,2,1,0:T(8,128)(2,1)S(1)} %constant_dynamic-update-slice_fusion.refs_0_), channel_id=1, source_target_pairs={{0,1},{1,0},{2,3},{3,2},{4,5},{5,4},{6,7},{7,6},{8,9},{9,8},{10,11... | collective-permute-start | bytes 786440 | tf_op jit(solution)/shard_map/ppermute | solution.py:311
  12.6 13.2 %collective-permute-start.5 = (bf16[8,2,64,128]{3,2,1,0:T(8,128)(2,1)S(1)}, bf16[8,2,64,128]{3,2,1,0:T(8,128)(2,1)S(1)}, u32[]{:S(2)}, u32[]{:S(2)}) collective-permute-start(bf16[8,2,64,128]{3,2,1,0:T(8,128)(2,1)S(1)} %constant_dynamic-update-slice_fusion.refs_0_), channel_id=1, source_target_pairs={{0,24},{1,7},{2,26},{3,1},{4,28},{5,3},{6,30},{7,5},{8,0},{9,15},{... | collective-permute-start | bytes 786440 | tf_op jit(solution)/shard_map/ppermute | solution.py:310
  15.6 10.2 %collective-permute-start.6 = (bf16[8,2,64,128]{3,2,1,0:T(8,128)(2,1)S(1)}, bf16[8,2,64,128]{3,2,1,0:T(8,128)(2,1)S(1)}, u32[]{:S(2)}, u32[]{:S(2)}) collective-permute-start(bf16[8,2,64,128]{3,2,1,0:T(8,128)(2,1)S(1)} %constant_dynamic-update-slice_fusion.refs_0_), channel_id=1, source_target_pairs={{0,16},{1,5},{2,18},{3,7},{4,20},{5,1},{6,22},{7,3},{8,24},{9,13},... | collective-permute-start | bytes 786440 | tf_op jit(solution)/shard_map/ppermute | solution.py:310
  16.3 10.1 %collective-permute-start.7 = (bf16[8,2,64,128]{3,2,1,0:T(8,128)(2,1)S(1)}, bf16[8,2,64,128]{3,2,1,0:T(8,128)(2,1)S(1)}, u32[]{:S(2)}, u32[]{:S(2)}) collective-permute-start(bf16[8,2,64,128]{3,2,1,0:T(8,128)(2,1)S(1)} %constant_dynamic-update-slice_fusion.refs_0_), channel_id=1, source_target_pairs={{0,8},{1,3},{2,10},{3,5},{4,12},{5,7},{6,14},{7,1},{8,16},{9,11},{... | collective-permute-start | bytes 786440 | tf_op jit(solution)/shard_map/ppermute | solution.py:310
  26.3 1.9 %collective-permute-start.8 = (bf16[8,2,64,128]{3,2,1,0:T(8,128)(2,1)S(1)}, bf16[8,2,64,128]{3,2,1,0:T(8,128)(2,1)S(1)}, u32[]{:S(2)}, u32[]{:S(2)}) collective-permute-start(bf16[8,2,64,128]{3,2,1,0:T(8,128)(2,1)S(1)} %collective-permute-done.6.refs_0_), channel_id=1, source_target_pairs={{0,1},{1,0},{2,3},{3,2},{4,5},{5,4},{6,7},{7,6},{8,9},{9,8},{10,11... | collective-permute-start | bytes 786440 | tf_op jit(solution)/shard_map/ppermute | solution.py:326
  27.7 2.5 %collective-permute-start.11 = (bf16[8,2,64,128]{3,2,1,0:T(8,128)(2,1)S(1)}, bf16[8,2,64,128]{3,2,1,0:T(8,128)(2,1)S(1)}, u32[]{:S(2)}, u32[]{:S(2)}) collective-permute-start(bf16[8,2,64,128]{3,2,1,0:T(8,128)(2,1)S(1)} %collective-permute-done.5.refs_0_), channel_id=1, source_target_pairs={{0,1},{1,0},{2,3},{3,2},{4,5},{5,4},{6,7},{7,6},{8,9},{9,8},{10,11... | collective-permute-start | bytes 786440 | tf_op jit(solution)/shard_map/ppermute | solution.py:326
  29.6 7.9 %collective-permute-start.9 = (f32[8,4,64,128]{3,2,1,0:T(8,128)S(1)}, f32[8,4,64,128]{3,2,1,0:T(8,128)S(1)}, u32[]{:S(2)}, u32[]{:S(2)}) collective-permute-start(f32[8,4,64,128]{3,2,1,0:T(8,128)S(1)} %rotate.11), channel_id=1, source_target_pairs={{0,1},{1,0},{2,3},{3,2},{4,5},{5,4},{6,7},{7,6},{8,9},{9,8},{10,11... | collective-permute-start | bytes 3145736 | tf_op jit(solution)/shard_map/ppermute | solution.py:322
  29.7 3.0 %collective-permute-start.12 = (bf16[8,2,64,128]{3,2,1,0:T(8,128)(2,1)S(1)}, bf16[8,2,64,128]{3,2,1,0:T(8,128)(2,1)S(1)}, u32[]{:S(2)}, u32[]{:S(2)}) collective-permute-start(bf16[8,2,64,128]{3,2,1,0:T(8,128)(2,1)S(1)} %collective-permute-done.7.refs_0_), channel_id=1, source_target_pairs={{0,1},{1,0},{2,3},{3,2},{4,5},{5,4},{6,7},{7,6},{8,9},{9,8},{10,11... | collective-permute-start | bytes 786440 | tf_op jit(solution)/shard_map/ppermute | solution.py:326
  31.5 7.7 %collective-permute-start.13 = (f32[8,4,64,128]{3,2,1,0:T(8,128)S(1)}, f32[8,4,64,128]{3,2,1,0:T(8,128)S(1)}, u32[]{:S(2)}, u32[]{:S(2)}) collective-permute-start(f32[8,4,64,128]{3,2,1,0:T(8,128)S(1)} %rotate.12), channel_id=1, source_target_pairs={{0,1},{1,0},{2,3},{3,2},{4,5},{5,4},{6,7},{7,6},{8,9},{9,8},{10,11... | collective-permute-start | bytes 3145736 | tf_op jit(solution)/shard_map/ppermute | solution.py:322
  34.0 6.7 %collective-permute-start.15 = (f32[8,4,64,128]{3,2,1,0:T(8,128)S(1)}, f32[8,4,64,128]{3,2,1,0:T(8,128)S(1)}, u32[]{:S(2)}, u32[]{:S(2)}) collective-permute-start(f32[8,4,64,128]{3,2,1,0:T(8,128)S(1)} %rotate.13), channel_id=1, source_target_pairs={{0,1},{1,0},{2,3},{3,2},{4,5},{5,4},{6,7},{7,6},{8,9},{9,8},{10,11... | collective-permute-start | bytes 3145736 | tf_op jit(solution)/shard_map/ppermute | solution.py:322
  34.4 8.6 %collective-permute-start.4 = (f32[8,4,64,128]{3,2,1,0:T(8,128)S(1)}, f32[8,4,64,128]{3,2,1,0:T(8,128)S(1)}, u32[]{:S(2)}, u32[]{:S(2)}) collective-permute-start(f32[8,4,64,128]{3,2,1,0:T(8,128)S(1)} %rotate.9), channel_id=1, source_target_pairs={{0,1},{1,0},{2,3},{3,2},{4,5},{5,4},{6,7},{7,6},{8,9},{9,8},{10,11... | collective-permute-start | bytes 3145736 | tf_op jit(solution)/shard_map/ppermute | solution.py:322
  37.7 10.9 %collective-permute-start.10 = (bf16[8,4,64,128]{3,2,1,0:T(8,128)(2,1)S(1)}, bf16[8,4,64,128]{3,2,1,0:T(8,128)(2,1)S(1)}, u32[]{:S(2)}, u32[]{:S(2)}) collective-permute-start(bf16[8,4,64,128]{3,2,1,0:T(8,128)(2,1)S(1)} %add_convert_fusion.2), channel_id=1, source_target_pairs={{0,16},{1,5},{2,18},{3,7},{4,20},{5,1},{6,22},{7,3},{8,24},{9,13},... | collective-permute-start | bytes 1572872 | tf_op jit(solution)/shard_map/ppermute | solution.py:330
  39.4 14.6 %collective-permute-start.14 = (bf16[8,4,64,128]{3,2,1,0:T(8,128)(2,1)S(1)}, bf16[8,4,64,128]{3,2,1,0:T(8,128)(2,1)S(1)}, u32[]{:S(2)}, u32[]{:S(2)}) collective-permute-start(bf16[8,4,64,128]{3,2,1,0:T(8,128)(2,1)S(1)} %add_convert_fusion.1), channel_id=1, source_target_pairs={{0,8},{1,3},{2,10},{3,5},{4,12},{5,7},{6,14},{7,1},{8,16},{9,11},{... | collective-permute-start | bytes 1572872 | tf_op jit(solution)/shard_map/ppermute | solution.py:330
  40.9 13.2 %collective-permute-start.16 = (bf16[8,4,64,128]{3,2,1,0:T(8,128)(2,1)S(1)}, bf16[8,4,64,128]{3,2,1,0:T(8,128)(2,1)S(1)}, u32[]{:S(2)}, u32[]{:S(2)}) collective-permute-start(bf16[8,4,64,128]{3,2,1,0:T(8,128)(2,1)S(1)} %add_convert_fusion), channel_id=1, source_target_pairs={{0,24},{1,7},{2,26},{3,1},{4,28},{5,3},{6,30},{7,5},{8,0},{9,15},{... | collective-permute-start | bytes 1572872 | tf_op jit(solution)/shard_map/ppermute | solution.py:330
  54.5 8.1 %collective-permute-start.17 = (f32[2,4,64,128]{3,2,1,0:T(8,128)S(1)}, f32[2,4,64,128]{3,2,1,0:T(8,128)S(1)}, u32[]{:S(2)}, u32[]{:S(2)}) collective-permute-start(f32[2,4,64,128]{3,2,1,0:T(8,128)S(1)} %get-tuple-element.75), channel_id=1, source_target_pairs={{0,4},{1,17},{2,6},{3,19},{4,0},{5,21},{6,2},{7,23},{8,12},{9,25},... | collective-permute-start | bytes 786440 | tf_op jit(solution)/shard_map/ppermute | solution.py:335
  56.0 7.9 %collective-permute-start.18 = (f32[2,4,64,128]{3,2,1,0:T(8,128)S(1)}, f32[2,4,64,128]{3,2,1,0:T(8,128)S(1)}, u32[]{:S(2)}, u32[]{:S(2)}) collective-permute-start(f32[2,4,64,128]{3,2,1,0:T(8,128)S(1)} %get-tuple-element.74), channel_id=1, source_target_pairs={{0,2},{1,9},{2,4},{3,11},{4,6},{5,13},{6,0},{7,15},{8,10},{9,17},{... | collective-permute-start | bytes 786440 | tf_op jit(solution)/shard_map/ppermute | solution.py:335
  56.3 9.0 %collective-permute-start.19 = (f32[2,4,64,128]{3,2,1,0:T(8,128)S(1)}, f32[2,4,64,128]{3,2,1,0:T(8,128)S(1)}, u32[]{:S(2)}, u32[]{:S(2)}) collective-permute-start(f32[2,4,64,128]{3,2,1,0:T(8,128)S(1)} %get-tuple-element.73), channel_id=1, source_target_pairs={{0,6},{1,25},{2,0},{3,27},{4,2},{5,29},{6,4},{7,31},{8,14},{9,1},{... | collective-permute-start | bytes 786440 | tf_op jit(solution)/shard_map/ppermute | solution.py:335

commit v2 on v1

--- a/solution.py
+++ b/solution.py
@@ -232,6 +232,27 @@
     return high, (value - high.astype(jnp.float32)).astype(jnp.bfloat16)
 
 
+def collect_body(half, own_ref, got_ref, far_ref, up_ref, down_ref, *out_refs):
+    for place, out_ref in enumerate(out_refs):
+        for slot in range(2):
+            near = 2 * place + slot
+            at = 4 * half + near
+            value = own_ref[at] + got_ref[at] + far_ref[at].astype(jnp.float32)
+            out_ref[slot] = value + up_ref[near].astype(jnp.float32) + down_ref[near].astype(jnp.float32)
+
+
+def collect(half, own, got, came):
+    whole = pl.BlockSpec(memory_space=pltpu.VMEM)
+    return pl.pallas_call(
+        functools.partial(collect_body, half),
+        in_specs=[whole] * 5,
+        out_specs=[whole] * 2,
+        out_shape=[jax.ShapeDtypeStruct((2, 4, 64, 128), jnp.float32)] * 2,
+        compiler_params=pltpu.CompilerParams(vmem_limit_bytes=8 << 20),
+        name="collect",
+    )(own, got, *came)
+
+
 def final_body(kept_ref, *refs):
     came, o_ref, hold_ref = refs[:-2], refs[-2], refs[-1]
     factor = 1.0 / math.sqrt(64)
@@ -294,7 +315,6 @@
 
 def on_device(wannier_ops, r_coords, degeneracy, kpoints, bloch_vectors):
     me = lax.axis_index(WHOLE).astype(jnp.int32).reshape(1)
-    slots = bloch_vectors.shape[0]
     swap = [(0, 1), (1, 0)]
 
     near = []
@@ -312,27 +332,38 @@
     second = fourier(1, phases, ops)
     sums = [first, second]
 
-    parts, came, got, own = {}, {}, {}, {}
-    for whose, shift in ((0, 0), (1, 0), (0, 2), (1, 2), (1, 1), (1, 3), (0, 1), (0, 3)):
+    got, own, held = {}, {}, {}
+    for whose, shift in ((0, 2), (1, 2), (0, 1), (1, 1), (0, 3), (1, 3), (0, 0), (1, 0)):
+        if not whose and shift:
+            theirs[shift] = lax.ppermute(mine[shift], "c", swap)
         made = rotate((mine, theirs)[whose], sums, whose, (shift,))
         sums, made = lax.optimization_barrier((sums, made))
         if not whose:
             own[shift] = made
-        else:
-            got[shift] = lax.ppermute(made, "c", swap)
-        if (whose, shift) == (1, 0):
-            sums, mine = lax.optimization_barrier((sums, mine))
-            for other in (2, 1, 3):
-                theirs[other] = lax.ppermute(mine[other], "c", swap)
-    for shift in (2, 1, 3, 0):
-        parts[shift] = own[shift] + got[shift]
-        if shift:
-            came[shift] = lax.ppermute(parts[shift].astype(LINK), WHOLE, shift_pairs(0, shift))
-    total = parts[0]
-    for shift in (2, 1, 3):
-        total = total + came[shift].astype(jnp.float32)
-    parts = total.reshape(SIDE, slots, 4, 64, 128)
-    return final(parts[0], [lax.ppermute(parts[s], WHOLE, shift_pairs(1, s)) for s in (2, 1, 3)])
+            continue
+        got[shift] = lax.ppermute(made, "c", swap)
+    late = [own[1], got[1], own[3], got[3]]
+    *late, sums = lax.optimization_barrier((*late, sums))
+    held[1], held[3] = late[:2], late[2:]
+
+    def part(shift, half, after=False):
+        first, second = held[shift] if after else (own[shift], got[shift])
+        return first[4 * half : 4 * half + 4] + second[4 * half : 4 * half + 4]
+
+    came = {}
+    whole = lax.ppermute((own[2] + got[2]).astype(LINK), WHOLE, shift_pairs(0, 2))
+    for half in (1, 0):
+        for shift in (1, 3):
+            came[shift, half] = lax.ppermute(part(shift, half, half == 0).astype(LINK), WHOLE, shift_pairs(0, shift))
+    last, kept = [], None
+    for half in (1, 0):
+        total = collect(half, own[0], got[0], (whole, came[1, half], came[3, half]))
+        for place in (0, 1):
+            if half or place:
+                last.append(lax.ppermute(total[place], WHOLE, shift_pairs(1, 2 * half + place)))
+            else:
+                kept = total[0]
+    return final(kept, last)
 
 
 def solution(mesh):

time: 66.5 us -> 74.3 us (1.12)
  the two profiles are of different devices: /device:TPU:98 before, /device:TPU:66 now
where the time goes in v2:
time: 74.3 us; the launch traced here: 74.1 us
  waiting for transfers between devices  25.9 us (35%)
  Pallas kernels  24.5 us (33%)
  starting transfers between devices  22.1 us (30%)
  local copies, waits for them, and re-layouts  0.89 us (1%)
    ppermute x4, waiting for transfers between devices, on_device(): lax.ppermute(part(shift, half, half == 0).astype(LINK), WHOLE, shift_pair...  13.2 us
    pallas_call x8, Pallas kernels, rotate(): pl.pallas_call(functools.partial(rotate_body, shifts, half), in_specs=[wh...  10.6 us
    pallas_call x1, Pallas kernels, fourier(): pl.pallas_call(functools.partial(fourier_first, rows), grid_spec=pltpu.Pr...  6.77 us
    ppermute x3, waiting for transfers between devices, on_device(): lax.ppermute(total[place], WHOLE, shift_pairs(1, 2 * half + place))  6.36 us
    pallas_call x1, Pallas kernels, fourier(): pl.pallas_call(functools.partial(fourier_second, rows), grid=(width // ro...  5.88 us
    ppermute x4, starting transfers between devices, on_device(): lax.ppermute(part(shift, half, half == 0).astype(LINK), WHOLE, shift_pair...  5.43 us
    ppermute x3, starting transfers between devices, on_device(): mine[shift] = lax.ppermute(near, WHOLE, shift_pairs(0, -shift))  5.3 us
    ppermute x3, starting transfers between devices, on_device(): near.append(lax.ppermute(bloch_vectors, WHOLE, shift_pairs(1, -shift)))  4.76 us
  transfers between devices with their start and end apart: 22, of which 7 were waited for; matrix products, arithmetic and copies ran while one was open for 2% of the time, Pallas kernels for 30%

profile of v2, /device:TPU:66, one launch (start us, length us, event | category | flops | bytes accessed | tf_op | source)
XLA Modules:
  0.0 74.1 jit_solution(13233037669613963694)
XLA Ops:
  0.0 0.5 collective-permute-start
  0.5 2.4 %collective-permute-start.1 = (bf16[2,2,64,128]{3,2,1,0:T(8,128)(2,1)}, bf16[2,2,64,128]{3,2,1,0:T(8,128)(2,1)S(1)}, u32[]{:S(2)}, u32[]{:S(2)}) collective-permute-start(bf16[2,2,64,128]{3,2,1,0:T(8,128)(2,1)} %param.9), channel_id=1, source_target_pairs={{0,4},{1,17},{2,6},{3,19},{4,0},{5,21},{6,2},{7,23},{8,12},{9,25},... | collective-permute-start | bytes 196616 | tf_op jit(solution)/shard_map/ppermute | solution.py:322
  3.0 1.8 %collective-permute-start.2 = (bf16[2,2,64,128]{3,2,1,0:T(8,128)(2,1)}, bf16[2,2,64,128]{3,2,1,0:T(8,128)(2,1)S(1)}, u32[]{:S(2)}, u32[]{:S(2)}) collective-permute-start(bf16[2,2,64,128]{3,2,1,0:T(8,128)(2,1)} %param.9), channel_id=1, source_target_pairs={{0,2},{1,9},{2,4},{3,11},{4,6},{5,13},{6,0},{7,15},{8,10},{9,17},{... | collective-permute-start | bytes 196616 | tf_op jit(solution)/shard_map/ppermute | solution.py:322
  4.8 6.8 %fourier_first.1 = (f32[33280,128]{1,0:T(8,128)S(1)}, bf16[256,256]{1,0:T(8,128)(2,1)S(1)}) custom-call(s32[1]{0:T(128)} %bitcast.me_ref, s32[3,125]{1,0:T(4,128)} %bitcast.5, s32[1,125]{1,0:T(1,128)} %bitcast.6, s32[3,256]{1,0:T(4,128)} %bitcast.4, bf16[2,125,2,128,128]{4,3,2,1,0:T(8,128)(2,1)} %o_ref.3), custom_call_target="tpu_custom_call" | custom-call | flops 4000000000 | bytes 16000000 | tf_op jit(solution)/shard_map/fourier_first/pallas_call | solution.py:148
  11.5 0.8 %constant_dynamic-update-slice_fusion.3 = bf16[8,2,64,128]{3,2,1,0:T(8,128)(2,1)S(1)} fusion(bf16[2,2,64,128]{3,2,1,0:T(8,128)(2,1)} %param.9), kind=kLoop, calls=%fused_computation.10 | loop fusion | bytes 131072
  12.4 0.0 collective-permute-done
  12.4 0.0 collective-permute-done.1
  12.4 0.0 collective-permute-done.2
  12.5 3.3 %collective-permute-start.3 = (bf16[8,2,64,128]{3,2,1,0:T(8,128)(2,1)S(1)}, bf16[8,2,64,128]{3,2,1,0:T(8,128)(2,1)S(1)}, u32[]{:S(2)}, u32[]{:S(2)}) collective-permute-start(bf16[8,2,64,128]{3,2,1,0:T(8,128)(2,1)S(1)} %constant_dynamic-update-slice_fusion.refs_0_), channel_id=1, source_target_pairs={{0,16},{1,5},{2,18},{3,7},{4,20},{5,1},{6,22},{7,3},{8,24},{9,13},... | collective-permute-start | bytes 786440 | tf_op jit(solution)/shard_map/ppermute | solution.py:330
  15.7 1.1 %collective-permute-start.5 = (bf16[8,2,64,128]{3,2,1,0:T(8,128)(2,1)S(1)}, bf16[8,2,64,128]{3,2,1,0:T(8,128)(2,1)S(1)}, u32[]{:S(2)}, u32[]{:S(2)}) collective-permute-start(bf16[8,2,64,128]{3,2,1,0:T(8,128)(2,1)S(1)} %constant_dynamic-update-slice_fusion.refs_0_), channel_id=1, source_target_pairs={{0,24},{1,7},{2,26},{3,1},{4,28},{5,3},{6,30},{7,5},{8,0},{9,15},{... | collective-permute-start | bytes 786440 | tf_op jit(solution)/shard_map/ppermute | solution.py:330
  16.8 1.0 %collective-permute-start.7 = (bf16[8,2,64,128]{3,2,1,0:T(8,128)(2,1)S(1)}, bf16[8,2,64,128]{3,2,1,0:T(8,128)(2,1)S(1)}, u32[]{:S(2)}, u32[]{:S(2)}) collective-permute-start(bf16[8,2,64,128]{3,2,1,0:T(8,128)(2,1)S(1)} %constant_dynamic-update-slice_fusion.refs_0_), channel_id=1, source_target_pairs={{0,8},{1,3},{2,10},{3,5},{4,12},{5,7},{6,14},{7,1},{8,16},{9,11},{... | collective-permute-start | bytes 786440 | tf_op jit(solution)/shard_map/ppermute | solution.py:330
  17.8 2.7 %collective-permute-done.3.refs_0_ = bf16[8,2,64,128]{3,2,1,0:T(8,128)(2,1)S(1)} collective-permute-done((bf16[8,2,64,128]{3,2,1,0:T(8,128)(2,1)S(1)}, bf16[8,2,64,128]{3,2,1,0:T(8,128)(2,1)S(1)}, u32[]{:S(2)}, u32[]{:S(2)}) %collective-permute-start.3) | collective-permute-done | bytes 262176 | tf_op jit(solution)/shard_map/ppermute | solution.py:330
  20.4 0.0 collective-permute-start.4
  20.4 5.9 %fourier_second.1.refs_2_ = f32[33280,128]{1,0:T(8,128)S(1)} custom-call(bf16[256,256]{1,0:T(8,128)(2,1)S(1)} %get-tuple-element.45.l_ref, bf16[2,125,2,128,128]{4,3,2,1,0:T(8,128)(2,1)} %o_ref.3), custom_call_target="tpu_custom_call" | custom-call | flops 4000000000 | bytes 16000000 | tf_op jit(solution)/shard_map/fourier_second/pallas_call | solution.py:162
  26.3 0.0 collective-permute-done.5.refs_0_
  26.3 0.6 collective-permute-start.6
  26.9 1.3 %rotate.8 = f32[8,4,64,128]{3,2,1,0:T(8,128)S(1)} custom-call(bf16[8,2,64,128]{3,2,1,0:T(8,128)(2,1)S(1)} %collective-permute-done.3.refs_0_, f32[33280,128]{1,0:T(8,128)S(1)} %get-tuple-element.62.refs_1_, f32[33280,128]{1,0:T(8,128)S(1)} %fourier_second.1.refs_2_), custom_call_target="tpu_custom_call" | custom-call | flops 960000000 | bytes 3200000 | tf_op jit(solution)/shard_map/rotate/pallas_call | solution.py:219
  28.2 0.0 collective-permute-done.7.refs_0_
  28.2 0.1 collective-permute-start.8
  28.3 0.0 collective-permute-done.4.refs_0_
  28.3 1.3 %rotate.9 = f32[8,4,64,128]{3,2,1,0:T(8,128)S(1)} custom-call(bf16[8,2,64,128]{3,2,1,0:T(8,128)(2,1)S(1)} %collective-permute-done.4.refs_0_, f32[33280,128]{1,0:T(8,128)S(1)} %get-tuple-element.62.refs_1_, f32[33280,128]{1,0:T(8,128)S(1)} %fourier_second.1.refs_2_), custom_call_target="tpu_custom_call" | custom-call | flops 960000000 | bytes 3200000 | tf_op jit(solution)/shard_map/rotate/pallas_call | solution.py:219
  29.7 1.3 %rotate.10 = f32[8,4,64,128]{3,2,1,0:T(8,128)S(1)} custom-call(bf16[8,2,64,128]{3,2,1,0:T(8,128)(2,1)S(1)} %collective-permute-done.5.refs_0_, f32[33280,128]{1,0:T(8,128)S(1)} %get-tuple-element.62.refs_1_, f32[33280,128]{1,0:T(8,128)S(1)} %fourier_second.1.refs_2_), custom_call_target="tpu_custom_call" | custom-call | flops 960000000 | bytes 3200000 | tf_op jit(solution)/shard_map/rotate/pallas_call | solution.py:219
  31.0 0.0 collective-permute-done.6.refs_0_
  31.0 1.3 %rotate.11 = f32[8,4,64,128]{3,2,1,0:T(8,128)S(1)} custom-call(bf16[8,2,64,128]{3,2,1,0:T(8,128)(2,1)S(1)} %collective-permute-done.6.refs_0_, f32[33280,128]{1,0:T(8,128)S(1)} %get-tuple-element.62.refs_1_, f32[33280,128]{1,0:T(8,128)S(1)} %fourier_second.1.refs_2_), custom_call_target="tpu_custom_call" | custom-call | flops 960000000 | bytes 3200000 | tf_op jit(solution)/shard_map/rotate/pallas_call | solution.py:219
  32.3 1.3 %rotate.12 = f32[8,4,64,128]{3,2,1,0:T(8,128)S(1)} custom-call(bf16[8,2,64,128]{3,2,1,0:T(8,128)(2,1)S(1)} %collective-permute-done.7.refs_0_, f32[33280,128]{1,0:T(8,128)S(1)} %get-tuple-element.62.refs_1_, f32[33280,128]{1,0:T(8,128)S(1)} %fourier_second.1.refs_2_), custom_call_target="tpu_custom_call" | custom-call | flops 960000000 | bytes 3200000 | tf_op jit(solution)/shard_map/rotate/pallas_call | solution.py:219
  33.7 0.0 collective-permute-done.8.refs_0_
  33.7 1.3 %rotate.13 = f32[8,4,64,128]{3,2,1,0:T(8,128)S(1)} custom-call(bf16[8,2,64,128]{3,2,1,0:T(8,128)(2,1)S(1)} %collective-permute-done.8.refs_0_, f32[33280,128]{1,0:T(8,128)S(1)} %get-tuple-element.62.refs_1_, f32[33280,128]{1,0:T(8,128)S(1)} %fourier_second.1.refs_2_), custom_call_target="tpu_custom_call" | custom-call | flops 960000000 | bytes 3200000 | tf_op jit(solution)/shard_map/rotate/pallas_call | solution.py:219
  35.0 0.6 collective-permute-start.14
  35.6 0.1 collective-permute-start.13
  35.7 0.4 collective-permute-start.11
  36.1 0.1 collective-permute-start.9
  36.2 1.3 %rotate.14.own_ref = f32[8,4,64,128]{3,2,1,0:T(8,128)S(1)} custom-call(bf16[8,2,64,128]{3,2,1,0:T(8,128)(2,1)S(1)} %constant_dynamic-update-slice_fusion.refs_0_, f32[33280,128]{1,0:T(8,128)S(1)} %get-tuple-element.62.refs_1_, f32[33280,128]{1,0:T(8,128)S(1)} %fourier_second.1.refs_2_), custom_call_target="tpu_custom_call" | custom-call | flops 960000000 | bytes 3200000 | tf_op jit(solution)/shard_map/rotate/pallas_call | solution.py:219
  37.5 3.7 %collective-permute-done.9.refs_0_ = bf16[8,2,64,128]{3,2,1,0:T(8,128)(2,1)S(1)} collective-permute-done((bf16[8,2,64,128]{3,2,1,0:T(8,128)(2,1)S(1)}, bf16[8,2,64,128]{3,2,1,0:T(8,128)(2,1)S(1)}, u32[]{:S(2)}, u32[]{:S(2)}) %collective-permute-start.9) | collective-permute-done | bytes 262176 | tf_op jit(solution)/shard_map/ppermute | solution.py:331
  41.2 1.3 %rotate.15 = f32[8,4,64,128]{3,2,1,0:T(8,128)S(1)} custom-call(bf16[8,2,64,128]{3,2,1,0:T(8,128)(2,1)S(1)} %collective-permute-done.9.refs_0_, f32[33280,128]{1,0:T(8,128)S(1)} %get-tuple-element.62.refs_1_, f32[33280,128]{1,0:T(8,128)S(1)} %fourier_second.1.refs_2_), custom_call_target="tpu_custom_call" | custom-call | flops 960000000 | bytes 3200000 | tf_op jit(solution)/shard_map/rotate/pallas_call | solution.py:219
  42.6 0.5 collective-permute-start.10
  43.0 0.0 collective-permute-done.14
  43.0 0.1 fusion
  43.1 3.2 %collective-permute-start.18 = (bf16[4,4,64,128]{3,2,1,0:T(8,128)(2,1)S(1)}, bf16[4,4,64,128]{3,2,1,0:T(8,128)(2,1)S(1)}, u32[]{:S(2)}, u32[]{:S(2)}) collective-permute-start(bf16[4,4,64,128]{3,2,1,0:T(8,128)(2,1)S(1)} %fusion), channel_id=1, source_target_pairs={{0,24},{1,7},{2,26},{3,1},{4,28},{5,3},{6,30},{7,5},{8,0},{9,15},{... | collective-permute-start | bytes 786440 | tf_op jit(solution)/shard_map/ppermute | solution.py:357
  46.3 0.0 collective-permute-done.13
  46.3 0.1 fusion.1
  46.4 0.1 collective-permute-start.17
  46.4 0.0 collective-permute-done.11
  46.5 0.2 add_convert_fusion
  46.6 2.3 %collective-permute-start.12 = (bf16[8,4,64,128]{3,2,1,0:T(8,128)(2,1)S(1)}, bf16[8,4,64,128]{3,2,1,0:T(8,128)(2,1)S(1)}, u32[]{:S(2)}, u32[]{:S(2)}) collective-permute-start(bf16[8,4,64,128]{3,2,1,0:T(8,128)(2,1)S(1)} %add_convert_fusion), channel_id=1, source_target_pairs={{0,16},{1,5},{2,18},{3,7},{4,20},{5,1},{6,22},{7,3},{8,24},{9,13},... | collective-permute-start | bytes 1572872 | tf_op jit(solution)/shard_map/ppermute | solution.py:354
  48.9 0.1 add_convert_fusion.1
  49.0 1.1 %collective-permute-start.16 = (bf16[4,4,64,128]{3,2,1,0:T(8,128)(2,1)S(1)}, bf16[4,4,64,128]{3,2,1,0:T(8,128)(2,1)S(1)}, u32[]{:S(2)}, u32[]{:S(2)}) collective-permute-start(bf16[4,4,64,128]{3,2,1,0:T(8,128)(2,1)S(1)} %add_convert_fusion.1), channel_id=1, source_target_pairs={{0,24},{1,7},{2,26},{3,1},{4,28},{5,3},{6,30},{7,5},{8,0},{9,15},{... | collective-permute-start | bytes 786440 | tf_op jit(solution)/shard_map/ppermute | solution.py:357
  50.1 0.1 add_convert_fusion.2
  50.2 0.0 collective-permute-done.10.got_ref
  50.2 1.0 %collective-permute-start.15 = (bf16[4,4,64,128]{3,2,1,0:T(8,128)(2,1)S(1)}, bf16[4,4,64,128]{3,2,1,0:T(8,128)(2,1)S(1)}, u32[]{:S(2)}, u32[]{:S(2)}) collective-permute-start(bf16[4,4,64,128]{3,2,1,0:T(8,128)(2,1)S(1)} %add_convert_fusion.2), channel_id=1, source_target_pairs={{0,8},{1,3},{2,10},{3,5},{4,12},{5,7},{6,14},{7,1},{8,16},{9,11},{... | collective-permute-start | bytes 786440 | tf_op jit(solution)/shard_map/ppermute | solution.py:357
  51.2 0.0 collective-permute-done.18.down_ref
  51.2 8.6 %collective-permute-done.17.up_ref = bf16[4,4,64,128]{3,2,1,0:T(8,128)(2,1)S(1)} collective-permute-done((bf16[4,4,64,128]{3,2,1,0:T(8,128)(2,1)S(1)}, bf16[4,4,64,128]{3,2,1,0:T(8,128)(2,1)S(1)}, u32[]{:S(2)}, u32[]{:S(2)}) %collective-permute-start.17) | collective-permute-done | bytes 262176 | tf_op jit(solution)/shard_map/ppermute | solution.py:357
  59.9 0.0 collective-permute-done.12.far_ref
  59.9 0.1 collect.3
  60.0 1.3 %collective-permute-start.19 = (f32[2,4,64,128]{3,2,1,0:T(8,128)S(1)}, f32[2,4,64,128]{3,2,1,0:T(8,128)S(1)}, u32[]{:S(2)}, u32[]{:S(2)}) collective-permute-start(f32[2,4,64,128]{3,2,1,0:T(8,128)S(1)} %get-tuple-element.76), channel_id=1, source_target_pairs={{0,4},{1,17},{2,6},{3,19},{4,0},{5,21},{6,2},{7,23},{8,12},{9,25},... | collective-permute-start | bytes 786440 | tf_op jit(solution)/shard_map/ppermute | solution.py:363
  61.2 0.7 collective-permute-start.20
  61.9 0.0 collective-permute-done.16.down_ref
  61.9 4.5 %collective-permute-done.15.up_ref = bf16[4,4,64,128]{3,2,1,0:T(8,128)(2,1)S(1)} collective-permute-done((bf16[4,4,64,128]{3,2,1,0:T(8,128)(2,1)S(1)}, bf16[4,4,64,128]{3,2,1,0:T(8,128)(2,1)S(1)}, u32[]{:S(2)}, u32[]{:S(2)}) %collective-permute-start.15) | collective-permute-done | bytes 262176 | tf_op jit(solution)/shard_map/ppermute | solution.py:357
  66.5 0.1 collect.2
  66.6 0.1 collective-permute-start.21
  66.7 1.4 %collective-permute-done.19.refs_0_ = f32[2,4,64,128]{3,2,1,0:T(8,128)S(1)} collective-permute-done((f32[2,4,64,128]{3,2,1,0:T(8,128)S(1)}, f32[2,4,64,128]{3,2,1,0:T(8,128)S(1)}, u32[]{:S(2)}, u32[]{:S(2)}) %collective-permute-start.19) | collective-permute-done | bytes 262176 | tf_op jit(solution)/shard_map/ppermute | solution.py:363
  68.0 2.4 %collective-permute-done.20.refs_1_ = f32[2,4,64,128]{3,2,1,0:T(8,128)S(1)} collective-permute-done((f32[2,4,64,128]{3,2,1,0:T(8,128)S(1)}, f32[2,4,64,128]{3,2,1,0:T(8,128)S(1)}, u32[]{:S(2)}, u32[]{:S(2)}) %collective-permute-start.20) | collective-permute-done | bytes 262176 | tf_op jit(solution)/shard_map/ppermute | solution.py:363
  70.4 2.6 %collective-permute-done.21.refs_2_ = f32[2,4,64,128]{3,2,1,0:T(8,128)S(1)} collective-permute-done((f32[2,4,64,128]{3,2,1,0:T(8,128)S(1)}, f32[2,4,64,128]{3,2,1,0:T(8,128)S(1)}, u32[]{:S(2)}, u32[]{:S(2)}) %collective-permute-start.21) | collective-permute-done | bytes 262176 | tf_op jit(solution)/shard_map/ppermute | solution.py:363
  73.0 1.1 %final.1 = f32[2,2,4096]{2,1,0:T(2,128)} custom-call(f32[2,4,64,128]{3,2,1,0:T(8,128)S(1)} %get-tuple-element.75.kept_ref, f32[2,4,64,128]{3,2,1,0:T(8,128)S(1)} %collective-permute-done.19.refs_0_, f32[2,4,64,128]{3,2,1,0:T(8,128)S(1)} %collective-permute-done.20.refs_1_, f32[2,4,64,128]{3,2,1,0:T(8,128)S(1)} %collective-permute-done.21.refs_2_), custom_call_target="tpu_custom_call" | custom-call | tf_op jit(solution)/shard_map/final/pallas_call | solution.py:293
  (3 shorter events, 0.0 us)
Async XLA Ops:
  0.0 12.4 %collective-permute-start = (bf16[2,2,64,128]{3,2,1,0:T(8,128)(2,1)}, bf16[2,2,64,128]{3,2,1,0:T(8,128)(2,1)S(1)}, u32[]{:S(2)}, u32[]{:S(2)}) collective-permute-start(bf16[2,2,64,128]{3,2,1,0:T(8,128)(2,1)} %param.9), channel_id=1, source_target_pairs={{0,6},{1,25},{2,0},{3,27},{4,2},{5,29},{6,4},{7,31},{8,14},{9,1},{... | collective-permute-start | bytes 196616 | tf_op jit(solution)/shard_map/ppermute | solution.py:322
  0.5 11.8 %collective-permute-start.1 = (bf16[2,2,64,128]{3,2,1,0:T(8,128)(2,1)}, bf16[2,2,64,128]{3,2,1,0:T(8,128)(2,1)S(1)}, u32[]{:S(2)}, u32[]{:S(2)}) collective-permute-start(bf16[2,2,64,128]{3,2,1,0:T(8,128)(2,1)} %param.9), channel_id=1, source_target_pairs={{0,4},{1,17},{2,6},{3,19},{4,0},{5,21},{6,2},{7,23},{8,12},{9,25},... | collective-permute-start | bytes 196616 | tf_op jit(solution)/shard_map/ppermute | solution.py:322
  3.0 9.4 %collective-permute-start.2 = (bf16[2,2,64,128]{3,2,1,0:T(8,128)(2,1)}, bf16[2,2,64,128]{3,2,1,0:T(8,128)(2,1)S(1)}, u32[]{:S(2)}, u32[]{:S(2)}) collective-permute-start(bf16[2,2,64,128]{3,2,1,0:T(8,128)(2,1)} %param.9), channel_id=1, source_target_pairs={{0,2},{1,9},{2,4},{3,11},{4,6},{5,13},{6,0},{7,15},{8,10},{9,17},{... | collective-permute-start | bytes 196616 | tf_op jit(solution)/shard_map/ppermute | solution.py:322
  12.5 8.0 %collective-permute-start.3 = (bf16[8,2,64,128]{3,2,1,0:T(8,128)(2,1)S(1)}, bf16[8,2,64,128]{3,2,1,0:T(8,128)(2,1)S(1)}, u32[]{:S(2)}, u32[]{:S(2)}) collective-permute-start(bf16[8,2,64,128]{3,2,1,0:T(8,128)(2,1)S(1)} %constant_dynamic-update-slice_fusion.refs_0_), channel_id=1, source_target_pairs={{0,16},{1,5},{2,18},{3,7},{4,20},{5,1},{6,22},{7,3},{8,24},{9,13},... | collective-permute-start | bytes 786440 | tf_op jit(solution)/shard_map/ppermute | solution.py:330
  15.7 10.6 %collective-permute-start.5 = (bf16[8,2,64,128]{3,2,1,0:T(8,128)(2,1)S(1)}, bf16[8,2,64,128]{3,2,1,0:T(8,128)(2,1)S(1)}, u32[]{:S(2)}, u32[]{:S(2)}) collective-permute-start(bf16[8,2,64,128]{3,2,1,0:T(8,128)(2,1)S(1)} %constant_dynamic-update-slice_fusion.refs_0_), channel_id=1, source_target_pairs={{0,24},{1,7},{2,26},{3,1},{4,28},{5,3},{6,30},{7,5},{8,0},{9,15},{... | collective-permute-start | bytes 786440 | tf_op jit(solution)/shard_map/ppermute | solution.py:330
  16.8 11.4 %collective-permute-start.7 = (bf16[8,2,64,128]{3,2,1,0:T(8,128)(2,1)S(1)}, bf16[8,2,64,128]{3,2,1,0:T(8,128)(2,1)S(1)}, u32[]{:S(2)}, u32[]{:S(2)}) collective-permute-start(bf16[8,2,64,128]{3,2,1,0:T(8,128)(2,1)S(1)} %constant_dynamic-update-slice_fusion.refs_0_), channel_id=1, source_target_pairs={{0,8},{1,3},{2,10},{3,5},{4,12},{5,7},{6,14},{7,1},{8,16},{9,11},{... | collective-permute-start | bytes 786440 | tf_op jit(solution)/shard_map/ppermute | solution.py:330
  20.4 7.9 %collective-permute-start.4 = (bf16[8,2,64,128]{3,2,1,0:T(8,128)(2,1)S(1)}, bf16[8,2,64,128]{3,2,1,0:T(8,128)(2,1)S(1)}, u32[]{:S(2)}, u32[]{:S(2)}) collective-permute-start(bf16[8,2,64,128]{3,2,1,0:T(8,128)(2,1)S(1)} %collective-permute-done.3.refs_0_), channel_id=1, source_target_pairs={{0,1},{1,0},{2,3},{3,2},{4,5},{5,4},{6,7},{7,6},{8,9},{9,8},{10,11... | collective-permute-start | bytes 786440 | tf_op jit(solution)/shard_map/ppermute | solution.py:338
  26.3 4.7 %collective-permute-start.6 = (bf16[8,2,64,128]{3,2,1,0:T(8,128)(2,1)S(1)}, bf16[8,2,64,128]{3,2,1,0:T(8,128)(2,1)S(1)}, u32[]{:S(2)}, u32[]{:S(2)}) collective-permute-start(bf16[8,2,64,128]{3,2,1,0:T(8,128)(2,1)S(1)} %collective-permute-done.5.refs_0_), channel_id=1, source_target_pairs={{0,1},{1,0},{2,3},{3,2},{4,5},{5,4},{6,7},{7,6},{8,9},{9,8},{10,11... | collective-permute-start | bytes 786440 | tf_op jit(solution)/shard_map/ppermute | solution.py:338
  28.2 5.4 %collective-permute-start.8 = (bf16[8,2,64,128]{3,2,1,0:T(8,128)(2,1)S(1)}, bf16[8,2,64,128]{3,2,1,0:T(8,128)(2,1)S(1)}, u32[]{:S(2)}, u32[]{:S(2)}) collective-permute-start(bf16[8,2,64,128]{3,2,1,0:T(8,128)(2,1)S(1)} %collective-permute-done.7.refs_0_), channel_id=1, source_target_pairs={{0,1},{1,0},{2,3},{3,2},{4,5},{5,4},{6,7},{7,6},{8,9},{9,8},{10,11... | collective-permute-start | bytes 786440 | tf_op jit(solution)/shard_map/ppermute | solution.py:338
  35.0 8.0 %collective-permute-start.14 = (f32[8,4,64,128]{3,2,1,0:T(8,128)S(1)}, f32[8,4,64,128]{3,2,1,0:T(8,128)S(1)}, u32[]{:S(2)}, u32[]{:S(2)}) collective-permute-start(f32[8,4,64,128]{3,2,1,0:T(8,128)S(1)} %rotate.13), channel_id=1, source_target_pairs={{0,1},{1,0},{2,3},{3,2},{4,5},{5,4},{6,7},{7,6},{8,9},{9,8},{10,11... | collective-permute-start | bytes 3145736 | tf_op jit(solution)/shard_map/ppermute | solution.py:344
  35.6 10.7 %collective-permute-start.13 = (f32[8,4,64,128]{3,2,1,0:T(8,128)S(1)}, f32[8,4,64,128]{3,2,1,0:T(8,128)S(1)}, u32[]{:S(2)}, u32[]{:S(2)}) collective-permute-start(f32[8,4,64,128]{3,2,1,0:T(8,128)S(1)} %rotate.11), channel_id=1, source_target_pairs={{0,1},{1,0},{2,3},{3,2},{4,5},{5,4},{6,7},{7,6},{8,9},{9,8},{10,11... | collective-permute-start | bytes 3145736 | tf_op jit(solution)/shard_map/ppermute | solution.py:344
  35.7 10.8 %collective-permute-start.11 = (f32[8,4,64,128]{3,2,1,0:T(8,128)S(1)}, f32[8,4,64,128]{3,2,1,0:T(8,128)S(1)}, u32[]{:S(2)}, u32[]{:S(2)}) collective-permute-start(f32[8,4,64,128]{3,2,1,0:T(8,128)S(1)} %rotate.9), channel_id=1, source_target_pairs={{0,1},{1,0},{2,3},{3,2},{4,5},{5,4},{6,7},{7,6},{8,9},{9,8},{10,11... | collective-permute-start | bytes 3145736 | tf_op jit(solution)/shard_map/ppermute | solution.py:344
  36.1 5.2 %collective-permute-start.9 = (bf16[8,2,64,128]{3,2,1,0:T(8,128)(2,1)S(1)}, bf16[8,2,64,128]{3,2,1,0:T(8,128)(2,1)S(1)}, u32[]{:S(2)}, u32[]{:S(2)}) collective-permute-start(bf16[8,2,64,128]{3,2,1,0:T(8,128)(2,1)S(1)} %constant_dynamic-update-slice_fusion.refs_0_), channel_id=1, source_target_pairs={{0,1},{1,0},{2,3},{3,2},{4,5},{5,4},{6,7},{7,6},{8,9},{9,8},{10,11... | collective-permute-start | bytes 786440 | tf_op jit(solution)/shard_map/ppermute | solution.py:331
  42.6 7.6 %collective-permute-start.10 = (f32[8,4,64,128]{3,2,1,0:T(8,128)S(1)}, f32[8,4,64,128]{3,2,1,0:T(8,128)S(1)}, u32[]{:S(2)}, u32[]{:S(2)}) collective-permute-start(f32[8,4,64,128]{3,2,1,0:T(8,128)S(1)} %rotate.15), channel_id=1, source_target_pairs={{0,1},{1,0},{2,3},{3,2},{4,5},{5,4},{6,7},{7,6},{8,9},{9,8},{10,11... | collective-permute-start | bytes 3145736 | tf_op jit(solution)/shard_map/ppermute | solution.py:344
  43.1 8.1 %collective-permute-start.18 = (bf16[4,4,64,128]{3,2,1,0:T(8,128)(2,1)S(1)}, bf16[4,4,64,128]{3,2,1,0:T(8,128)(2,1)S(1)}, u32[]{:S(2)}, u32[]{:S(2)}) collective-permute-start(bf16[4,4,64,128]{3,2,1,0:T(8,128)(2,1)S(1)} %fusion), channel_id=1, source_target_pairs={{0,24},{1,7},{2,26},{3,1},{4,28},{5,3},{6,30},{7,5},{8,0},{9,15},{... | collective-permute-start | bytes 786440 | tf_op jit(solution)/shard_map/ppermute | solution.py:357
  46.4 13.5 %collective-permute-start.17 = (bf16[4,4,64,128]{3,2,1,0:T(8,128)(2,1)S(1)}, bf16[4,4,64,128]{3,2,1,0:T(8,128)(2,1)S(1)}, u32[]{:S(2)}, u32[]{:S(2)}) collective-permute-start(bf16[4,4,64,128]{3,2,1,0:T(8,128)(2,1)S(1)} %fusion.1), channel_id=1, source_target_pairs={{0,8},{1,3},{2,10},{3,5},{4,12},{5,7},{6,14},{7,1},{8,16},{9,11},{... | collective-permute-start | bytes 786440 | tf_op jit(solution)/shard_map/ppermute | solution.py:357
  46.6 13.2 %collective-permute-start.12 = (bf16[8,4,64,128]{3,2,1,0:T(8,128)(2,1)S(1)}, bf16[8,4,64,128]{3,2,1,0:T(8,128)(2,1)S(1)}, u32[]{:S(2)}, u32[]{:S(2)}) collective-permute-start(bf16[8,4,64,128]{3,2,1,0:T(8,128)(2,1)S(1)} %add_convert_fusion), channel_id=1, source_target_pairs={{0,16},{1,5},{2,18},{3,7},{4,20},{5,1},{6,22},{7,3},{8,24},{9,13},... | collective-permute-start | bytes 1572872 | tf_op jit(solution)/shard_map/ppermute | solution.py:354
  49.0 12.9 %collective-permute-start.16 = (bf16[4,4,64,128]{3,2,1,0:T(8,128)(2,1)S(1)}, bf16[4,4,64,128]{3,2,1,0:T(8,128)(2,1)S(1)}, u32[]{:S(2)}, u32[]{:S(2)}) collective-permute-start(bf16[4,4,64,128]{3,2,1,0:T(8,128)(2,1)S(1)} %add_convert_fusion.1), channel_id=1, source_target_pairs={{0,24},{1,7},{2,26},{3,1},{4,28},{5,3},{6,30},{7,5},{8,0},{9,15},{... | collective-permute-start | bytes 786440 | tf_op jit(solution)/shard_map/ppermute | solution.py:357
  50.2 16.3 %collective-permute-start.15 = (bf16[4,4,64,128]{3,2,1,0:T(8,128)(2,1)S(1)}, bf16[4,4,64,128]{3,2,1,0:T(8,128)(2,1)S(1)}, u32[]{:S(2)}, u32[]{:S(2)}) collective-permute-start(bf16[4,4,64,128]{3,2,1,0:T(8,128)(2,1)S(1)} %add_convert_fusion.2), channel_id=1, source_target_pairs={{0,8},{1,3},{2,10},{3,5},{4,12},{5,7},{6,14},{7,1},{8,16},{9,11},{... | collective-permute-start | bytes 786440 | tf_op jit(solution)/shard_map/ppermute | solution.py:357
  60.0 8.1 %collective-permute-start.19 = (f32[2,4,64,128]{3,2,1,0:T(8,128)S(1)}, f32[2,4,64,128]{3,2,1,0:T(8,128)S(1)}, u32[]{:S(2)}, u32[]{:S(2)}) collective-permute-start(f32[2,4,64,128]{3,2,1,0:T(8,128)S(1)} %get-tuple-element.76), channel_id=1, source_target_pairs={{0,4},{1,17},{2,6},{3,19},{4,0},{5,21},{6,2},{7,23},{8,12},{9,25},... | collective-permute-start | bytes 786440 | tf_op jit(solution)/shard_map/ppermute | solution.py:363
  61.2 9.2 %collective-permute-start.20 = (f32[2,4,64,128]{3,2,1,0:T(8,128)S(1)}, f32[2,4,64,128]{3,2,1,0:T(8,128)S(1)}, u32[]{:S(2)}, u32[]{:S(2)}) collective-permute-start(f32[2,4,64,128]{3,2,1,0:T(8,128)S(1)} %get-tuple-element.77), channel_id=1, source_target_pairs={{0,6},{1,25},{2,0},{3,27},{4,2},{5,29},{6,4},{7,31},{8,14},{9,1},{... | collective-permute-start | bytes 786440 | tf_op jit(solution)/shard_map/ppermute | solution.py:363
  66.6 6.4 %collective-permute-start.21 = (f32[2,4,64,128]{3,2,1,0:T(8,128)S(1)}, f32[2,4,64,128]{3,2,1,0:T(8,128)S(1)}, u32[]{:S(2)}, u32[]{:S(2)}) collective-permute-start(f32[2,4,64,128]{3,2,1,0:T(8,128)S(1)} %get-tuple-element.78), channel_id=1, source_target_pairs={{0,2},{1,9},{2,4},{3,11},{4,6},{5,13},{6,0},{7,15},{8,10},{9,17},{... | collective-permute-start | bytes 786440 | tf_op jit(solution)/shard_map/ppermute | solution.py:363

commit v3 on v1

--- a/solution.py
+++ b/solution.py
@@ -21,6 +21,7 @@
 ROTATE_VMEM = 12 << 20
 IN_STEP = 20
 OUT_STEP = 260
+LAG = 2
 
 
 def owner_place(k, y, x, core):
@@ -174,43 +175,49 @@
 
 def rotate_body(shifts, half, *refs):
     v_refs, f_refs, b_ref = refs[: len(shifts)], refs[-3:-1], refs[-1]
+    waiting = []
+
+    def left_product(group, shift, j):
+        k = half * 32 + shift * 8 + j
+        v_re, v_im = v_refs[group][j, 0], v_refs[group][j, 1]
+        left = jnp.concatenate(
+            [jnp.concatenate([v_re, v_im], axis=1), jnp.concatenate([-v_im, v_re], axis=1)], axis=0
+        )
+        found = []
+        for o in range(2):
+            parts = [
+                f_refs[o][pl.ds(64 * line + k, 128, stride=OUT_STEP), :].astype(jnp.bfloat16) for line in range(4)
+            ]
+            right = jnp.concatenate([jnp.concatenate(parts[2 * p : 2 * p + 2], axis=0) for p in range(2)], axis=1)
+            found.append(jnp.dot(left, right, preferred_element_type=jnp.float32))
+        waiting.append((group, j, v_re, v_im, found))
+
+    def right_product():
+        group, j, v_re, v_im, found = waiting.pop(0)
+        lines = []
+        for o in range(2):
+            for p in range(2):
+                tile = found[o][:, 128 * p : 128 * p + 128]
+                lines.append(jnp.concatenate([tile[:64], tile[64:]], axis=1))
+        high, low = halves_of(jnp.concatenate(lines, axis=0))
+        right = jnp.concatenate(
+            [jnp.concatenate([v_re, -v_im], axis=1), jnp.concatenate([v_im, v_re], axis=1)], axis=0
+        )
+        out = lax.dot_general(
+            jnp.concatenate([high, low], axis=0),
+            right,
+            (((1,), (1,)), ((), ())),
+            preferred_element_type=jnp.float32,
+        )
+        b_ref[8 * group + j] = (out[:256] + out[256:]).reshape(4, 64, 128)
+
     for group, shift in enumerate(shifts):
-        pairs, mids = [], []
         for j in range(8):
-            k = half * 32 + shift * 8 + j
-            v_re, v_im = v_refs[group][j, 0], v_refs[group][j, 1]
-            pairs.append((v_re, v_im))
-            left = jnp.concatenate(
-                [jnp.concatenate([v_re, v_im], axis=1), jnp.concatenate([-v_im, v_re], axis=1)], axis=0
-            )
-            found = []
-            for o in range(2):
-                parts = [
-                    f_refs[o][pl.ds(64 * line + k, 128, stride=OUT_STEP), :].astype(jnp.bfloat16) for line in range(4)
-                ]
-                right = jnp.concatenate(
-                    [jnp.concatenate(parts[2 * p : 2 * p + 2], axis=0) for p in range(2)], axis=1
-                )
-                found.append(jnp.dot(left, right, preferred_element_type=jnp.float32))
-            mids.append(found)
-        for j in range(8):
-            v_re, v_im = pairs[j]
-            lines = []
-            for o in range(2):
-                for p in range(2):
-                    tile = mids[j][o][:, 128 * p : 128 * p + 128]
-                    lines.append(jnp.concatenate([tile[:64], tile[64:]], axis=1))
-            high, low = halves_of(jnp.concatenate(lines, axis=0))
-            right = jnp.concatenate(
-                [jnp.concatenate([v_re, -v_im], axis=1), jnp.concatenate([v_im, v_re], axis=1)], axis=0
-            )
-            out = lax.dot_general(
-                jnp.concatenate([high, low], axis=0),
-                right,
-                (((1,), (1,)), ((), ())),
-                preferred_element_type=jnp.float32,
-            )
-            b_ref[8 * group + j] = (out[:256] + out[256:]).reshape(4, 64, 128)
+            left_product(group, shift, j)
+            if len(waiting) > LAG:
+                right_product()
+    while waiting:
+        right_product()
 
 
 def rotate(vectors, sums, half, shifts):
@@ -232,6 +239,26 @@
     return high, (value - high.astype(jnp.float32)).astype(jnp.bfloat16)
 
 
+def collect_body(own_ref, got_ref, far_ref, up_ref, down_ref, *out_refs):
+    for place, out_ref in enumerate(out_refs):
+        for slot in range(2):
+            at = 2 * place + slot
+            value = own_ref[at] + got_ref[at] + far_ref[at].astype(jnp.float32)
+            out_ref[slot] = value + up_ref[at].astype(jnp.float32) + down_ref[at].astype(jnp.float32)
+
+
+def collect(own, got, came):
+    whole = pl.BlockSpec(memory_space=pltpu.VMEM)
+    return pl.pallas_call(
+        collect_body,
+        in_specs=[whole] * 5,
+        out_specs=[whole] * SIDE,
+        out_shape=[jax.ShapeDtypeStruct((2, 4, 64, 128), jnp.float32)] * SIDE,
+        compiler_params=pltpu.CompilerParams(vmem_limit_bytes=8 << 20),
+        name="collect",
+    )(own, got, *came)
+
+
 def final_body(kept_ref, *refs):
     came, o_ref, hold_ref = refs[:-2], refs[-2], refs[-1]
     factor = 1.0 / math.sqrt(64)
@@ -294,7 +321,6 @@
 
 def on_device(wannier_ops, r_coords, degeneracy, kpoints, bloch_vectors):
     me = lax.axis_index(WHOLE).astype(jnp.int32).reshape(1)
-    slots = bloch_vectors.shape[0]
     swap = [(0, 1), (1, 0)]
 
     near = []
@@ -312,27 +338,20 @@
     second = fourier(1, phases, ops)
     sums = [first, second]
 
-    parts, came, got, own = {}, {}, {}, {}
-    for whose, shift in ((0, 0), (1, 0), (0, 2), (1, 2), (1, 1), (1, 3), (0, 1), (0, 3)):
+    got, own, came = {}, {}, {}
+    for whose, shift in ((0, 2), (1, 2), (0, 1), (1, 1), (1, 3), (0, 3), (0, 0), (1, 0)):
+        if shift and shift not in theirs:
+            theirs[shift] = lax.ppermute(mine[shift], "c", swap)
         made = rotate((mine, theirs)[whose], sums, whose, (shift,))
         sums, made = lax.optimization_barrier((sums, made))
         if not whose:
             own[shift] = made
-        else:
-            got[shift] = lax.ppermute(made, "c", swap)
-        if (whose, shift) == (1, 0):
-            sums, mine = lax.optimization_barrier((sums, mine))
-            for other in (2, 1, 3):
-                theirs[other] = lax.ppermute(mine[other], "c", swap)
-    for shift in (2, 1, 3, 0):
-        parts[shift] = own[shift] + got[shift]
-        if shift:
-            came[shift] = lax.ppermute(parts[shift].astype(LINK), WHOLE, shift_pairs(0, shift))
-    total = parts[0]
+            continue
+        got[shift] = lax.ppermute(made, "c", swap)
     for shift in (2, 1, 3):
-        total = total + came[shift].astype(jnp.float32)
-    parts = total.reshape(SIDE, slots, 4, 64, 128)
-    return final(parts[0], [lax.ppermute(parts[s], WHOLE, shift_pairs(1, s)) for s in (2, 1, 3)])
+        came[shift] = lax.ppermute((own[shift] + got[shift]).astype(LINK), WHOLE, shift_pairs(0, shift))
+    total = collect(own[0], got[0], [came[shift] for shift in (2, 1, 3)])
+    return final(total[0], [lax.ppermute(total[shift], WHOLE, shift_pairs(1, shift)) for shift in (2, 1, 3)])
 
 
 def solution(mesh):

time: 66.5 us -> 75.6 us (1.14)
  the two profiles are of different devices: /device:TPU:98 before, /device:TPU:66 now
where the time goes in v3:
time: 75.6 us; the launch traced here: 75.5 us
  waiting for transfers between devices  31.3 us (41%)
  Pallas kernels  22.4 us (30%)
  starting transfers between devices  20.1 us (27%)
  local copies, waits for them, and re-layouts  0.89 us (1%)
    ppermute x3, waiting for transfers between devices, on_device(): lax.ppermute((own[shift] + got[shift]).astype(LINK), WHOLE, shift_pairs(0...  17.2 us
    ppermute x3, waiting for transfers between devices, on_device(): lax.ppermute(total[shift], WHOLE, shift_pairs(1, shift))  8.57 us
    pallas_call x8, Pallas kernels, rotate(): pl.pallas_call(functools.partial(rotate_body, shifts, half), in_specs=[wh...  8.45 us
    pallas_call x1, Pallas kernels, fourier(): pl.pallas_call(functools.partial(fourier_first, rows), grid_spec=pltpu.Pr...  6.77 us
    pallas_call x1, Pallas kernels, fourier(): pl.pallas_call(functools.partial(fourier_second, rows), grid=(width // ro...  5.88 us
    ppermute x3, starting transfers between devices, on_device(): lax.ppermute((own[shift] + got[shift]).astype(LINK), WHOLE, shift_pairs(0...  5.52 us
    ppermute x3, starting transfers between devices, on_device(): mine[shift] = lax.ppermute(near, WHOLE, shift_pairs(0, -shift))  5.3 us
    ppermute x3, starting transfers between devices, on_device(): near.append(lax.ppermute(bloch_vectors, WHOLE, shift_pairs(1, -shift)))  4.76 us
  transfers between devices with their start and end apart: 20, of which 6 were waited for; matrix products, arithmetic and copies ran while one was open for 2% of the time, Pallas kernels for 27%

profile of v3, /device:TPU:66, one launch (start us, length us, event | category | flops | bytes accessed | tf_op | source)
XLA Modules:
  0.0 75.5 jit_solution(8606390502876272517)
XLA Ops:
  0.0 0.5 collective-permute-start
  0.5 2.4 %collective-permute-start.1 = (bf16[2,2,64,128]{3,2,1,0:T(8,128)(2,1)}, bf16[2,2,64,128]{3,2,1,0:T(8,128)(2,1)S(1)}, u32[]{:S(2)}, u32[]{:S(2)}) collective-permute-start(bf16[2,2,64,128]{3,2,1,0:T(8,128)(2,1)} %param.9), channel_id=1, source_target_pairs={{0,4},{1,17},{2,6},{3,19},{4,0},{5,21},{6,2},{7,23},{8,12},{9,25},... | collective-permute-start | bytes 196616 | tf_op jit(solution)/shard_map/ppermute | solution.py:328
  3.0 1.8 %collective-permute-start.2 = (bf16[2,2,64,128]{3,2,1,0:T(8,128)(2,1)}, bf16[2,2,64,128]{3,2,1,0:T(8,128)(2,1)S(1)}, u32[]{:S(2)}, u32[]{:S(2)}) collective-permute-start(bf16[2,2,64,128]{3,2,1,0:T(8,128)(2,1)} %param.9), channel_id=1, source_target_pairs={{0,2},{1,9},{2,4},{3,11},{4,6},{5,13},{6,0},{7,15},{8,10},{9,17},{... | collective-permute-start | bytes 196616 | tf_op jit(solution)/shard_map/ppermute | solution.py:328
  4.8 6.8 %fourier_first.1 = (f32[33280,128]{1,0:T(8,128)S(1)}, bf16[256,256]{1,0:T(8,128)(2,1)S(1)}) custom-call(s32[1]{0:T(128)} %bitcast.me_ref, s32[3,125]{1,0:T(4,128)} %bitcast.5, s32[1,125]{1,0:T(1,128)} %bitcast.6, s32[3,256]{1,0:T(4,128)} %bitcast.4, bf16[2,125,2,128,128]{4,3,2,1,0:T(8,128)(2,1)} %o_ref.3), custom_call_target="tpu_custom_call" | custom-call | flops 4000000000 | bytes 16000000 | tf_op jit(solution)/shard_map/fourier_first/pallas_call | solution.py:149
  11.5 0.8 %constant_dynamic-update-slice_fusion.3 = bf16[8,2,64,128]{3,2,1,0:T(8,128)(2,1)S(1)} fusion(bf16[2,2,64,128]{3,2,1,0:T(8,128)(2,1)} %param.9), kind=kLoop, calls=%fused_computation.6 | loop fusion | bytes 131072
  12.4 0.0 collective-permute-done
  12.4 0.0 collective-permute-done.1
  12.4 0.0 collective-permute-done.2
  12.5 3.3 %collective-permute-start.3 = (bf16[8,2,64,128]{3,2,1,0:T(8,128)(2,1)S(1)}, bf16[8,2,64,128]{3,2,1,0:T(8,128)(2,1)S(1)}, u32[]{:S(2)}, u32[]{:S(2)}) collective-permute-start(bf16[8,2,64,128]{3,2,1,0:T(8,128)(2,1)S(1)} %constant_dynamic-update-slice_fusion.refs_0_), channel_id=1, source_target_pairs={{0,16},{1,5},{2,18},{3,7},{4,20},{5,1},{6,22},{7,3},{8,24},{9,13},... | collective-permute-start | bytes 786440 | tf_op jit(solution)/shard_map/ppermute | solution.py:336
  15.7 1.1 %collective-permute-start.5 = (bf16[8,2,64,128]{3,2,1,0:T(8,128)(2,1)S(1)}, bf16[8,2,64,128]{3,2,1,0:T(8,128)(2,1)S(1)}, u32[]{:S(2)}, u32[]{:S(2)}) collective-permute-start(bf16[8,2,64,128]{3,2,1,0:T(8,128)(2,1)S(1)} %constant_dynamic-update-slice_fusion.refs_0_), channel_id=1, source_target_pairs={{0,24},{1,7},{2,26},{3,1},{4,28},{5,3},{6,30},{7,5},{8,0},{9,15},{... | collective-permute-start | bytes 786440 | tf_op jit(solution)/shard_map/ppermute | solution.py:336
  16.8 1.0 %collective-permute-start.7 = (bf16[8,2,64,128]{3,2,1,0:T(8,128)(2,1)S(1)}, bf16[8,2,64,128]{3,2,1,0:T(8,128)(2,1)S(1)}, u32[]{:S(2)}, u32[]{:S(2)}) collective-permute-start(bf16[8,2,64,128]{3,2,1,0:T(8,128)(2,1)S(1)} %constant_dynamic-update-slice_fusion.refs_0_), channel_id=1, source_target_pairs={{0,8},{1,3},{2,10},{3,5},{4,12},{5,7},{6,14},{7,1},{8,16},{9,11},{... | collective-permute-start | bytes 786440 | tf_op jit(solution)/shard_map/ppermute | solution.py:336
  17.8 2.7 %collective-permute-done.3.refs_0_ = bf16[8,2,64,128]{3,2,1,0:T(8,128)(2,1)S(1)} collective-permute-done((bf16[8,2,64,128]{3,2,1,0:T(8,128)(2,1)S(1)}, bf16[8,2,64,128]{3,2,1,0:T(8,128)(2,1)S(1)}, u32[]{:S(2)}, u32[]{:S(2)}) %collective-permute-start.3) | collective-permute-done | bytes 262176 | tf_op jit(solution)/shard_map/ppermute | solution.py:336
  20.4 0.0 collective-permute-start.4
  20.4 5.9 %fourier_second.1.refs_2_ = f32[33280,128]{1,0:T(8,128)S(1)} custom-call(bf16[256,256]{1,0:T(8,128)(2,1)S(1)} %get-tuple-element.41.l_ref, bf16[2,125,2,128,128]{4,3,2,1,0:T(8,128)(2,1)} %o_ref.3), custom_call_target="tpu_custom_call" | custom-call | flops 4000000000 | bytes 16000000 | tf_op jit(solution)/shard_map/fourier_second/pallas_call | solution.py:163
  26.3 0.0 collective-permute-done.5.refs_0_
  26.3 0.6 collective-permute-start.6
  26.9 1.1 %rotate.8 = f32[8,4,64,128]{3,2,1,0:T(8,128)S(1)} custom-call(bf16[8,2,64,128]{3,2,1,0:T(8,128)(2,1)S(1)} %collective-permute-done.3.refs_0_, f32[33280,128]{1,0:T(8,128)S(1)} %get-tuple-element.58.refs_1_, f32[33280,128]{1,0:T(8,128)S(1)} %fourier_second.1.refs_2_), custom_call_target="tpu_custom_call" | custom-call | flops 960000000 | bytes 3200000 | tf_op jit(solution)/shard_map/rotate/pallas_call | solution.py:226
  28.0 0.0 collective-permute-done.7.refs_0_
  28.0 0.1 collective-permute-start.8
  28.1 0.0 collective-permute-done.4.refs_0_
  28.1 1.1 %rotate.9 = f32[8,4,64,128]{3,2,1,0:T(8,128)S(1)} custom-call(bf16[8,2,64,128]{3,2,1,0:T(8,128)(2,1)S(1)} %collective-permute-done.4.refs_0_, f32[33280,128]{1,0:T(8,128)S(1)} %get-tuple-element.58.refs_1_, f32[33280,128]{1,0:T(8,128)S(1)} %fourier_second.1.refs_2_), custom_call_target="tpu_custom_call" | custom-call | flops 960000000 | bytes 3200000 | tf_op jit(solution)/shard_map/rotate/pallas_call | solution.py:226
  29.1 1.1 %rotate.10 = f32[8,4,64,128]{3,2,1,0:T(8,128)S(1)} custom-call(bf16[8,2,64,128]{3,2,1,0:T(8,128)(2,1)S(1)} %collective-permute-done.5.refs_0_, f32[33280,128]{1,0:T(8,128)S(1)} %get-tuple-element.58.refs_1_, f32[33280,128]{1,0:T(8,128)S(1)} %fourier_second.1.refs_2_), custom_call_target="tpu_custom_call" | custom-call | flops 960000000 | bytes 3200000 | tf_op jit(solution)/shard_map/rotate/pallas_call | solution.py:226
  30.2 0.0 collective-permute-done.6.refs_0_
  30.2 1.1 %rotate.11 = f32[8,4,64,128]{3,2,1,0:T(8,128)S(1)} custom-call(bf16[8,2,64,128]{3,2,1,0:T(8,128)(2,1)S(1)} %collective-permute-done.6.refs_0_, f32[33280,128]{1,0:T(8,128)S(1)} %get-tuple-element.58.refs_1_, f32[33280,128]{1,0:T(8,128)S(1)} %fourier_second.1.refs_2_), custom_call_target="tpu_custom_call" | custom-call | flops 960000000 | bytes 3200000 | tf_op jit(solution)/shard_map/rotate/pallas_call | solution.py:226
  31.3 0.0 collective-permute-done.8.refs_0_
  31.3 1.1 %rotate.12 = f32[8,4,64,128]{3,2,1,0:T(8,128)S(1)} custom-call(bf16[8,2,64,128]{3,2,1,0:T(8,128)(2,1)S(1)} %collective-permute-done.8.refs_0_, f32[33280,128]{1,0:T(8,128)S(1)} %get-tuple-element.58.refs_1_, f32[33280,128]{1,0:T(8,128)S(1)} %fourier_second.1.refs_2_), custom_call_target="tpu_custom_call" | custom-call | flops 960000000 | bytes 3200000 | tf_op jit(solution)/shard_map/rotate/pallas_call | solution.py:226
  32.4 0.6 collective-permute-start.15
  32.9 0.1 collective-permute-start.13
  33.0 0.4 collective-permute-start.11
  33.4 0.1 collective-permute-start.9
  33.5 1.1 %rotate.13 = f32[8,4,64,128]{3,2,1,0:T(8,128)S(1)} custom-call(bf16[8,2,64,128]{3,2,1,0:T(8,128)(2,1)S(1)} %collective-permute-done.7.refs_0_, f32[33280,128]{1,0:T(8,128)S(1)} %get-tuple-element.58.refs_1_, f32[33280,128]{1,0:T(8,128)S(1)} %fourier_second.1.refs_2_), custom_call_target="tpu_custom_call" | custom-call | flops 960000000 | bytes 3200000 | tf_op jit(solution)/shard_map/rotate/pallas_call | solution.py:226
  34.6 1.1 %rotate.14.own_ref = f32[8,4,64,128]{3,2,1,0:T(8,128)S(1)} custom-call(bf16[8,2,64,128]{3,2,1,0:T(8,128)(2,1)S(1)} %constant_dynamic-update-slice_fusion.refs_0_, f32[33280,128]{1,0:T(8,128)S(1)} %get-tuple-element.58.refs_1_, f32[33280,128]{1,0:T(8,128)S(1)} %fourier_second.1.refs_2_), custom_call_target="tpu_custom_call" | custom-call | flops 960000000 | bytes 3200000 | tf_op jit(solution)/shard_map/rotate/pallas_call | solution.py:226
  35.7 2.9 %collective-permute-done.9.refs_0_ = bf16[8,2,64,128]{3,2,1,0:T(8,128)(2,1)S(1)} collective-permute-done((bf16[8,2,64,128]{3,2,1,0:T(8,128)(2,1)S(1)}, bf16[8,2,64,128]{3,2,1,0:T(8,128)(2,1)S(1)}, u32[]{:S(2)}, u32[]{:S(2)}) %collective-permute-start.9) | collective-permute-done | bytes 262176 | tf_op jit(solution)/shard_map/ppermute | solution.py:337
  38.6 1.1 %rotate.15 = f32[8,4,64,128]{3,2,1,0:T(8,128)S(1)} custom-call(bf16[8,2,64,128]{3,2,1,0:T(8,128)(2,1)S(1)} %collective-permute-done.9.refs_0_, f32[33280,128]{1,0:T(8,128)S(1)} %get-tuple-element.58.refs_1_, f32[33280,128]{1,0:T(8,128)S(1)} %fourier_second.1.refs_2_), custom_call_target="tpu_custom_call" | custom-call | flops 960000000 | bytes 3200000 | tf_op jit(solution)/shard_map/rotate/pallas_call | solution.py:226
  39.7 0.5 collective-permute-start.10
  40.1 0.0 collective-permute-done.15
  40.1 0.2 add_convert_fusion
  40.3 3.2 %collective-permute-start.16 = (bf16[8,4,64,128]{3,2,1,0:T(8,128)(2,1)S(1)}, bf16[8,4,64,128]{3,2,1,0:T(8,128)(2,1)S(1)}, u32[]{:S(2)}, u32[]{:S(2)}) collective-permute-start(bf16[8,4,64,128]{3,2,1,0:T(8,128)(2,1)S(1)} %add_convert_fusion), channel_id=1, source_target_pairs={{0,24},{1,7},{2,26},{3,1},{4,28},{5,3},{6,30},{7,5},{8,0},{9,15},{... | collective-permute-start | bytes 1572872 | tf_op jit(solution)/shard_map/ppermute | solution.py:352
  43.5 0.0 collective-permute-done.13
  43.5 0.2 add_convert_fusion.1
  43.7 0.1 collective-permute-start.14
  43.7 0.0 collective-permute-done.11
  43.8 0.2 add_convert_fusion.2
  43.9 2.3 %collective-permute-start.12 = (bf16[8,4,64,128]{3,2,1,0:T(8,128)(2,1)S(1)}, bf16[8,4,64,128]{3,2,1,0:T(8,128)(2,1)S(1)}, u32[]{:S(2)}, u32[]{:S(2)}) collective-permute-start(bf16[8,4,64,128]{3,2,1,0:T(8,128)(2,1)S(1)} %add_convert_fusion.2), channel_id=1, source_target_pairs={{0,16},{1,5},{2,18},{3,7},{4,20},{5,1},{6,22},{7,3},{8,24},{9,13},... | collective-permute-start | bytes 1572872 | tf_op jit(solution)/shard_map/ppermute | solution.py:352
  46.2 0.0 collective-permute-done.10.got_ref
  46.2 9.6 %collective-permute-done.16.down_ref = bf16[8,4,64,128]{3,2,1,0:T(8,128)(2,1)S(1)} collective-permute-done((bf16[8,4,64,128]{3,2,1,0:T(8,128)(2,1)S(1)}, bf16[8,4,64,128]{3,2,1,0:T(8,128)(2,1)S(1)}, u32[]{:S(2)}, u32[]{:S(2)}) %collective-permute-start.16) | collective-permute-done | bytes 524320 | tf_op jit(solution)/shard_map/ppermute | solution.py:352
  55.8 7.6 %collective-permute-done.14.up_ref = bf16[8,4,64,128]{3,2,1,0:T(8,128)(2,1)S(1)} collective-permute-done((bf16[8,4,64,128]{3,2,1,0:T(8,128)(2,1)S(1)}, bf16[8,4,64,128]{3,2,1,0:T(8,128)(2,1)S(1)}, u32[]{:S(2)}, u32[]{:S(2)}) %collective-permute-start.14) | collective-permute-done | bytes 524320 | tf_op jit(solution)/shard_map/ppermute | solution.py:352
  63.4 0.0 collective-permute-done.12.far_ref
  63.4 0.2 collect.1
  63.6 0.1 collective-permute-start.17
  63.7 0.1 collective-permute-start.18
  63.8 2.0 %collective-permute-start.19 = (f32[2,4,64,128]{3,2,1,0:T(8,128)S(1)}, f32[2,4,64,128]{3,2,1,0:T(8,128)S(1)}, u32[]{:S(2)}, u32[]{:S(2)}) collective-permute-start(f32[2,4,64,128]{3,2,1,0:T(8,128)S(1)} %get-tuple-element.70), channel_id=1, source_target_pairs={{0,6},{1,25},{2,0},{3,27},{4,2},{5,29},{6,4},{7,31},{8,14},{9,1},{... | collective-permute-start | bytes 786440 | tf_op jit(solution)/shard_map/ppermute | solution.py:354
  65.8 5.9 %collective-permute-done.17.refs_0_ = f32[2,4,64,128]{3,2,1,0:T(8,128)S(1)} collective-permute-done((f32[2,4,64,128]{3,2,1,0:T(8,128)S(1)}, f32[2,4,64,128]{3,2,1,0:T(8,128)S(1)}, u32[]{:S(2)}, u32[]{:S(2)}) %collective-permute-start.17) | collective-permute-done | bytes 262176 | tf_op jit(solution)/shard_map/ppermute | solution.py:354
  71.7 0.0 collective-permute-done.18.refs_1_
  71.7 2.7 %collective-permute-done.19.refs_2_ = f32[2,4,64,128]{3,2,1,0:T(8,128)S(1)} collective-permute-done((f32[2,4,64,128]{3,2,1,0:T(8,128)S(1)}, f32[2,4,64,128]{3,2,1,0:T(8,128)S(1)}, u32[]{:S(2)}, u32[]{:S(2)}) %collective-permute-start.19) | collective-permute-done | bytes 262176 | tf_op jit(solution)/shard_map/ppermute | solution.py:354
  74.4 1.1 %final.1 = f32[2,2,4096]{2,1,0:T(2,128)} custom-call(f32[2,4,64,128]{3,2,1,0:T(8,128)S(1)} %get-tuple-element.67.kept_ref, f32[2,4,64,128]{3,2,1,0:T(8,128)S(1)} %collective-permute-done.17.refs_0_, f32[2,4,64,128]{3,2,1,0:T(8,128)S(1)} %collective-permute-done.18.refs_1_, f32[2,4,64,128]{3,2,1,0:T(8,128)S(1)} %collective-permute-done.19.refs_2_), custom_call_target="tpu_custom_call" | custom-call | tf_op jit(solution)/shard_map/final/pallas_call | solution.py:299
  (3 shorter events, 0.0 us)
Async XLA Ops:
  0.0 12.4 %collective-permute-start = (bf16[2,2,64,128]{3,2,1,0:T(8,128)(2,1)}, bf16[2,2,64,128]{3,2,1,0:T(8,128)(2,1)S(1)}, u32[]{:S(2)}, u32[]{:S(2)}) collective-permute-start(bf16[2,2,64,128]{3,2,1,0:T(8,128)(2,1)} %param.9), channel_id=1, source_target_pairs={{0,6},{1,25},{2,0},{3,27},{4,2},{5,29},{6,4},{7,31},{8,14},{9,1},{... | collective-permute-start | bytes 196616 | tf_op jit(solution)/shard_map/ppermute | solution.py:328
  0.5 11.8 %collective-permute-start.1 = (bf16[2,2,64,128]{3,2,1,0:T(8,128)(2,1)}, bf16[2,2,64,128]{3,2,1,0:T(8,128)(2,1)S(1)}, u32[]{:S(2)}, u32[]{:S(2)}) collective-permute-start(bf16[2,2,64,128]{3,2,1,0:T(8,128)(2,1)} %param.9), channel_id=1, source_target_pairs={{0,4},{1,17},{2,6},{3,19},{4,0},{5,21},{6,2},{7,23},{8,12},{9,25},... | collective-permute-start | bytes 196616 | tf_op jit(solution)/shard_map/ppermute | solution.py:328
  3.0 9.4 %collective-permute-start.2 = (bf16[2,2,64,128]{3,2,1,0:T(8,128)(2,1)}, bf16[2,2,64,128]{3,2,1,0:T(8,128)(2,1)S(1)}, u32[]{:S(2)}, u32[]{:S(2)}) collective-permute-start(bf16[2,2,64,128]{3,2,1,0:T(8,128)(2,1)} %param.9), channel_id=1, source_target_pairs={{0,2},{1,9},{2,4},{3,11},{4,6},{5,13},{6,0},{7,15},{8,10},{9,17},{... | collective-permute-start | bytes 196616 | tf_op jit(solution)/shard_map/ppermute | solution.py:328
  12.5 8.0 %collective-permute-start.3 = (bf16[8,2,64,128]{3,2,1,0:T(8,128)(2,1)S(1)}, bf16[8,2,64,128]{3,2,1,0:T(8,128)(2,1)S(1)}, u32[]{:S(2)}, u32[]{:S(2)}) collective-permute-start(bf16[8,2,64,128]{3,2,1,0:T(8,128)(2,1)S(1)} %constant_dynamic-update-slice_fusion.refs_0_), channel_id=1, source_target_pairs={{0,16},{1,5},{2,18},{3,7},{4,20},{5,1},{6,22},{7,3},{8,24},{9,13},... | collective-permute-start | bytes 786440 | tf_op jit(solution)/shard_map/ppermute | solution.py:336
  15.7 10.6 %collective-permute-start.5 = (bf16[8,2,64,128]{3,2,1,0:T(8,128)(2,1)S(1)}, bf16[8,2,64,128]{3,2,1,0:T(8,128)(2,1)S(1)}, u32[]{:S(2)}, u32[]{:S(2)}) collective-permute-start(bf16[8,2,64,128]{3,2,1,0:T(8,128)(2,1)S(1)} %constant_dynamic-update-slice_fusion.refs_0_), channel_id=1, source_target_pairs={{0,24},{1,7},{2,26},{3,1},{4,28},{5,3},{6,30},{7,5},{8,0},{9,15},{... | collective-permute-start | bytes 786440 | tf_op jit(solution)/shard_map/ppermute | solution.py:336
  16.8 11.2 %collective-permute-start.7 = (bf16[8,2,64,128]{3,2,1,0:T(8,128)(2,1)S(1)}, bf16[8,2,64,128]{3,2,1,0:T(8,128)(2,1)S(1)}, u32[]{:S(2)}, u32[]{:S(2)}) collective-permute-start(bf16[8,2,64,128]{3,2,1,0:T(8,128)(2,1)S(1)} %constant_dynamic-update-slice_fusion.refs_0_), channel_id=1, source_target_pairs={{0,8},{1,3},{2,10},{3,5},{4,12},{5,7},{6,14},{7,1},{8,16},{9,11},{... | collective-permute-start | bytes 786440 | tf_op jit(solution)/shard_map/ppermute | solution.py:336
  20.4 7.7 %collective-permute-start.4 = (bf16[8,2,64,128]{3,2,1,0:T(8,128)(2,1)S(1)}, bf16[8,2,64,128]{3,2,1,0:T(8,128)(2,1)S(1)}, u32[]{:S(2)}, u32[]{:S(2)}) collective-permute-start(bf16[8,2,64,128]{3,2,1,0:T(8,128)(2,1)S(1)} %collective-permute-done.3.refs_0_), channel_id=1, source_target_pairs={{0,1},{1,0},{2,3},{3,2},{4,5},{5,4},{6,7},{7,6},{8,9},{9,8},{10,11... | collective-permute-start | bytes 786440 | tf_op jit(solution)/shard_map/ppermute | solution.py:344
  26.3 3.9 %collective-permute-start.6 = (bf16[8,2,64,128]{3,2,1,0:T(8,128)(2,1)S(1)}, bf16[8,2,64,128]{3,2,1,0:T(8,128)(2,1)S(1)}, u32[]{:S(2)}, u32[]{:S(2)}) collective-permute-start(bf16[8,2,64,128]{3,2,1,0:T(8,128)(2,1)S(1)} %collective-permute-done.5.refs_0_), channel_id=1, source_target_pairs={{0,1},{1,0},{2,3},{3,2},{4,5},{5,4},{6,7},{7,6},{8,9},{9,8},{10,11... | collective-permute-start | bytes 786440 | tf_op jit(solution)/shard_map/ppermute | solution.py:344
  28.0 3.3 %collective-permute-start.8 = (bf16[8,2,64,128]{3,2,1,0:T(8,128)(2,1)S(1)}, bf16[8,2,64,128]{3,2,1,0:T(8,128)(2,1)S(1)}, u32[]{:S(2)}, u32[]{:S(2)}) collective-permute-start(bf16[8,2,64,128]{3,2,1,0:T(8,128)(2,1)S(1)} %collective-permute-done.7.refs_0_), channel_id=1, source_target_pairs={{0,1},{1,0},{2,3},{3,2},{4,5},{5,4},{6,7},{7,6},{8,9},{9,8},{10,11... | collective-permute-start | bytes 786440 | tf_op jit(solution)/shard_map/ppermute | solution.py:344
  32.4 7.7 %collective-permute-start.15 = (f32[8,4,64,128]{3,2,1,0:T(8,128)S(1)}, f32[8,4,64,128]{3,2,1,0:T(8,128)S(1)}, u32[]{:S(2)}, u32[]{:S(2)}) collective-permute-start(f32[8,4,64,128]{3,2,1,0:T(8,128)S(1)} %rotate.12), channel_id=1, source_target_pairs={{0,1},{1,0},{2,3},{3,2},{4,5},{5,4},{6,7},{7,6},{8,9},{9,8},{10,11... | collective-permute-start | bytes 3145736 | tf_op jit(solution)/shard_map/ppermute | solution.py:350
  32.9 10.6 %collective-permute-start.13 = (f32[8,4,64,128]{3,2,1,0:T(8,128)S(1)}, f32[8,4,64,128]{3,2,1,0:T(8,128)S(1)}, u32[]{:S(2)}, u32[]{:S(2)}) collective-permute-start(f32[8,4,64,128]{3,2,1,0:T(8,128)S(1)} %rotate.11), channel_id=1, source_target_pairs={{0,1},{1,0},{2,3},{3,2},{4,5},{5,4},{6,7},{7,6},{8,9},{9,8},{10,11... | collective-permute-start | bytes 3145736 | tf_op jit(solution)/shard_map/ppermute | solution.py:350
  33.0 10.7 %collective-permute-start.11 = (f32[8,4,64,128]{3,2,1,0:T(8,128)S(1)}, f32[8,4,64,128]{3,2,1,0:T(8,128)S(1)}, u32[]{:S(2)}, u32[]{:S(2)}) collective-permute-start(f32[8,4,64,128]{3,2,1,0:T(8,128)S(1)} %rotate.9), channel_id=1, source_target_pairs={{0,1},{1,0},{2,3},{3,2},{4,5},{5,4},{6,7},{7,6},{8,9},{9,8},{10,11... | collective-permute-start | bytes 3145736 | tf_op jit(solution)/shard_map/ppermute | solution.py:350
  33.4 5.2 %collective-permute-start.9 = (bf16[8,2,64,128]{3,2,1,0:T(8,128)(2,1)S(1)}, bf16[8,2,64,128]{3,2,1,0:T(8,128)(2,1)S(1)}, u32[]{:S(2)}, u32[]{:S(2)}) collective-permute-start(bf16[8,2,64,128]{3,2,1,0:T(8,128)(2,1)S(1)} %constant_dynamic-update-slice_fusion.refs_0_), channel_id=1, source_target_pairs={{0,1},{1,0},{2,3},{3,2},{4,5},{5,4},{6,7},{7,6},{8,9},{9,8},{10,11... | collective-permute-start | bytes 786440 | tf_op jit(solution)/shard_map/ppermute | solution.py:337
  39.7 6.6 %collective-permute-start.10 = (f32[8,4,64,128]{3,2,1,0:T(8,128)S(1)}, f32[8,4,64,128]{3,2,1,0:T(8,128)S(1)}, u32[]{:S(2)}, u32[]{:S(2)}) collective-permute-start(f32[8,4,64,128]{3,2,1,0:T(8,128)S(1)} %rotate.15), channel_id=1, source_target_pairs={{0,1},{1,0},{2,3},{3,2},{4,5},{5,4},{6,7},{7,6},{8,9},{9,8},{10,11... | collective-permute-start | bytes 3145736 | tf_op jit(solution)/shard_map/ppermute | solution.py:350
  40.3 15.5 %collective-permute-start.16 = (bf16[8,4,64,128]{3,2,1,0:T(8,128)(2,1)S(1)}, bf16[8,4,64,128]{3,2,1,0:T(8,128)(2,1)S(1)}, u32[]{:S(2)}, u32[]{:S(2)}) collective-permute-start(bf16[8,4,64,128]{3,2,1,0:T(8,128)(2,1)S(1)} %add_convert_fusion), channel_id=1, source_target_pairs={{0,24},{1,7},{2,26},{3,1},{4,28},{5,3},{6,30},{7,5},{8,0},{9,15},{... | collective-permute-start | bytes 1572872 | tf_op jit(solution)/shard_map/ppermute | solution.py:352
  43.7 19.7 %collective-permute-start.14 = (bf16[8,4,64,128]{3,2,1,0:T(8,128)(2,1)S(1)}, bf16[8,4,64,128]{3,2,1,0:T(8,128)(2,1)S(1)}, u32[]{:S(2)}, u32[]{:S(2)}) collective-permute-start(bf16[8,4,64,128]{3,2,1,0:T(8,128)(2,1)S(1)} %add_convert_fusion.1), channel_id=1, source_target_pairs={{0,8},{1,3},{2,10},{3,5},{4,12},{5,7},{6,14},{7,1},{8,16},{9,11},{... | collective-permute-start | bytes 1572872 | tf_op jit(solution)/shard_map/ppermute | solution.py:352
  43.9 19.4 %collective-permute-start.12 = (bf16[8,4,64,128]{3,2,1,0:T(8,128)(2,1)S(1)}, bf16[8,4,64,128]{3,2,1,0:T(8,128)(2,1)S(1)}, u32[]{:S(2)}, u32[]{:S(2)}) collective-permute-start(bf16[8,4,64,128]{3,2,1,0:T(8,128)(2,1)S(1)} %add_convert_fusion.2), channel_id=1, source_target_pairs={{0,16},{1,5},{2,18},{3,7},{4,20},{5,1},{6,22},{7,3},{8,24},{9,13},... | collective-permute-start | bytes 1572872 | tf_op jit(solution)/shard_map/ppermute | solution.py:352
  63.6 8.1 %collective-permute-start.17 = (f32[2,4,64,128]{3,2,1,0:T(8,128)S(1)}, f32[2,4,64,128]{3,2,1,0:T(8,128)S(1)}, u32[]{:S(2)}, u32[]{:S(2)}) collective-permute-start(f32[2,4,64,128]{3,2,1,0:T(8,128)S(1)} %get-tuple-element.68), channel_id=1, source_target_pairs={{0,4},{1,17},{2,6},{3,19},{4,0},{5,21},{6,2},{7,23},{8,12},{9,25},... | collective-permute-start | bytes 786440 | tf_op jit(solution)/shard_map/ppermute | solution.py:354
  63.7 8.0 %collective-permute-start.18 = (f32[2,4,64,128]{3,2,1,0:T(8,128)S(1)}, f32[2,4,64,128]{3,2,1,0:T(8,128)S(1)}, u32[]{:S(2)}, u32[]{:S(2)}) collective-permute-start(f32[2,4,64,128]{3,2,1,0:T(8,128)S(1)} %get-tuple-element.69), channel_id=1, source_target_pairs={{0,2},{1,9},{2,4},{3,11},{4,6},{5,13},{6,0},{7,15},{8,10},{9,17},{... | collective-permute-start | bytes 786440 | tf_op jit(solution)/shard_map/ppermute | solution.py:354
  63.8 10.6 %collective-permute-start.19 = (f32[2,4,64,128]{3,2,1,0:T(8,128)S(1)}, f32[2,4,64,128]{3,2,1,0:T(8,128)S(1)}, u32[]{:S(2)}, u32[]{:S(2)}) collective-permute-start(f32[2,4,64,128]{3,2,1,0:T(8,128)S(1)} %get-tuple-element.70), channel_id=1, source_target_pairs={{0,6},{1,25},{2,0},{3,27},{4,2},{5,29},{6,4},{7,31},{8,14},{9,1},{... | collective-permute-start | bytes 786440 | tf_op jit(solution)/shard_map/ppermute | solution.py:354

commit v4 on v3

--- a/solution.py
+++ b/solution.py
@@ -104,11 +104,11 @@
             f_ref[pl.ds(at, both.shape[0]), :] = both[:, 128 * i : 128 * i + 128]
 
 
-def fourier_first(rows, me_ref, c_ref, d_ref, k_ref, o_ref, f_ref, l_ref, cv_ref, dv_ref, kv_ref, raw_ref, turn_ref, sem, in_sem):
+def fourier_first(rows, me_ref, c_ref, d_ref, k_ref, v_ref, o_ref, f_ref, l_ref, vv_ref, cv_ref, dv_ref, kv_ref, raw_ref, turn_ref, sem, in_sem):
     step = pl.program_id(0)
     moves = [
         pltpu.make_async_copy(src, dst, in_sem.at[i])
-        for i, (src, dst) in enumerate(((c_ref, cv_ref), (d_ref, dv_ref), (k_ref, kv_ref)))
+        for i, (src, dst) in enumerate(((c_ref, cv_ref), (d_ref, dv_ref), (k_ref, kv_ref), (v_ref, vv_ref)))
     ]
 
     @pl.when(step == 0)
@@ -145,17 +145,21 @@
     params = pltpu.CompilerParams(dimension_semantics=("arbitrary",), vmem_limit_bytes=FOURIER_VMEM)
     cost = pl.CostEstimate(flops=4_000_000_000, bytes_accessed=16_000_000, transcendentals=0)
     if op == 0:
-        copies = [pltpu.VMEM(part.shape, part.dtype) for part in small[1:]]
+        copies = [pltpu.VMEM(part.shape, part.dtype) for part in small[1:4]]
         return pl.pallas_call(
             functools.partial(fourier_first, rows),
             grid_spec=pltpu.PrefetchScalarGridSpec(
                 num_scalar_prefetch=1,
                 grid=(width // rows,),
-                in_specs=[far] * 4,
-                out_specs=[local, local],
-                scratch_shapes=[*copies, *scratch, pltpu.SemaphoreType.DMA((3,))],
+                in_specs=[far] * 5,
+                out_specs=[local, local, local],
+                scratch_shapes=[*copies, *scratch, pltpu.SemaphoreType.DMA((4,))],
             ),
-            out_shape=[*out, jax.ShapeDtypeStruct((lines, 2 * ROWS), jnp.bfloat16)],
+            out_shape=[
+                *out,
+                jax.ShapeDtypeStruct((lines, 2 * ROWS), jnp.bfloat16),
+                jax.ShapeDtypeStruct(small[4].shape, small[4].dtype),
+            ],
             compiler_params=params,
             cost_estimate=cost,
             name="fourier_first",
@@ -326,11 +330,11 @@
     near = []
     for shift in (1, 2, 3):
         near.append(lax.ppermute(bloch_vectors, WHOLE, shift_pairs(1, -shift)))
-    far = [pltpu.with_memory_space_constraint(part, pltpu.HBM) for part in (r_coords.T, degeneracy.reshape(1, -1), kpoints.T)]
+    far = [pltpu.with_memory_space_constraint(part, pltpu.HBM) for part in (r_coords.T, degeneracy.reshape(1, -1), kpoints.T, bloch_vectors)]
     ops = pltpu.with_memory_space_constraint(wannier_ops, pltpu.HBM)
-    first, phases = fourier(0, (me, *far), ops)
-    near, first, phases = lax.optimization_barrier((near, first, phases))
-    near = jnp.concatenate([bloch_vectors, *near], axis=0)
+    first, phases, held = fourier(0, (me, *far), ops)
+    near, first, phases, held = lax.optimization_barrier((near, first, phases, held))
+    near = jnp.concatenate([held, *near], axis=0)
     mine, theirs = {0: near}, {}
     for shift in (2, 1, 3):
         mine[shift] = lax.ppermute(near, WHOLE, shift_pairs(0, -shift))
@@ -351,7 +355,7 @@
     for shift in (2, 1, 3):
         came[shift] = lax.ppermute((own[shift] + got[shift]).astype(LINK), WHOLE, shift_pairs(0, shift))
     total = collect(own[0], got[0], [came[shift] for shift in (2, 1, 3)])
-    return final(total[0], [lax.ppermute(total[shift], WHOLE, shift_pairs(1, shift)) for shift in (2, 1, 3)])
+    return final(total[0], [lax.ppermute(total[shift], WHOLE, shift_pairs(1, shift)) for shift in (1, 3, 2)])
 
 
 def solution(mesh):

time: 75.6 us -> 72.1 us (0.954)
  the two profiles are of different devices: /device:TPU:66 before, /device:TPU:102 now
where the time goes in v4:
time: 72.1 us; the launch traced here: 72 us
  waiting for transfers between devices  26.3 us (36%)
  Pallas kernels  22.6 us (31%)
  starting transfers between devices  22.3 us (31%)
    ppermute x3, waiting for transfers between devices, on_device(): lax.ppermute((own[shift] + got[shift]).astype(LINK), WHOLE, shift_pairs(0...  13.5 us
    pallas_call x8, Pallas kernels, rotate(): pl.pallas_call(functools.partial(rotate_body, shifts, half), in_specs=[wh...  8.45 us
    ppermute x3, waiting for transfers between devices, on_device(): lax.ppermute(total[shift], WHOLE, shift_pairs(1, shift))  7.15 us
    pallas_call x1, Pallas kernels, fourier(): pl.pallas_call(functools.partial(fourier_first, rows), grid_spec=pltpu.Pr...  6.95 us
    pallas_call x1, Pallas kernels, fourier(): pl.pallas_call(functools.partial(fourier_second, rows), grid=(width // ro...  5.88 us
    ppermute x3, starting transfers between devices, on_device(): lax.ppermute((own[shift] + got[shift]).astype(LINK), WHOLE, shift_pairs(0...  5.52 us
    ppermute x3, starting transfers between devices, on_device(): mine[shift] = lax.ppermute(near, WHOLE, shift_pairs(0, -shift))  5.3 us
    ppermute x3, starting transfers between devices, on_device(): lax.ppermute(total[shift], WHOLE, shift_pairs(1, shift))  5.15 us
  transfers between devices with their start and end apart: 20, of which 7 were waited for; matrix products, arithmetic and copies ran while one was open for 1% of the time, Pallas kernels for 28%

profile of v4, /device:TPU:102, one launch (start us, length us, event | category | flops | bytes accessed | tf_op | source)
XLA Modules:
  0.0 72.0 jit_solution(8709351974957797380)
XLA Ops:
  0.0 0.8 %collective-permute-start = (bf16[2,2,64,128]{3,2,1,0:T(8,128)(2,1)}, bf16[2,2,64,128]{3,2,1,0:T(8,128)(2,1)S(1)}, u32[]{:S(2)}, u32[]{:S(2)}) collective-permute-start(bf16[2,2,64,128]{3,2,1,0:T(8,128)(2,1)} %v_ref.1), channel_id=1, source_target_pairs={{0,6},{1,25},{2,0},{3,27},{4,2},{5,29},{6,4},{7,31},{8,14},{9,1},{... | collective-permute-start | bytes 196616 | tf_op jit(solution)/shard_map/ppermute | solution.py:332
  0.8 1.1 %collective-permute-start.1 = (bf16[2,2,64,128]{3,2,1,0:T(8,128)(2,1)}, bf16[2,2,64,128]{3,2,1,0:T(8,128)(2,1)S(1)}, u32[]{:S(2)}, u32[]{:S(2)}) collective-permute-start(bf16[2,2,64,128]{3,2,1,0:T(8,128)(2,1)} %v_ref.1), channel_id=1, source_target_pairs={{0,4},{1,17},{2,6},{3,19},{4,0},{5,21},{6,2},{7,23},{8,12},{9,25},... | collective-permute-start | bytes 196616 | tf_op jit(solution)/shard_map/ppermute | solution.py:332
  1.9 2.1 %collective-permute-start.2 = (bf16[2,2,64,128]{3,2,1,0:T(8,128)(2,1)}, bf16[2,2,64,128]{3,2,1,0:T(8,128)(2,1)S(1)}, u32[]{:S(2)}, u32[]{:S(2)}) collective-permute-start(bf16[2,2,64,128]{3,2,1,0:T(8,128)(2,1)} %v_ref.1), channel_id=1, source_target_pairs={{0,2},{1,9},{2,4},{3,11},{4,6},{5,13},{6,0},{7,15},{8,10},{9,17},{... | collective-permute-start | bytes 196616 | tf_op jit(solution)/shard_map/ppermute | solution.py:332
  4.0 7.0 %fourier_first.1 = (f32[33280,128]{1,0:T(8,128)S(1)}, bf16[256,256]{1,0:T(8,128)(2,1)S(1)}, bf16[2,2,64,128]{3,2,1,0:T(8,128)(2,1)S(1)}) custom-call(s32[1]{0:T(128)} %bitcast.me_ref, s32[3,125]{1,0:T(4,128)} %bitcast.5, s32[1,125]{1,0:T(1,128)} %bitcast.6, s32[3,256]{1,0:T(4,128)} %bitcast.4, bf16[2,2,64,128]{3,2,1,0:T(8,128)(2,1)} %v_ref.1, ...), custom_call_target="tpu_custom_call" | custom-call | flops 4000000000 | bytes 16000000 | tf_op jit(solution)/shard_map/fourier_first/pallas_call | solution.py:149
  11.0 0.0 collective-permute-done
  11.0 0.0 collective-permute-done.1
  11.0 0.0 collective-permute-done.2
  11.1 3.3 %collective-permute-start.3 = (bf16[8,2,64,128]{3,2,1,0:T(8,128)(2,1)S(1)}, bf16[8,2,64,128]{3,2,1,0:T(8,128)(2,1)S(1)}, u32[]{:S(2)}, u32[]{:S(2)}) collective-permute-start(bf16[8,2,64,128]{3,2,1,0:T(8,128)(2,1)S(1)} %constant_dynamic-update-slice_fusion.refs_0_), channel_id=1, source_target_pairs={{0,16},{1,5},{2,18},{3,7},{4,20},{5,1},{6,22},{7,3},{8,24},{9,13},... | collective-permute-start | bytes 786440 | tf_op jit(solution)/shard_map/ppermute | solution.py:340
  14.4 1.1 %collective-permute-start.5 = (bf16[8,2,64,128]{3,2,1,0:T(8,128)(2,1)S(1)}, bf16[8,2,64,128]{3,2,1,0:T(8,128)(2,1)S(1)}, u32[]{:S(2)}, u32[]{:S(2)}) collective-permute-start(bf16[8,2,64,128]{3,2,1,0:T(8,128)(2,1)S(1)} %constant_dynamic-update-slice_fusion.refs_0_), channel_id=1, source_target_pairs={{0,24},{1,7},{2,26},{3,1},{4,28},{5,3},{6,30},{7,5},{8,0},{9,15},{... | collective-permute-start | bytes 786440 | tf_op jit(solution)/shard_map/ppermute | solution.py:340
  15.4 1.0 %collective-permute-start.7 = (bf16[8,2,64,128]{3,2,1,0:T(8,128)(2,1)S(1)}, bf16[8,2,64,128]{3,2,1,0:T(8,128)(2,1)S(1)}, u32[]{:S(2)}, u32[]{:S(2)}) collective-permute-start(bf16[8,2,64,128]{3,2,1,0:T(8,128)(2,1)S(1)} %constant_dynamic-update-slice_fusion.refs_0_), channel_id=1, source_target_pairs={{0,8},{1,3},{2,10},{3,5},{4,12},{5,7},{6,14},{7,1},{8,16},{9,11},{... | collective-permute-start | bytes 786440 | tf_op jit(solution)/shard_map/ppermute | solution.py:340
  16.4 2.7 %collective-permute-done.3.refs_0_ = bf16[8,2,64,128]{3,2,1,0:T(8,128)(2,1)S(1)} collective-permute-done((bf16[8,2,64,128]{3,2,1,0:T(8,128)(2,1)S(1)}, bf16[8,2,64,128]{3,2,1,0:T(8,128)(2,1)S(1)}, u32[]{:S(2)}, u32[]{:S(2)}) %collective-permute-start.3) | collective-permute-done | bytes 262176 | tf_op jit(solution)/shard_map/ppermute | solution.py:340
  19.1 0.0 collective-permute-start.4
  19.1 5.9 %fourier_second.1.refs_2_ = f32[33280,128]{1,0:T(8,128)S(1)} custom-call(bf16[256,256]{1,0:T(8,128)(2,1)S(1)} %get-tuple-element.44.l_ref, bf16[2,125,2,128,128]{4,3,2,1,0:T(8,128)(2,1)} %o_ref.3), custom_call_target="tpu_custom_call" | custom-call | flops 4000000000 | bytes 16000000 | tf_op jit(solution)/shard_map/fourier_second/pallas_call | solution.py:167
  25.0 0.0 collective-permute-done.5.refs_0_
  25.0 0.6 collective-permute-start.6
  25.5 1.1 %rotate.8 = f32[8,4,64,128]{3,2,1,0:T(8,128)S(1)} custom-call(bf16[8,2,64,128]{3,2,1,0:T(8,128)(2,1)S(1)} %collective-permute-done.3.refs_0_, f32[33280,128]{1,0:T(8,128)S(1)} %get-tuple-element.62.refs_1_, f32[33280,128]{1,0:T(8,128)S(1)} %fourier_second.1.refs_2_), custom_call_target="tpu_custom_call" | custom-call | flops 960000000 | bytes 3200000 | tf_op jit(solution)/shard_map/rotate/pallas_call | solution.py:230
  26.6 0.0 collective-permute-done.7.refs_0_
  26.6 0.1 collective-permute-start.8
  26.7 0.0 collective-permute-done.4.refs_0_
  26.7 1.1 %rotate.9 = f32[8,4,64,128]{3,2,1,0:T(8,128)S(1)} custom-call(bf16[8,2,64,128]{3,2,1,0:T(8,128)(2,1)S(1)} %collective-permute-done.4.refs_0_, f32[33280,128]{1,0:T(8,128)S(1)} %get-tuple-element.62.refs_1_, f32[33280,128]{1,0:T(8,128)S(1)} %fourier_second.1.refs_2_), custom_call_target="tpu_custom_call" | custom-call | flops 960000000 | bytes 3200000 | tf_op jit(solution)/shard_map/rotate/pallas_call | solution.py:230
  27.8 1.1 %rotate.10 = f32[8,4,64,128]{3,2,1,0:T(8,128)S(1)} custom-call(bf16[8,2,64,128]{3,2,1,0:T(8,128)(2,1)S(1)} %collective-permute-done.5.refs_0_, f32[33280,128]{1,0:T(8,128)S(1)} %get-tuple-element.62.refs_1_, f32[33280,128]{1,0:T(8,128)S(1)} %fourier_second.1.refs_2_), custom_call_target="tpu_custom_call" | custom-call | flops 960000000 | bytes 3200000 | tf_op jit(solution)/shard_map/rotate/pallas_call | solution.py:230
  28.9 0.0 collective-permute-done.6.refs_0_
  28.9 1.1 %rotate.11 = f32[8,4,64,128]{3,2,1,0:T(8,128)S(1)} custom-call(bf16[8,2,64,128]{3,2,1,0:T(8,128)(2,1)S(1)} %collective-permute-done.6.refs_0_, f32[33280,128]{1,0:T(8,128)S(1)} %get-tuple-element.62.refs_1_, f32[33280,128]{1,0:T(8,128)S(1)} %fourier_second.1.refs_2_), custom_call_target="tpu_custom_call" | custom-call | flops 960000000 | bytes 3200000 | tf_op jit(solution)/shard_map/rotate/pallas_call | solution.py:230
  29.9 0.0 collective-permute-done.8.refs_0_
  29.9 1.1 %rotate.12 = f32[8,4,64,128]{3,2,1,0:T(8,128)S(1)} custom-call(bf16[8,2,64,128]{3,2,1,0:T(8,128)(2,1)S(1)} %collective-permute-done.8.refs_0_, f32[33280,128]{1,0:T(8,128)S(1)} %get-tuple-element.62.refs_1_, f32[33280,128]{1,0:T(8,128)S(1)} %fourier_second.1.refs_2_), custom_call_target="tpu_custom_call" | custom-call | flops 960000000 | bytes 3200000 | tf_op jit(solution)/shard_map/rotate/pallas_call | solution.py:230
  31.0 0.6 collective-permute-start.15
  31.6 0.1 collective-permute-start.13
  31.7 0.4 collective-permute-start.11
  32.1 0.1 collective-permute-start.9
  32.2 1.1 %rotate.13 = f32[8,4,64,128]{3,2,1,0:T(8,128)S(1)} custom-call(bf16[8,2,64,128]{3,2,1,0:T(8,128)(2,1)S(1)} %collective-permute-done.7.refs_0_, f32[33280,128]{1,0:T(8,128)S(1)} %get-tuple-element.62.refs_1_, f32[33280,128]{1,0:T(8,128)S(1)} %fourier_second.1.refs_2_), custom_call_target="tpu_custom_call" | custom-call | flops 960000000 | bytes 3200000 | tf_op jit(solution)/shard_map/rotate/pallas_call | solution.py:230
  33.2 1.1 %rotate.14.own_ref = f32[8,4,64,128]{3,2,1,0:T(8,128)S(1)} custom-call(bf16[8,2,64,128]{3,2,1,0:T(8,128)(2,1)S(1)} %constant_dynamic-update-slice_fusion.refs_0_, f32[33280,128]{1,0:T(8,128)S(1)} %get-tuple-element.62.refs_1_, f32[33280,128]{1,0:T(8,128)S(1)} %fourier_second.1.refs_2_), custom_call_target="tpu_custom_call" | custom-call | flops 960000000 | bytes 3200000 | tf_op jit(solution)/shard_map/rotate/pallas_call | solution.py:230
  34.3 2.9 %collective-permute-done.9.refs_0_ = bf16[8,2,64,128]{3,2,1,0:T(8,128)(2,1)S(1)} collective-permute-done((bf16[8,2,64,128]{3,2,1,0:T(8,128)(2,1)S(1)}, bf16[8,2,64,128]{3,2,1,0:T(8,128)(2,1)S(1)}, u32[]{:S(2)}, u32[]{:S(2)}) %collective-permute-start.9) | collective-permute-done | bytes 262176 | tf_op jit(solution)/shard_map/ppermute | solution.py:341
  37.2 1.1 %rotate.15 = f32[8,4,64,128]{3,2,1,0:T(8,128)S(1)} custom-call(bf16[8,2,64,128]{3,2,1,0:T(8,128)(2,1)S(1)} %collective-permute-done.9.refs_0_, f32[33280,128]{1,0:T(8,128)S(1)} %get-tuple-element.62.refs_1_, f32[33280,128]{1,0:T(8,128)S(1)} %fourier_second.1.refs_2_), custom_call_target="tpu_custom_call" | custom-call | flops 960000000 | bytes 3200000 | tf_op jit(solution)/shard_map/rotate/pallas_call | solution.py:230
  38.3 0.5 collective-permute-start.10
  38.7 0.0 collective-permute-done.15
  38.8 0.2 add_convert_fusion
  38.9 3.2 %collective-permute-start.16 = (bf16[8,4,64,128]{3,2,1,0:T(8,128)(2,1)S(1)}, bf16[8,4,64,128]{3,2,1,0:T(8,128)(2,1)S(1)}, u32[]{:S(2)}, u32[]{:S(2)}) collective-permute-start(bf16[8,4,64,128]{3,2,1,0:T(8,128)(2,1)S(1)} %add_convert_fusion), channel_id=1, source_target_pairs={{0,24},{1,7},{2,26},{3,1},{4,28},{5,3},{6,30},{7,5},{8,0},{9,15},{... | collective-permute-start | bytes 1572872 | tf_op jit(solution)/shard_map/ppermute | solution.py:356
  42.1 0.0 collective-permute-done.13
  42.1 0.2 add_convert_fusion.1
  42.3 0.1 collective-permute-start.14
  42.4 0.0 collective-permute-done.11
  42.4 0.2 add_convert_fusion.2
  42.6 2.3 %collective-permute-start.12 = (bf16[8,4,64,128]{3,2,1,0:T(8,128)(2,1)S(1)}, bf16[8,4,64,128]{3,2,1,0:T(8,128)(2,1)S(1)}, u32[]{:S(2)}, u32[]{:S(2)}) collective-permute-start(bf16[8,4,64,128]{3,2,1,0:T(8,128)(2,1)S(1)} %add_convert_fusion.2), channel_id=1, source_target_pairs={{0,16},{1,5},{2,18},{3,7},{4,20},{5,1},{6,22},{7,3},{8,24},{9,13},... | collective-permute-start | bytes 1572872 | tf_op jit(solution)/shard_map/ppermute | solution.py:356
  44.8 0.0 collective-permute-done.10.got_ref
  44.9 9.6 %collective-permute-done.16.down_ref = bf16[8,4,64,128]{3,2,1,0:T(8,128)(2,1)S(1)} collective-permute-done((bf16[8,4,64,128]{3,2,1,0:T(8,128)(2,1)S(1)}, bf16[8,4,64,128]{3,2,1,0:T(8,128)(2,1)S(1)}, u32[]{:S(2)}, u32[]{:S(2)}) %collective-permute-start.16) | collective-permute-done | bytes 524320 | tf_op jit(solution)/shard_map/ppermute | solution.py:356
  54.4 3.9 %collective-permute-done.14.up_ref = bf16[8,4,64,128]{3,2,1,0:T(8,128)(2,1)S(1)} collective-permute-done((bf16[8,4,64,128]{3,2,1,0:T(8,128)(2,1)S(1)}, bf16[8,4,64,128]{3,2,1,0:T(8,128)(2,1)S(1)}, u32[]{:S(2)}, u32[]{:S(2)}) %collective-permute-start.14) | collective-permute-done | bytes 524320 | tf_op jit(solution)/shard_map/ppermute | solution.py:356
  58.4 0.0 collective-permute-done.12.far_ref
  58.4 0.2 collect.1
  58.6 1.0 %collective-permute-start.17 = (f32[2,4,64,128]{3,2,1,0:T(8,128)S(1)}, f32[2,4,64,128]{3,2,1,0:T(8,128)S(1)}, u32[]{:S(2)}, u32[]{:S(2)}) collective-permute-start(f32[2,4,64,128]{3,2,1,0:T(8,128)S(1)} %get-tuple-element.72), channel_id=1, source_target_pairs={{0,2},{1,9},{2,4},{3,11},{4,6},{5,13},{6,0},{7,15},{8,10},{9,17},{... | collective-permute-start | bytes 786440 | tf_op jit(solution)/shard_map/ppermute | solution.py:358
  59.6 1.1 %collective-permute-start.18 = (f32[2,4,64,128]{3,2,1,0:T(8,128)S(1)}, f32[2,4,64,128]{3,2,1,0:T(8,128)S(1)}, u32[]{:S(2)}, u32[]{:S(2)}) collective-permute-start(f32[2,4,64,128]{3,2,1,0:T(8,128)S(1)} %get-tuple-element.73), channel_id=1, source_target_pairs={{0,6},{1,25},{2,0},{3,27},{4,2},{5,29},{6,4},{7,31},{8,14},{9,1},{... | collective-permute-start | bytes 786440 | tf_op jit(solution)/shard_map/ppermute | solution.py:358
  60.7 3.1 %collective-permute-start.19 = (f32[2,4,64,128]{3,2,1,0:T(8,128)S(1)}, f32[2,4,64,128]{3,2,1,0:T(8,128)S(1)}, u32[]{:S(2)}, u32[]{:S(2)}) collective-permute-start(f32[2,4,64,128]{3,2,1,0:T(8,128)S(1)} %get-tuple-element.74), channel_id=1, source_target_pairs={{0,4},{1,17},{2,6},{3,19},{4,0},{5,21},{6,2},{7,23},{8,12},{9,25},... | collective-permute-start | bytes 786440 | tf_op jit(solution)/shard_map/ppermute | solution.py:358
  63.8 1.3 %collective-permute-done.17.refs_0_ = f32[2,4,64,128]{3,2,1,0:T(8,128)S(1)} collective-permute-done((f32[2,4,64,128]{3,2,1,0:T(8,128)S(1)}, f32[2,4,64,128]{3,2,1,0:T(8,128)S(1)}, u32[]{:S(2)}, u32[]{:S(2)}) %collective-permute-start.17) | collective-permute-done | bytes 262176 | tf_op jit(solution)/shard_map/ppermute | solution.py:358
  65.1 2.1 %collective-permute-done.18.refs_1_ = f32[2,4,64,128]{3,2,1,0:T(8,128)S(1)} collective-permute-done((f32[2,4,64,128]{3,2,1,0:T(8,128)S(1)}, f32[2,4,64,128]{3,2,1,0:T(8,128)S(1)}, u32[]{:S(2)}, u32[]{:S(2)}) %collective-permute-start.18) | collective-permute-done | bytes 262176 | tf_op jit(solution)/shard_map/ppermute | solution.py:358
  67.2 3.8 %collective-permute-done.19.refs_2_ = f32[2,4,64,128]{3,2,1,0:T(8,128)S(1)} collective-permute-done((f32[2,4,64,128]{3,2,1,0:T(8,128)S(1)}, f32[2,4,64,128]{3,2,1,0:T(8,128)S(1)}, u32[]{:S(2)}, u32[]{:S(2)}) %collective-permute-start.19) | collective-permute-done | bytes 262176 | tf_op jit(solution)/shard_map/ppermute | solution.py:358
  70.9 1.1 %final.1 = f32[2,2,4096]{2,1,0:T(2,128)} custom-call(f32[2,4,64,128]{3,2,1,0:T(8,128)S(1)} %get-tuple-element.71.kept_ref, f32[2,4,64,128]{3,2,1,0:T(8,128)S(1)} %collective-permute-done.17.refs_0_, f32[2,4,64,128]{3,2,1,0:T(8,128)S(1)} %collective-permute-done.18.refs_1_, f32[2,4,64,128]{3,2,1,0:T(8,128)S(1)} %collective-permute-done.19.refs_2_), custom_call_target="tpu_custom_call" | custom-call | tf_op jit(solution)/shard_map/final/pallas_call | solution.py:303
  (4 shorter events, 0.1 us)
Async XLA Ops:
  0.0 11.0 %collective-permute-start = (bf16[2,2,64,128]{3,2,1,0:T(8,128)(2,1)}, bf16[2,2,64,128]{3,2,1,0:T(8,128)(2,1)S(1)}, u32[]{:S(2)}, u32[]{:S(2)}) collective-permute-start(bf16[2,2,64,128]{3,2,1,0:T(8,128)(2,1)} %v_ref.1), channel_id=1, source_target_pairs={{0,6},{1,25},{2,0},{3,27},{4,2},{5,29},{6,4},{7,31},{8,14},{9,1},{... | collective-permute-start | bytes 196616 | tf_op jit(solution)/shard_map/ppermute | solution.py:332
  0.8 10.2 %collective-permute-start.1 = (bf16[2,2,64,128]{3,2,1,0:T(8,128)(2,1)}, bf16[2,2,64,128]{3,2,1,0:T(8,128)(2,1)S(1)}, u32[]{:S(2)}, u32[]{:S(2)}) collective-permute-start(bf16[2,2,64,128]{3,2,1,0:T(8,128)(2,1)} %v_ref.1), channel_id=1, source_target_pairs={{0,4},{1,17},{2,6},{3,19},{4,0},{5,21},{6,2},{7,23},{8,12},{9,25},... | collective-permute-start | bytes 196616 | tf_op jit(solution)/shard_map/ppermute | solution.py:332
  1.9 9.1 %collective-permute-start.2 = (bf16[2,2,64,128]{3,2,1,0:T(8,128)(2,1)}, bf16[2,2,64,128]{3,2,1,0:T(8,128)(2,1)S(1)}, u32[]{:S(2)}, u32[]{:S(2)}) collective-permute-start(bf16[2,2,64,128]{3,2,1,0:T(8,128)(2,1)} %v_ref.1), channel_id=1, source_target_pairs={{0,2},{1,9},{2,4},{3,11},{4,6},{5,13},{6,0},{7,15},{8,10},{9,17},{... | collective-permute-start | bytes 196616 | tf_op jit(solution)/shard_map/ppermute | solution.py:332
  11.1 8.0 %collective-permute-start.3 = (bf16[8,2,64,128]{3,2,1,0:T(8,128)(2,1)S(1)}, bf16[8,2,64,128]{3,2,1,0:T(8,128)(2,1)S(1)}, u32[]{:S(2)}, u32[]{:S(2)}) collective-permute-start(bf16[8,2,64,128]{3,2,1,0:T(8,128)(2,1)S(1)} %constant_dynamic-update-slice_fusion.refs_0_), channel_id=1, source_target_pairs={{0,16},{1,5},{2,18},{3,7},{4,20},{5,1},{6,22},{7,3},{8,24},{9,13},... | collective-permute-start | bytes 786440 | tf_op jit(solution)/shard_map/ppermute | solution.py:340
  14.4 10.6 %collective-permute-start.5 = (bf16[8,2,64,128]{3,2,1,0:T(8,128)(2,1)S(1)}, bf16[8,2,64,128]{3,2,1,0:T(8,128)(2,1)S(1)}, u32[]{:S(2)}, u32[]{:S(2)}) collective-permute-start(bf16[8,2,64,128]{3,2,1,0:T(8,128)(2,1)S(1)} %constant_dynamic-update-slice_fusion.refs_0_), channel_id=1, source_target_pairs={{0,24},{1,7},{2,26},{3,1},{4,28},{5,3},{6,30},{7,5},{8,0},{9,15},{... | collective-permute-start | bytes 786440 | tf_op jit(solution)/shard_map/ppermute | solution.py:340
  15.4 11.2 %collective-permute-start.7 = (bf16[8,2,64,128]{3,2,1,0:T(8,128)(2,1)S(1)}, bf16[8,2,64,128]{3,2,1,0:T(8,128)(2,1)S(1)}, u32[]{:S(2)}, u32[]{:S(2)}) collective-permute-start(bf16[8,2,64,128]{3,2,1,0:T(8,128)(2,1)S(1)} %constant_dynamic-update-slice_fusion.refs_0_), channel_id=1, source_target_pairs={{0,8},{1,3},{2,10},{3,5},{4,12},{5,7},{6,14},{7,1},{8,16},{9,11},{... | collective-permute-start | bytes 786440 | tf_op jit(solution)/shard_map/ppermute | solution.py:340
  19.1 7.7 %collective-permute-start.4 = (bf16[8,2,64,128]{3,2,1,0:T(8,128)(2,1)S(1)}, bf16[8,2,64,128]{3,2,1,0:T(8,128)(2,1)S(1)}, u32[]{:S(2)}, u32[]{:S(2)}) collective-permute-start(bf16[8,2,64,128]{3,2,1,0:T(8,128)(2,1)S(1)} %collective-permute-done.3.refs_0_), channel_id=1, source_target_pairs={{0,1},{1,0},{2,3},{3,2},{4,5},{5,4},{6,7},{7,6},{8,9},{9,8},{10,11... | collective-permute-start | bytes 786440 | tf_op jit(solution)/shard_map/ppermute | solution.py:348
  25.0 3.9 %collective-permute-start.6 = (bf16[8,2,64,128]{3,2,1,0:T(8,128)(2,1)S(1)}, bf16[8,2,64,128]{3,2,1,0:T(8,128)(2,1)S(1)}, u32[]{:S(2)}, u32[]{:S(2)}) collective-permute-start(bf16[8,2,64,128]{3,2,1,0:T(8,128)(2,1)S(1)} %collective-permute-done.5.refs_0_), channel_id=1, source_target_pairs={{0,1},{1,0},{2,3},{3,2},{4,5},{5,4},{6,7},{7,6},{8,9},{9,8},{10,11... | collective-permute-start | bytes 786440 | tf_op jit(solution)/shard_map/ppermute | solution.py:348
  26.6 3.3 %collective-permute-start.8 = (bf16[8,2,64,128]{3,2,1,0:T(8,128)(2,1)S(1)}, bf16[8,2,64,128]{3,2,1,0:T(8,128)(2,1)S(1)}, u32[]{:S(2)}, u32[]{:S(2)}) collective-permute-start(bf16[8,2,64,128]{3,2,1,0:T(8,128)(2,1)S(1)} %collective-permute-done.7.refs_0_), channel_id=1, source_target_pairs={{0,1},{1,0},{2,3},{3,2},{4,5},{5,4},{6,7},{7,6},{8,9},{9,8},{10,11... | collective-permute-start | bytes 786440 | tf_op jit(solution)/shard_map/ppermute | solution.py:348
  31.0 7.7 %collective-permute-start.15 = (f32[8,4,64,128]{3,2,1,0:T(8,128)S(1)}, f32[8,4,64,128]{3,2,1,0:T(8,128)S(1)}, u32[]{:S(2)}, u32[]{:S(2)}) collective-permute-start(f32[8,4,64,128]{3,2,1,0:T(8,128)S(1)} %rotate.12), channel_id=1, source_target_pairs={{0,1},{1,0},{2,3},{3,2},{4,5},{5,4},{6,7},{7,6},{8,9},{9,8},{10,11... | collective-permute-start | bytes 3145736 | tf_op jit(solution)/shard_map/ppermute | solution.py:354
  31.6 10.6 %collective-permute-start.13 = (f32[8,4,64,128]{3,2,1,0:T(8,128)S(1)}, f32[8,4,64,128]{3,2,1,0:T(8,128)S(1)}, u32[]{:S(2)}, u32[]{:S(2)}) collective-permute-start(f32[8,4,64,128]{3,2,1,0:T(8,128)S(1)} %rotate.11), channel_id=1, source_target_pairs={{0,1},{1,0},{2,3},{3,2},{4,5},{5,4},{6,7},{7,6},{8,9},{9,8},{10,11... | collective-permute-start | bytes 3145736 | tf_op jit(solution)/shard_map/ppermute | solution.py:354
  31.7 10.7 %collective-permute-start.11 = (f32[8,4,64,128]{3,2,1,0:T(8,128)S(1)}, f32[8,4,64,128]{3,2,1,0:T(8,128)S(1)}, u32[]{:S(2)}, u32[]{:S(2)}) collective-permute-start(f32[8,4,64,128]{3,2,1,0:T(8,128)S(1)} %rotate.9), channel_id=1, source_target_pairs={{0,1},{1,0},{2,3},{3,2},{4,5},{5,4},{6,7},{7,6},{8,9},{9,8},{10,11... | collective-permute-start | bytes 3145736 | tf_op jit(solution)/shard_map/ppermute | solution.py:354
  32.1 5.2 %collective-permute-start.9 = (bf16[8,2,64,128]{3,2,1,0:T(8,128)(2,1)S(1)}, bf16[8,2,64,128]{3,2,1,0:T(8,128)(2,1)S(1)}, u32[]{:S(2)}, u32[]{:S(2)}) collective-permute-start(bf16[8,2,64,128]{3,2,1,0:T(8,128)(2,1)S(1)} %constant_dynamic-update-slice_fusion.refs_0_), channel_id=1, source_target_pairs={{0,1},{1,0},{2,3},{3,2},{4,5},{5,4},{6,7},{7,6},{8,9},{9,8},{10,11... | collective-permute-start | bytes 786440 | tf_op jit(solution)/shard_map/ppermute | solution.py:341
  38.3 6.6 %collective-permute-start.10 = (f32[8,4,64,128]{3,2,1,0:T(8,128)S(1)}, f32[8,4,64,128]{3,2,1,0:T(8,128)S(1)}, u32[]{:S(2)}, u32[]{:S(2)}) collective-permute-start(f32[8,4,64,128]{3,2,1,0:T(8,128)S(1)} %rotate.15), channel_id=1, source_target_pairs={{0,1},{1,0},{2,3},{3,2},{4,5},{5,4},{6,7},{7,6},{8,9},{9,8},{10,11... | collective-permute-start | bytes 3145736 | tf_op jit(solution)/shard_map/ppermute | solution.py:354
  38.9 15.5 %collective-permute-start.16 = (bf16[8,4,64,128]{3,2,1,0:T(8,128)(2,1)S(1)}, bf16[8,4,64,128]{3,2,1,0:T(8,128)(2,1)S(1)}, u32[]{:S(2)}, u32[]{:S(2)}) collective-permute-start(bf16[8,4,64,128]{3,2,1,0:T(8,128)(2,1)S(1)} %add_convert_fusion), channel_id=1, source_target_pairs={{0,24},{1,7},{2,26},{3,1},{4,28},{5,3},{6,30},{7,5},{8,0},{9,15},{... | collective-permute-start | bytes 1572872 | tf_op jit(solution)/shard_map/ppermute | solution.py:356
  42.3 16.1 %collective-permute-start.14 = (bf16[8,4,64,128]{3,2,1,0:T(8,128)(2,1)S(1)}, bf16[8,4,64,128]{3,2,1,0:T(8,128)(2,1)S(1)}, u32[]{:S(2)}, u32[]{:S(2)}) collective-permute-start(bf16[8,4,64,128]{3,2,1,0:T(8,128)(2,1)S(1)} %add_convert_fusion.1), channel_id=1, source_target_pairs={{0,8},{1,3},{2,10},{3,5},{4,12},{5,7},{6,14},{7,1},{8,16},{9,11},{... | collective-permute-start | bytes 1572872 | tf_op jit(solution)/shard_map/ppermute | solution.py:356
  42.6 15.8 %collective-permute-start.12 = (bf16[8,4,64,128]{3,2,1,0:T(8,128)(2,1)S(1)}, bf16[8,4,64,128]{3,2,1,0:T(8,128)(2,1)S(1)}, u32[]{:S(2)}, u32[]{:S(2)}) collective-permute-start(bf16[8,4,64,128]{3,2,1,0:T(8,128)(2,1)S(1)} %add_convert_fusion.2), channel_id=1, source_target_pairs={{0,16},{1,5},{2,18},{3,7},{4,20},{5,1},{6,22},{7,3},{8,24},{9,13},... | collective-permute-start | bytes 1572872 | tf_op jit(solution)/shard_map/ppermute | solution.py:356
  58.6 6.4 %collective-permute-start.17 = (f32[2,4,64,128]{3,2,1,0:T(8,128)S(1)}, f32[2,4,64,128]{3,2,1,0:T(8,128)S(1)}, u32[]{:S(2)}, u32[]{:S(2)}) collective-permute-start(f32[2,4,64,128]{3,2,1,0:T(8,128)S(1)} %get-tuple-element.72), channel_id=1, source_target_pairs={{0,2},{1,9},{2,4},{3,11},{4,6},{5,13},{6,0},{7,15},{8,10},{9,17},{... | collective-permute-start | bytes 786440 | tf_op jit(solution)/shard_map/ppermute | solution.py:358
  59.6 7.6 %collective-permute-start.18 = (f32[2,4,64,128]{3,2,1,0:T(8,128)S(1)}, f32[2,4,64,128]{3,2,1,0:T(8,128)S(1)}, u32[]{:S(2)}, u32[]{:S(2)}) collective-permute-start(f32[2,4,64,128]{3,2,1,0:T(8,128)S(1)} %get-tuple-element.73), channel_id=1, source_target_pairs={{0,6},{1,25},{2,0},{3,27},{4,2},{5,29},{6,4},{7,31},{8,14},{9,1},{... | collective-permute-start | bytes 786440 | tf_op jit(solution)/shard_map/ppermute | solution.py:358
  60.7 10.2 %collective-permute-start.19 = (f32[2,4,64,128]{3,2,1,0:T(8,128)S(1)}, f32[2,4,64,128]{3,2,1,0:T(8,128)S(1)}, u32[]{:S(2)}, u32[]{:S(2)}) collective-permute-start(f32[2,4,64,128]{3,2,1,0:T(8,128)S(1)} %get-tuple-element.74), channel_id=1, source_target_pairs={{0,4},{1,17},{2,6},{3,19},{4,0},{5,21},{6,2},{7,23},{8,12},{9,25},... | collective-permute-start | bytes 786440 | tf_op jit(solution)/shard_map/ppermute | solution.py:358
